TPU v7x, 32 devices: a whole 2x2x4 slice. The times are simulated.
32 devices in a mesh: rep: 4 (over x, core), fsdp: 8 (over z, y).
Axes of the slice: x: 2, y: 2, z: 4, core: 2. Of those that a mesh axis runs over, the one named last changes fastest.
Arguments:
- layer_input: bfloat16 [2, 24576, 768], P(None, ('rep', 'fsdp')), may hold values from -6 to 6
- cotangent: bfloat16 [2, 24576, 768], P(None, ('rep', 'fsdp')), may hold values from -6 to 6
- lengths: int32 [2, 384], P(None, ('rep', 'fsdp')), may hold values from 0 to 320, as said below
- attn_gain: bfloat16 [768], P('fsdp'), may hold values from 0.5 to 1.5
- global_gain: bfloat16 [768], P('fsdp'), may hold values from 0.5 to 1.5
- query_weight: bfloat16 [768, 768], P('fsdp'), may hold values from -0.0546875 to 0.0546875
- key_weight: bfloat16 [768, 768], P('fsdp'), may hold values from -0.21875 to 0.21875
- value_weight: bfloat16 [768, 768], P('fsdp'), may hold values from -0.21875 to 0.21875
- out_weight: bfloat16 [768, 768], P('fsdp'), may hold values from -0.875 to 0.875
- ffn_gain: bfloat16 [768], P('fsdp'), may hold values from 0.5 to 1.5
- gate_weight: bfloat16 [768, 2048], P('fsdp'), may hold values from -0.21875 to 0.21875
- up_weight: bfloat16 [768, 2048], P('fsdp'), may hold values from -0.21875 to 0.21875
- down_weight: bfloat16 [2048, 768], P('fsdp'), may hold values from -0.125 to 0.125
Outputs:
- layer_output: bfloat16 [2, 24576, 768], P(None, ('rep', 'fsdp'))
- in_grad: bfloat16 [2, 24576, 768], P(None, ('rep', 'fsdp'))
- attn_gain_grad: float32 [768], P('fsdp')
- global_gain_grad: float32 [768], P('fsdp')
- query_grad: float32 [768, 768], P('fsdp')
- key_grad: float32 [768, 768], P('fsdp')
- value_grad: float32 [768, 768], P('fsdp')
- out_weight_grad: float32 [768, 768], P('fsdp')
- ffn_gain_grad: float32 [768], P('fsdp')
- gate_grad: float32 [768, 2048], P('fsdp')
- up_grad: float32 [768, 2048], P('fsdp')
- down_grad: float32 [2048, 768], P('fsdp')
Inputs may be any that keep to these rules, and one draw needn't show every extreme that they name: `lengths`: entry b of the 12 entries that one device holds for one micro-batch is 0 or the length of a sequence whose first token is in block b; a sequence of n tokens fills its first block and the next ceil(n / 64) - 1 blocks of the same device, ending before the next nonzero entry. A device's filled blocks come first. On the 4 devices of one fsdp index, sequences fill exactly 16 blocks of each micro-batch. Some sequence of every draw has 320 tokens.
All inputs are finite; a program needn't handle non-finite values.
Results may differ from a plain program's by a relative error of at most 0.03.
Values may be sent and summed in bfloat16 or wider, within the bound.
A program may use at most 256 MiB of HBM per device.

v0:
```python
from functools import partial

import jax
import jax.numpy as jnp
from jax import lax
from jax.sharding import PartitionSpec as P

H = 12
DH = 64
RADIUS = 127
GBLK = 16
BLK = 64
AVG_BLOCKS = 4
DEAL_BLOCKS = 8
QB = 256
KPAD = 128


EPSILON = 1e-06
MASKED_SCORE = -1e30


def contract_rows(left_op, right_op):
    return lax.dot_general(
        left_op, right_op, (((0,), (0,)), ((), ())), preferred_element_type=jnp.float32
    )


def contract_cols(left_op, right_op):
    return lax.dot_general(
        left_op, right_op, (((1,), (1,)), ((), ())), preferred_element_type=jnp.float32
    )


def rms_norm(row_data, gain_vec):
    return (
        row_data
        * lax.rsqrt(jnp.mean(row_data * row_data, axis=-1, keepdims=True) + EPSILON)
        * gain_vec
    )


def layout(block_lens):
    block_count = block_lens.shape[0]
    block_index = jnp.arange(block_count, dtype=jnp.int32)
    first_start = lax.cummax(jnp.where(block_lens > 0, block_index, -1), axis=0)
    safe_first = jnp.maximum(first_start, 0)
    owner_len = jnp.sum(
        jnp.where(block_index[None, :] == safe_first[:, None], block_lens[None, :], 0), axis=1
    )
    offset = (block_index - first_start)[:, None] * BLK + jnp.arange(BLK, dtype=jnp.int32)[None, :]
    valid_tok = (first_start[:, None] >= 0) & (offset < owner_len[:, None])
    seg_tok = jnp.broadcast_to(first_start[:, None], (block_count, BLK))
    return (seg_tok.reshape(-1), valid_tok.reshape(-1))


def deal_table(all_lens, own_rank):
    block_count = all_lens.shape[0]
    block_index = jnp.arange(block_count, dtype=jnp.int32)
    first_start = lax.cummax(jnp.where(all_lens > 0, block_index, -1), axis=0)
    safe_first = jnp.maximum(first_start, 0)
    same_owner = block_index[None, :] == safe_first[:, None]
    owner_len = jnp.sum(jnp.where(same_owner, all_lens[None, :], 0), axis=1)
    in_use = (first_start >= 0) & ((block_index - first_start) * BLK < owner_len)
    use_count = in_use.astype(jnp.int32)
    position = jnp.cumsum(use_count) - use_count
    start_position = jnp.sum(jnp.where(same_owner, position[None, :], 0), axis=1)
    target = start_position // AVG_BLOCKS
    lowest = jnp.sum(jnp.where(in_use & (target < own_rank), 1, 0))
    slot_index = jnp.arange(DEAL_BLOCKS, dtype=jnp.int32)
    table = (in_use & (target == own_rank))[None, :] & (
        position[None, :] == lowest + slot_index[:, None]
    )
    dealt_lens = jnp.sum(jnp.where(table, all_lens[None, :], 0), axis=1)
    return (table.astype(jnp.bfloat16), dealt_lens)


def band_table():
    query_pos = jnp.arange(QB, dtype=jnp.int32)[:, None] + KPAD
    key_pos = jnp.arange(QB + 2 * KPAD, dtype=jnp.int32)[None, :]
    return jnp.abs(query_pos - key_pos) <= RADIUS


def block_terms(
    row_start, queries, keys_pad, values_pad, global_keys, seg_query, seg_key_pad, seg_global
):
    key_width = QB + 2 * KPAD
    query_blk = queries[row_start : row_start + QB].reshape(QB, H, DH)
    key_win = keys_pad[row_start : row_start + key_width]
    value_win = values_pad[row_start : row_start + key_width]
    local_scores = jnp.einsum(
        "qhd,khd->hqk", query_blk, key_win, preferred_element_type=jnp.float32
    )
    global_scores = jnp.einsum(
        "qhd,ghd->hqg", query_blk, global_keys, preferred_element_type=jnp.float32
    )
    seg_rows = seg_query[row_start : row_start + QB]
    allow_local = band_table() & (
        seg_rows[:, None] == seg_key_pad[row_start : row_start + key_width][None, :]
    )
    allow_global = seg_rows[:, None] == seg_global[None, :]
    masked_local = jnp.where(allow_local[None], local_scores, MASKED_SCORE)
    masked_global = jnp.where(allow_global[None], global_scores, MASKED_SCORE)
    return (query_blk, key_win, value_win, masked_local, masked_global)


def attend_forward(
    queries, keys_pad, values_pad, global_keys, global_values, seg_query, seg_key_pad, seg_global
):
    mixed_blocks = []
    kept = []
    for row_start in range(0, queries.shape[0], QB):
        query_blk, key_win, value_win, masked_local, masked_global = block_terms(
            row_start,
            queries,
            keys_pad,
            values_pad,
            global_keys,
            seg_query,
            seg_key_pad,
            seg_global,
        )
        row_peak = jnp.maximum(
            jnp.max(masked_local, axis=-1, keepdims=True),
            jnp.max(masked_global, axis=-1, keepdims=True),
        )
        local_exp = jnp.exp(masked_local - row_peak)
        global_exp = jnp.exp(masked_global - row_peak)
        denominator = jnp.sum(local_exp, axis=-1, keepdims=True) + jnp.sum(
            global_exp, axis=-1, keepdims=True
        )
        local_low = (local_exp / denominator).astype(jnp.bfloat16)
        global_low = (global_exp / denominator).astype(jnp.bfloat16)
        mixed_rows = jnp.einsum(
            "hqk,khd->qhd", local_low, value_win, preferred_element_type=jnp.float32
        )
        mixed_rows = mixed_rows + jnp.einsum(
            "hqg,ghd->qhd", global_low, global_values, preferred_element_type=jnp.float32
        )
        mixed_blocks.append(mixed_rows.reshape(QB, H * DH).astype(jnp.bfloat16))
        kept.append((row_peak, denominator))
    return (jnp.concatenate(mixed_blocks, axis=0), kept)


def attend_backward(
    grad_mixed,
    kept,
    queries,
    keys_pad,
    values_pad,
    global_keys,
    global_values,
    seg_query,
    seg_key_pad,
    seg_global,
):
    key_width = QB + 2 * KPAD
    row_count = queries.shape[0]
    grad_keys = jnp.zeros(keys_pad.shape, jnp.float32)
    grad_values = jnp.zeros(values_pad.shape, jnp.float32)
    grad_gkeys = jnp.zeros(global_keys.shape, jnp.float32)
    grad_gvalues = jnp.zeros(global_values.shape, jnp.float32)
    grad_query_blocks = []
    for number, row_start in enumerate(range(0, row_count, QB)):
        row_peak, denominator = kept[number]
        query_blk, key_win, value_win, masked_local, masked_global = block_terms(
            row_start,
            queries,
            keys_pad,
            values_pad,
            global_keys,
            seg_query,
            seg_key_pad,
            seg_global,
        )
        local_probs = jnp.exp(masked_local - row_peak) / denominator
        global_probs = jnp.exp(masked_global - row_peak) / denominator
        grad_blk = grad_mixed[row_start : row_start + QB].reshape(QB, H, DH)
        local_dp = jnp.einsum(
            "qhd,khd->hqk", grad_blk, value_win, preferred_element_type=jnp.float32
        )
        global_dp = jnp.einsum(
            "qhd,ghd->hqg", grad_blk, global_values, preferred_element_type=jnp.float32
        )
        centre = jnp.sum(local_probs * local_dp, axis=-1, keepdims=True) + jnp.sum(
            global_probs * global_dp, axis=-1, keepdims=True
        )
        local_ds = (local_probs * (local_dp - centre)).astype(jnp.bfloat16)
        global_ds = (global_probs * (global_dp - centre)).astype(jnp.bfloat16)
        grad_query_rows = jnp.einsum(
            "hqk,khd->qhd", local_ds, key_win, preferred_element_type=jnp.float32
        )
        grad_query_rows = grad_query_rows + jnp.einsum(
            "hqg,ghd->qhd", global_ds, global_keys, preferred_element_type=jnp.float32
        )
        grad_query_blocks.append(grad_query_rows.reshape(QB, H * DH).astype(jnp.bfloat16))
        grad_keys = grad_keys.at[row_start : row_start + key_width].add(
            jnp.einsum("hqk,qhd->khd", local_ds, query_blk, preferred_element_type=jnp.float32)
        )
        grad_values = grad_values.at[row_start : row_start + key_width].add(
            jnp.einsum(
                "hqk,qhd->khd",
                local_probs.astype(jnp.bfloat16),
                grad_blk,
                preferred_element_type=jnp.float32,
            )
        )
        grad_gkeys = grad_gkeys + jnp.einsum(
            "hqg,qhd->ghd", global_ds, query_blk, preferred_element_type=jnp.float32
        )
        grad_gvalues = grad_gvalues + jnp.einsum(
            "hqg,qhd->ghd",
            global_probs.astype(jnp.bfloat16),
            grad_blk,
            preferred_element_type=jnp.float32,
        )
    slot_count = global_keys.shape[0]
    grad_k = grad_keys[KPAD : KPAD + row_count].reshape(row_count, H * DH).astype(jnp.bfloat16)
    grad_v = grad_values[KPAD : KPAD + row_count].reshape(row_count, H * DH).astype(jnp.bfloat16)
    grad_gk = grad_gkeys.reshape(slot_count, H * DH).astype(jnp.bfloat16)
    grad_gv = grad_gvalues.reshape(slot_count, H * DH).astype(jnp.bfloat16)
    return (jnp.concatenate(grad_query_blocks, axis=0), grad_k, grad_v, grad_gk, grad_gv)


def layer_pass(row_data, cot_data, block_lens, weights):
    (
        attn_gain,
        global_gain,
        query_weight,
        key_weight,
        value_weight,
        out_weight,
        ffn_gain,
        gate_weight,
        up_weight,
        down_weight,
    ) = weights
    row_count = row_data.shape[0]
    slot_count = row_count // GBLK
    seg_tok, valid_tok = layout(block_lens)
    valid_col = valid_tok.astype(jnp.float32)[:, None]
    inputs_f = row_data.astype(jnp.float32)
    gain_one = attn_gain.astype(jnp.float32)
    gain_side = global_gain.astype(jnp.float32)
    gain_two = ffn_gain.astype(jnp.float32)
    normed_f, norm_back_one = jax.vjp(rms_norm, inputs_f, gain_one)
    normed = normed_f.astype(jnp.bfloat16)
    side_sum = jnp.sum(
        (normed.astype(jnp.float32) * valid_col).reshape(slot_count, GBLK, -1), axis=1
    )
    side_f, side_back = jax.vjp(rms_norm, side_sum, gain_side)
    side_normed = side_f.astype(jnp.bfloat16)
    queries = jnp.dot(normed, query_weight, preferred_element_type=jnp.float32).astype(jnp.bfloat16)
    keys_all = jnp.dot(normed, key_weight, preferred_element_type=jnp.float32).astype(jnp.bfloat16)
    values_all = jnp.dot(normed, value_weight, preferred_element_type=jnp.float32).astype(
        jnp.bfloat16
    )
    global_keys = jnp.dot(side_normed, key_weight, preferred_element_type=jnp.float32).astype(
        jnp.bfloat16
    )
    global_values = jnp.dot(side_normed, value_weight, preferred_element_type=jnp.float32).astype(
        jnp.bfloat16
    )
    seg_key = jnp.where(valid_tok, seg_tok, -2)
    seg_global = seg_key[::GBLK]
    keys_pad = jnp.pad(keys_all, ((KPAD, KPAD), (0, 0))).reshape(-1, H, DH)
    values_pad = jnp.pad(values_all, ((KPAD, KPAD), (0, 0))).reshape(-1, H, DH)
    seg_key_pad = jnp.pad(seg_key, (KPAD, KPAD), constant_values=-3)
    global_key_heads = global_keys.reshape(slot_count, H, DH)
    global_value_heads = global_values.reshape(slot_count, H, DH)
    attended, kept = attend_forward(
        queries,
        keys_pad,
        values_pad,
        global_key_heads,
        global_value_heads,
        seg_tok,
        seg_key_pad,
        seg_global,
    )
    hidden_one = inputs_f + jnp.dot(attended, out_weight, preferred_element_type=jnp.float32)
    normed_two_f, norm_back_two = jax.vjp(rms_norm, hidden_one, gain_two)
    normed_two = normed_two_f.astype(jnp.bfloat16)
    gate_pre = jnp.dot(normed_two, gate_weight, preferred_element_type=jnp.float32)
    up_pre = jnp.dot(normed_two, up_weight, preferred_element_type=jnp.float32)
    activated, gelu_back = jax.vjp(partial(jax.nn.gelu, approximate=True), gate_pre)
    hidden_two = (activated * up_pre).astype(jnp.bfloat16)
    result = (
        valid_col
        * (hidden_one + jnp.dot(hidden_two, down_weight, preferred_element_type=jnp.float32))
    ).astype(jnp.bfloat16)
    grad_res = cot_data.astype(jnp.float32) * valid_col
    grad_out = grad_res.astype(jnp.bfloat16)
    grad_hidden = contract_cols(grad_out, down_weight)
    grad_down = contract_rows(hidden_two, grad_out)
    grad_gate = gelu_back(grad_hidden * up_pre)[0].astype(jnp.bfloat16)
    grad_up = (grad_hidden * activated).astype(jnp.bfloat16)
    grad_gate_w = contract_rows(normed_two, grad_gate)
    grad_up_w = contract_rows(normed_two, grad_up)
    grad_normed_two = contract_cols(grad_gate, gate_weight) + contract_cols(grad_up, up_weight)
    grad_norm_part, grad_gain_two = norm_back_two(grad_normed_two)
    grad_hidden_one = grad_res + grad_norm_part
    grad_branch = grad_hidden_one.astype(jnp.bfloat16)
    grad_out_w = contract_rows(attended, grad_branch)
    grad_attended = contract_cols(grad_branch, out_weight).astype(jnp.bfloat16)
    grad_q, grad_k, grad_v, grad_gk, grad_gv = attend_backward(
        grad_attended,
        kept,
        queries,
        keys_pad,
        values_pad,
        global_key_heads,
        global_value_heads,
        seg_tok,
        seg_key_pad,
        seg_global,
    )
    grad_query_w = contract_rows(normed, grad_q)
    grad_key_w = contract_rows(normed, grad_k) + contract_rows(side_normed, grad_gk)
    grad_value_w = contract_rows(normed, grad_v) + contract_rows(side_normed, grad_gv)
    grad_normed = (
        contract_cols(grad_q, query_weight)
        + contract_cols(grad_k, key_weight)
        + contract_cols(grad_v, value_weight)
    )
    grad_side_normed = contract_cols(grad_gk, key_weight) + contract_cols(grad_gv, value_weight)
    grad_side, grad_gain_side = side_back(grad_side_normed)
    spread_side = grad_side[:, None, :] * valid_col.reshape(slot_count, GBLK, 1)
    grad_normed = grad_normed + spread_side.reshape(row_count, -1)
    grad_inputs, grad_gain_one = norm_back_one(grad_normed)
    grad_rows = (grad_inputs + grad_hidden_one).astype(jnp.bfloat16)
    grads = (
        grad_gain_one,
        grad_gain_side,
        grad_query_w,
        grad_key_w,
        grad_value_w,
        grad_out_w,
        grad_gain_two,
        grad_gate_w,
        grad_up_w,
        grad_down,
    )
    return (result, grad_rows, grads)


def dealt_pass(rows_in, cot_in, lens_in, gathered_weights):
    width_d = rows_in.shape[1]
    own_rank = lax.axis_index("rep")
    group_rows, group_cot, group_lens = (
        lax.all_gather(rows_in, "rep", axis=0, tiled=True),
        lax.all_gather(cot_in, "rep", axis=0, tiled=True),
        lax.all_gather(lens_in, "rep", axis=0, tiled=True),
    )
    block_count = group_lens.shape[0]
    table, dealt_lens = deal_table(group_lens, own_rank)
    stacked = jnp.concatenate(
        [group_rows.reshape(block_count, -1), group_cot.reshape(block_count, -1)], axis=1
    )
    dealt = jnp.dot(table, stacked, preferred_element_type=jnp.float32).astype(jnp.bfloat16)
    half_width = dealt.shape[1] // 2
    dealt_rows = dealt[:, :half_width].reshape(-1, width_d)
    dealt_cot = dealt[:, half_width:].reshape(-1, width_d)
    result, grad_rows, grads = layer_pass(dealt_rows, dealt_cot, dealt_lens, gathered_weights)
    answer = jnp.concatenate(
        [result.reshape(table.shape[0], -1), grad_rows.reshape(table.shape[0], -1)], axis=1
    )
    returned = lax.psum_scatter(
        contract_rows(table, answer).astype(jnp.bfloat16), "rep", scatter_dimension=0, tiled=True
    ).astype(jnp.float32)
    own_rows = returned[:, :half_width].reshape(rows_in.shape).astype(jnp.bfloat16)
    own_grads = returned[:, half_width:].reshape(rows_in.shape).astype(jnp.bfloat16)
    return (own_rows, own_grads, grads)


def per_device(
    layer_input,
    cotangent,
    lengths,
    attn_gain,
    global_gain,
    query_weight,
    key_weight,
    value_weight,
    out_weight,
    ffn_gain,
    gate_weight,
    up_weight,
    down_weight,
):
    running = None
    outputs = []
    input_grads = []
    for batch_index in range(layer_input.shape[0]):
        rows_in = layer_input[batch_index]
        cot_in = cotangent[batch_index]
        lens_in = lengths[batch_index]
        gathered_weights = (
            lax.all_gather(attn_gain, "fsdp", axis=0, tiled=True),
            lax.all_gather(global_gain, "fsdp", axis=0, tiled=True),
            lax.all_gather(query_weight, "fsdp", axis=0, tiled=True),
            lax.all_gather(key_weight, "fsdp", axis=0, tiled=True),
            lax.all_gather(value_weight, "fsdp", axis=0, tiled=True),
            lax.all_gather(out_weight, "fsdp", axis=0, tiled=True),
            lax.all_gather(ffn_gain, "fsdp", axis=0, tiled=True),
            lax.all_gather(gate_weight, "fsdp", axis=0, tiled=True),
            lax.all_gather(up_weight, "fsdp", axis=0, tiled=True),
            lax.all_gather(down_weight, "fsdp", axis=0, tiled=True),
        )
        result, grad_rows, grads = dealt_pass(rows_in, cot_in, lens_in, gathered_weights)
        outputs.append(result)
        input_grads.append(grad_rows)
        running = (
            grads
            if running is None
            else tuple((sum_old + term_new for sum_old, term_new in zip(running, grads)))
        )
    shards = (
        lax.psum_scatter(
            running[0].astype(jnp.bfloat16), "fsdp", scatter_dimension=0, tiled=True
        ).astype(jnp.float32),
        lax.psum_scatter(
            running[1].astype(jnp.bfloat16), "fsdp", scatter_dimension=0, tiled=True
        ).astype(jnp.float32),
        lax.psum_scatter(
            running[2].astype(jnp.bfloat16), "fsdp", scatter_dimension=0, tiled=True
        ).astype(jnp.float32),
        lax.psum_scatter(
            running[3].astype(jnp.bfloat16), "fsdp", scatter_dimension=0, tiled=True
        ).astype(jnp.float32),
        lax.psum_scatter(
            running[4].astype(jnp.bfloat16), "fsdp", scatter_dimension=0, tiled=True
        ).astype(jnp.float32),
        lax.psum_scatter(
            running[5].astype(jnp.bfloat16), "fsdp", scatter_dimension=0, tiled=True
        ).astype(jnp.float32),
        lax.psum_scatter(
            running[6].astype(jnp.bfloat16), "fsdp", scatter_dimension=0, tiled=True
        ).astype(jnp.float32),
        lax.psum_scatter(
            running[7].astype(jnp.bfloat16), "fsdp", scatter_dimension=0, tiled=True
        ).astype(jnp.float32),
        lax.psum_scatter(
            running[8].astype(jnp.bfloat16), "fsdp", scatter_dimension=0, tiled=True
        ).astype(jnp.float32),
        lax.psum_scatter(
            running[9].astype(jnp.bfloat16), "fsdp", scatter_dimension=0, tiled=True
        ).astype(jnp.float32),
    )
    shards = (
        lax.psum(shards[0].astype(jnp.bfloat16), "rep").astype(jnp.float32),
        lax.psum(shards[1].astype(jnp.bfloat16), "rep").astype(jnp.float32),
        lax.psum(shards[2].astype(jnp.bfloat16), "rep").astype(jnp.float32),
        lax.psum(shards[3].astype(jnp.bfloat16), "rep").astype(jnp.float32),
        lax.psum(shards[4].astype(jnp.bfloat16), "rep").astype(jnp.float32),
        lax.psum(shards[5].astype(jnp.bfloat16), "rep").astype(jnp.float32),
        lax.psum(shards[6].astype(jnp.bfloat16), "rep").astype(jnp.float32),
        lax.psum(shards[7].astype(jnp.bfloat16), "rep").astype(jnp.float32),
        lax.psum(shards[8].astype(jnp.bfloat16), "rep").astype(jnp.float32),
        lax.psum(shards[9].astype(jnp.bfloat16), "rep").astype(jnp.float32),
    )
    return (jnp.stack(outputs, axis=0), jnp.stack(input_grads, axis=0)) + tuple(shards)


def solution(mesh):
    placed = (
        P(None, ("rep", "fsdp"), None),
        P(None, ("rep", "fsdp"), None),
        P(None, ("rep", "fsdp")),
        P("fsdp"),
        P("fsdp"),
        P("fsdp", None),
        P("fsdp", None),
        P("fsdp", None),
        P("fsdp", None),
        P("fsdp"),
        P("fsdp", None),
        P("fsdp", None),
        P("fsdp", None),
    )
    return jax.shard_map(
        per_device,
        mesh=mesh,
        in_specs=placed,
        out_specs=(
            P(None, ("rep", "fsdp"), None),
            P(None, ("rep", "fsdp"), None),
            P("fsdp"),
            P("fsdp"),
            P("fsdp", None),
            P("fsdp", None),
            P("fsdp", None),
            P("fsdp", None),
            P("fsdp"),
            P("fsdp", None),
            P("fsdp", None),
            P("fsdp", None),
        ),
        check_vma=False,
    )
```

profile of v0, /device:TPU:0, one launch (start us, length us, event | category | flops | bytes accessed | tf_op | source)
XLA Modules:
  0.0 1576.7 jit_solution(18309962889812698769)
XLA Ops:
  19.8 6.4 all-reduce.20
  34.9 21.9 %all-reduce.22 = (bf16[768]{0:T(1024)(128)(2,1)S(1)}, bf16[768]{0:T(1024)(128)(2,1)S(1)}, bf16[768]{0:T(1024)(128)(2,1)S(1)}) all-reduce(bf16[768]{0:T(1024)(128)(2,1)S(1)} %dynamic-update-slice.25, bf16[768]{0:T(1024)(128)(2,1)S(1)} %dynamic-update-slice.26, ...), channel_id=1, replica_groups=mesh['rep'=4,'fsdp'=8] {'fsdp'}, use_global_device_ids=true, to_apply=%add.11 | all-reduce | flops 2304 | bytes 9216
  63.8 6.9 reshape.1518
  70.7 20.1 %all-gather.38.cloned.1.call-done = bf16[1,3072,768]{2,1,0:T(8,128)(2,1)} async-done(((bf16[1,768,768]{2,1,0:T(8,128)(2,1)}), bf16[1,3072,768]{2,1,0:T(8,128)(2,1)}) %all-gather.38.cloned.1.call-update) | async-done | bytes 4718608 | tf_op jit(solution)/shard_map/all_gather | solution.py:352
  90.8 6.9 reshape.1519
  97.7 6.3 convolution_convert_fusion.2
  107.5 22.3 %all-gather.32.cloned.1.call-done = bf16[1,3072,768]{2,1,0:T(8,128)(2,1)} async-done(((bf16[1,768,768]{2,1,0:T(8,128)(2,1)}), bf16[1,3072,768]{2,1,0:T(8,128)(2,1)}) %all-gather.32.cloned.1.call-update) | async-done | bytes 4718608 | tf_op jit(solution)/shard_map/all_gather | solution.py:351
  129.8 6.9 reshape.1505
  136.7 32.6 %all-gather.34.cloned.1.call-done = bf16[1,3072,768]{2,1,0:T(8,128)(2,1)} async-done(((bf16[1,768,768]{2,1,0:T(8,128)(2,1)}), bf16[1,3072,768]{2,1,0:T(8,128)(2,1)}) %all-gather.34.cloned.1.call-update) | async-done | bytes 4718608 | tf_op jit(solution)/shard_map/all_gather | solution.py:352
  169.3 7.4 reshape.1506
  191.9 20.5 %all-gather.22.cloned.1.call-done = bf16[768,768]{1,0:T(8,128)(2,1)} async-done(((bf16[96,768]{1,0:T(8,128)(2,1)}), bf16[768,768]{1,0:T(8,128)(2,1)}) %all-gather.22.cloned.1.call-update) | async-done | bytes 1179664 | tf_op jit(solution)/shard_map/all_gather | solution.py:402
  216.9 37.4 %all-gather.20.cloned.1.call-done = bf16[768,768]{1,0:T(8,128)(2,1)} async-done(((bf16[96,768]{1,0:T(8,128)(2,1)}), bf16[768,768]{1,0:T(8,128)(2,1)}) %all-gather.20.cloned.1.call-update) | async-done | bytes 1179664 | tf_op jit(solution)/shard_map/all_gather | solution.py:401
  264.0 32.4 %all-gather.18.cloned.1.call-done = bf16[768,768]{1,0:T(8,128)(2,1)} async-done(((bf16[96,768]{1,0:T(8,128)(2,1)}), bf16[768,768]{1,0:T(8,128)(2,1)}) %all-gather.18.cloned.1.call-update) | async-done | bytes 1179664 | tf_op jit(solution)/shard_map/all_gather | solution.py:403
  326.0 12.5 all-gather.24.cloned.1.call-done
  342.3 57.6 %all-gather.26.cloned.1.call-done = bf16[768,2048]{1,0:T(8,128)(2,1)} async-done(((bf16[96,2048]{1,0:T(8,128)(2,1)}), bf16[768,2048]{1,0:T(8,128)(2,1)}) %all-gather.26.cloned.1.call-update) | async-done | bytes 3145744 | tf_op jit(solution)/shard_map/all_gather | solution.py:406
  405.5 55.5 %all-gather.30.cloned.1.call-done = bf16[2048,768]{1,0:T(8,128)(2,1)} async-done(((bf16[256,768]{1,0:T(8,128)(2,1)}), bf16[2048,768]{1,0:T(8,128)(2,1)}) %all-gather.30.cloned.1.call-update) | async-done | bytes 3145744 | tf_op jit(solution)/shard_map/all_gather | solution.py:408
  466.7 55.5 %all-gather.28.cloned.1.call-done = bf16[768,2048]{1,0:T(8,128)(2,1)} async-done(((bf16[96,2048]{1,0:T(8,128)(2,1)}), bf16[768,2048]{1,0:T(8,128)(2,1)}) %all-gather.28.cloned.1.call-update) | async-done | bytes 3145744 | tf_op jit(solution)/shard_map/all_gather | solution.py:407
  522.3 9.2 multiply_convert_fusion.7
  550.7 7.1 multiply_reduce_fusion.2
  631.2 6.9 multiply_reduce_fusion.1
  641.7 7.1 multiply_reduce_fusion
  657.4 7.0 multiply_convert_fusion.3
  729.9 7.7 multiply_convert_fusion
  815.2 8.1 convolution_convert_fusion.1
  823.3 8.1 convolution_convert_fusion
  831.4 58.1 %reduce-scatter.10.cloned.1.call-done = bf16[96,768]{1,0:T(8,128)(2,1)} async-done(((bf16[768,768]{1,0:T(8,128)(2,1)}), bf16[96,768]{1,0:T(8,128)(2,1)}) %reduce-scatter.10.cloned.1.call-update) | async-done | bytes 147472 | tf_op jit(solution)/shard_map/reduce_scatter | solution.py:428
  889.5 66.9 %reduce-scatter.8.cloned.1.call-done = bf16[96,768]{1,0:T(8,128)(2,1)} async-done(((bf16[768,768]{1,0:T(8,128)(2,1)}), bf16[96,768]{1,0:T(8,128)(2,1)}) %reduce-scatter.8.cloned.1.call-update) | async-done | bytes 147472 | tf_op jit(solution)/shard_map/reduce_scatter | solution.py:425
  956.4 76.8 %reduce-scatter.20.cloned.1.call-done = bf16[256,768]{1,0:T(8,128)(2,1)} async-done(((bf16[2048,768]{1,0:T(8,128)(2,1)}), bf16[256,768]{1,0:T(8,128)(2,1)}) %reduce-scatter.20.cloned.1.call-update) | async-done | bytes 393232 | tf_op jit(solution)/shard_map/reduce_scatter | solution.py:446
  1033.2 77.1 %reduce-scatter.18.cloned.1.call-done = bf16[96,2048]{1,0:T(8,128)(2,1)} async-done(((bf16[768,2048]{1,0:T(8,128)(2,1)}), bf16[96,2048]{1,0:T(8,128)(2,1)}) %reduce-scatter.18.cloned.1.call-update) | async-done | bytes 393232 | tf_op jit(solution)/shard_map/reduce_scatter | solution.py:443
  1110.3 77.1 %reduce-scatter.16.cloned.1.call-done = bf16[96,2048]{1,0:T(8,128)(2,1)} async-done(((bf16[768,2048]{1,0:T(8,128)(2,1)}), bf16[96,2048]{1,0:T(8,128)(2,1)}) %reduce-scatter.16.cloned.1.call-update) | async-done | bytes 393232 | tf_op jit(solution)/shard_map/reduce_scatter | solution.py:440
  1188.8 19.8 %all-reduce.21 = (bf16[768]{0:T(1024)(128)(2,1)S(1)}, bf16[768]{0:T(1024)(128)(2,1)S(1)}, bf16[768]{0:T(1024)(128)(2,1)S(1)}) all-reduce(bf16[768]{0:T(1024)(128)(2,1)S(1)} %add_convert_fusion.9, bf16[768]{0:T(1024)(128)(2,1)S(1)} %add_convert_fusion.8, ...), channel_id=10, replica_groups=mesh['rep'=4,'fsdp'=8] {'fsdp'}, use_global_device_ids=true, to_apply=%region_58.59.clone | all-reduce | flops 2304 | bytes 9216
  1216.7 328.1 %all-reduce.27.cloned.1.call-done = (bf16[48,98304]{1,0:T(8,128)(2,1)}, bf16[48,98304]{1,0:T(8,128)(2,1)}, bf16[96,768]{1,0:T(8,128)(2,1)}, bf16[96,768]{1,0:T(8...) async-done(((bf16[48,98304]{1,0:T(8,128)(2,1)}, ...) | async-done | bytes 20643856
  (1056 shorter events, 381.3 us)
Async XLA Ops:
  7.2 56.6 %all-gather.36.cloned.1.call-start = ((), (), s32[]{:S(2)}) async-start(), calls=%async_computation.23 | async-start | bytes 5898240 | tf_op jit(solution)/shard_map/all_gather | solution.py:351
  10.6 80.2 %all-gather.38.cloned.1.call-start = ((), (), s32[]{:S(2)}) async-start(), calls=%async_computation.24 | async-start | bytes 5898240 | tf_op jit(solution)/shard_map/all_gather | solution.py:352
  12.3 117.6 %all-gather.32.cloned.1.call-start = ((), (), s32[]{:S(2)}) async-start(), calls=%async_computation.21 | async-start | bytes 5898240 | tf_op jit(solution)/shard_map/all_gather | solution.py:351
  13.0 156.3 %all-gather.34.cloned.1.call-start = ((), (), s32[]{:S(2)}) async-start(), calls=%async_computation.22 | async-start | bytes 5898240 | tf_op jit(solution)/shard_map/all_gather | solution.py:352
  13.6 198.8 %all-gather.22.cloned.1.call-start = ((), (), s32[]{:S(2)}) async-start(), calls=%async_computation.9 | async-start | bytes 1327104 | tf_op jit(solution)/shard_map/all_gather | solution.py:402
  14.2 240.2 %all-gather.20.cloned.1.call-start = ((), (), s32[]{:S(2)}) async-start(), calls=%async_computation.8 | async-start | bytes 1327104 | tf_op jit(solution)/shard_map/all_gather | solution.py:401
  14.7 281.6 %all-gather.18.cloned.1.call-start = ((), (), s32[]{:S(2)}) async-start(), calls=%async_computation.7 | async-start | bytes 1327104 | tf_op jit(solution)/shard_map/all_gather | solution.py:403
  15.5 322.9 %all-gather.24.cloned.1.call-start = ((), (), s32[]{:S(2)}) async-start(), calls=%async_computation.10 | async-start | bytes 1327104 | tf_op jit(solution)/shard_map/all_gather | solution.py:404
  16.2 383.6 %all-gather.26.cloned.1.call-start = ((), (), s32[]{:S(2)}) async-start(), calls=%async_computation.11 | async-start | bytes 3538944 | tf_op jit(solution)/shard_map/all_gather | solution.py:406
  17.0 444.0 %all-gather.30.cloned.1.call-start = ((), (), s32[]{:S(2)}) async-start(), calls=%async_computation.13 | async-start | bytes 3538944 | tf_op jit(solution)/shard_map/all_gather | solution.py:408
  17.6 504.7 %all-gather.28.cloned.1.call-start = ((), (), s32[]{:S(2)}) async-start(), calls=%async_computation.12 | async-start | bytes 3538944 | tf_op jit(solution)/shard_map/all_gather | solution.py:407
  18.3 813.1 %reduce-scatter.14.cloned.1.call-start = ((), (), s32[]{:S(2)}) async-start(), calls=%async_computation.17 | async-start | bytes 1327104 | tf_op jit(solution)/shard_map/reduce_scatter | solution.py:434
  29.4 147.4 %copy-start.257 = (s32[48]{0:T(128)}, s32[48]{0:T(128)S(1)}, u32[]{:S(2)}) copy-start(s32[48]{0:T(128)S(1)} %get-tuple-element.144) | copy-start | bytes 580
  29.6 147.2 %copy-start.259 = (pred[48]{0:T(512)(128)(4,1)}, pred[48]{0:T(512)(128)(4,1)S(1)}, u32[]{:S(2)}) copy-start(pred[48]{0:T(512)(128)(4,1)S(1)} %get-tuple-element.142) | copy-start | bytes 148
  30.9 145.9 %copy-start.277 = (s32[8]{0:T(128)}, s32[8]{0:T(128)S(1)}, u32[]{:S(2)}) copy-start(s32[8]{0:T(128)S(1)} %iota_add_fusion.2) | copy-start | bytes 100
  56.8 201.3 %copy-start.221 = (f32[768]{0:T(1024)}, f32[768]{0:T(1024)S(1)}, u32[]{:S(2)}) copy-start(f32[768]{0:T(1024)S(1)} %convert_element_type.596) | copy-start | bytes 9220
  58.5 203.7 %copy-start.208 = (f32[768]{0:T(1024)}, f32[768]{0:T(1024)S(1)}, u32[]{:S(2)}) copy-start(f32[768]{0:T(1024)S(1)} %convert_element_type.606) | copy-start | bytes 9220
  105.9 84.5 %copy-start.6 = (f32[512,768]{1,0:T(8,128)}, f32[512,768]{1,0:T(8,128)S(1)}, u32[]{:S(2)}) copy-start(f32[512,768]{1,0:T(8,128)S(1)} %reshape.1533) | copy-start | bytes 4718596
  185.9 152.5 %copy-start.9 = (f32[512,768]{1,0:T(8,128)}, f32[512,768]{1,0:T(8,128)S(1)}, u32[]{:S(2)}) copy-start(f32[512,768]{1,0:T(8,128)S(1)} %reshape.1529) | copy-start | bytes 4718596
  309.5 228.5 %copy-start.18 = (f32[512,768]{1,0:T(8,128)}, f32[512,768]{1,0:T(8,128)S(1)}, u32[]{:S(2)}) copy-start(f32[512,768]{1,0:T(8,128)S(1)} %reshape.1531) | copy-start | bytes 4718596
  316.2 258.2 %copy-start.163 = (f32[12,256]{1,0:T(8,128)}, f32[12,256]{1,0:T(8,128)S(1)}, u32[]{:S(2)}) copy-start(f32[12,256]{1,0:T(8,128)S(1)} %max.63) | copy-start | bytes 36868
  318.4 256.1 %copy-start.191 = (f32[12,256]{1,0:T(8,128)}, f32[12,256]{1,0:T(8,128)S(1)}, u32[]{:S(2)}) copy-start(f32[12,256]{1,0:T(8,128)S(1)} %add.582) | copy-start | bytes 36868
  342.2 180.1 %copy-start.50 = (bf16[512,768]{1,0:T(8,128)(2,1)}, bf16[512,768]{1,0:T(8,128)(2,1)S(1)}, u32[]{:S(2)}) copy-start(bf16[512,768]{1,0:T(8,128)(2,1)S(1)} %multiply_convert_fusion.15) | copy-start | bytes 2359300
  342.3 118.7 %copy-start.235 = (f32[512]{0:T(512)S(1)}, f32[512]{0:T(512)}, u32[]{:S(2)}) copy-start(f32[512]{0:T(512)} %reshape.1528) | copy-start | bytes 6148
  588.5 89.8 %copy-start.73 = (f32[12,256,32]{1,2,0:T(8,128)}, f32[12,256,32]{1,2,0:T(8,128)S(1)}, u32[]{:S(2)}) copy-start(f32[12,256,32]{1,2,0:T(8,128)S(1)} %get-tuple-element.245) | copy-start | bytes 1179652
  693.3 138.1 %reduce-scatter.12.cloned.1.call-start = ((), (), s32[]{:S(2)}) async-start(), calls=%async_computation.16 | async-start | bytes 1327104 | tf_op jit(solution)/shard_map/reduce_scatter | solution.py:431
  737.6 151.8 %reduce-scatter.10.cloned.1.call-start = ((), (), s32[]{:S(2)}) async-start(), calls=%async_computation.15 | async-start | bytes 1327104 | tf_op jit(solution)/shard_map/reduce_scatter | solution.py:428
  752.0 204.3 %reduce-scatter.8.cloned.1.call-start = ((), (), s32[]{:S(2)}) async-start(), calls=%async_computation.14 | async-start | bytes 1327104 | tf_op jit(solution)/shard_map/reduce_scatter | solution.py:425
  762.5 270.7 %reduce-scatter.20.cloned.1.call-start = ((), (), s32[]{:S(2)}) async-start(), calls=%async_computation.20 | async-start | bytes 3538944 | tf_op jit(solution)/shard_map/reduce_scatter | solution.py:446
  770.2 340.1 %reduce-scatter.18.cloned.1.call-start = ((), (), s32[]{:S(2)}) async-start(), calls=%async_computation.19 | async-start | bytes 3538944 | tf_op jit(solution)/shard_map/reduce_scatter | solution.py:443
  777.5 409.8 %reduce-scatter.16.cloned.1.call-start = ((), (), s32[]{:S(2)}) async-start(), calls=%async_computation.18 | async-start | bytes 3538944 | tf_op jit(solution)/shard_map/reduce_scatter | solution.py:440
  784.8 759.9 %all-reduce.27.cloned.1.call-start = ((), (), s32[]{:S(2)}) async-start(), calls=%async_computation.25 | async-start | bytes 41287680
  (311 other events, 1536.6 us)
Sparse Core Ops, SparseCore 0:
  10.7 40.2 all-gather.35
  53.1 37.5 all-gather.37
  92.3 37.4 all-gather.31
  131.8 37.4 all-gather.33
  171.3 41.0 all-gather.21
  214.5 39.8 all-gather.19
  256.5 39.8 all-gather.17
  298.5 39.8 all-gather.23
  340.6 59.2 all-gather.25
  401.9 59.0 all-gather.29
  463.2 59.0 all-gather.27
  693.4 62.5 reduce-scatter.13
  759.4 63.1 reduce-scatter.11
  826.4 62.9 reduce-scatter.9
  893.3 63.0 reduce-scatter.7
  959.8 73.3 reduce-scatter.19
  1036.6 73.6 reduce-scatter.17
  1113.8 73.5 reduce-scatter.15
  1190.8 353.8 all-reduce.26
where the time goes:
time: 1590 us; the launch traced here: 1580 us
  waiting for transfers between devices  1040 us (65%)
  matrix products  243 us (15%)
  local copies, waits for them, and re-layouts  152 us (10%)
  other arithmetic  68.5 us (4%)
  blocking collectives  54.4 us (3%)
  between operations  21.1 us (1%)
    unnamed x20, waiting for transfers between devices  334 us
    reduce_scatter x1, waiting for transfers between devices, per_device(): lax.psum_scatter(running[8].astype(jnp.bfloat16), 'fsdp', scatter_dimensi...  77.1 us
    reduce_scatter x1, waiting for transfers between devices, per_device(): lax.psum_scatter(running[7].astype(jnp.bfloat16), 'fsdp', scatter_dimensi...  77.1 us
    reduce_scatter x1, waiting for transfers between devices, per_device(): lax.psum_scatter(running[9].astype(jnp.bfloat16), 'fsdp', scatter_dimensi...  76.8 us
    reduce_scatter x1, waiting for transfers between devices, per_device(): lax.psum_scatter(running[2].astype(jnp.bfloat16), 'fsdp', scatter_dimensi...  66.9 us
    reduce_scatter x1, waiting for transfers between devices, per_device(): lax.psum_scatter(running[3].astype(jnp.bfloat16), 'fsdp', scatter_dimensi...  58.1 us
    all_gather x1, waiting for transfers between devices, per_device(): lax.all_gather(gate_weight, 'fsdp', axis=0, tiled=True)  57.6 us
    all_gather x1, waiting for transfers between devices, per_device(): lax.all_gather(up_weight, 'fsdp', axis=0, tiled=True)  55.5 us
  transfers between devices with their start and end apart: 19, of which 16 were waited for; matrix products, arithmetic and copies ran while one was open for 16% of the time, Pallas kernels for 0%

commit v1 on v0

v1 whole, which is shorter than its diff:
```python
from functools import partial

import jax
import jax.numpy as jnp
from jax import lax
from jax.experimental import pallas as pl
from jax.experimental.pallas import tpu as pltpu
from jax.sharding import PartitionSpec as P

H = 12
DH = 64
RADIUS = 127
GBLK = 16
BLK = 64
SLOTS = 10
MAX_SEQ_BLOCKS = 5
EPSILON = 1e-06
MASKED_SCORE = -1e30
MESH = pl.DeviceIdType.MESH
VMEM_LIMIT = 60 * 1024 * 1024
SEG_AT, LEN_AT, DEST_AT, TABLE_SIZE = 40, 80, 120, 256

ANY = pl.BlockSpec(memory_space=pl.ANY)
VMEM = pl.BlockSpec(memory_space=pltpu.VMEM)
SMEM = pl.BlockSpec(memory_space=pltpu.SMEM)


def grid_of(count):
    inner = 2 if count <= 8 else 4
    return count // inner, inner


def core_of(rank):
    return rank + 1 - 2 * (rank % 2)


def across_of(rank):
    return (rank + 2) % 4


def lens_kernel(lens_ref, all_ref, send_sem, recv_sem):
    rank = lax.axis_index("rep")
    barrier = pltpu.get_barrier_semaphore()
    for step in range(1, 4):
        pl.semaphore_signal(
            barrier, inc=1, device_id={"rep": (rank + step) % 4}, device_id_type=MESH
        )
    pl.semaphore_wait(barrier, 3)
    copies = []
    for step in range(1, 4):
        copy = pltpu.make_async_remote_copy(
            src_ref=lens_ref,
            dst_ref=all_ref.at[rank],
            send_sem=send_sem.at[step - 1],
            recv_sem=recv_sem.at[step - 1],
            device_id={"rep": (rank + step) % 4},
            device_id_type=MESH,
        )
        copy.start()
        copies.append(copy)
    all_ref[rank] = lens_ref[...]
    for copy in copies:
        copy.wait()


def table_kernel(micro, per_dev, lens_ref, tab_ref, order_ref, count_ref, load_ref):
    total = 4 * micro * per_dev

    def length_at(spot):
        return lens_ref[spot // (micro * per_dev), (spot // per_dev) % micro, spot % per_dev]

    def blocks_of(length):
        return (length + (BLK - 1)) // BLK

    def clear(spot, carry):
        tab_ref[spot] = -1
        return carry

    lax.fori_loop(0, TABLE_SIZE, clear, 0)
    for spot in range(4 * SLOTS):
        tab_ref[LEN_AT + spot] = 0
    for size in range(8):
        count_ref[size] = 0
    for dev in range(4):
        load_ref[dev] = 0

    def tally(spot, carry):
        length = length_at(spot)

        @pl.when(length > 0)
        def _():
            size = blocks_of(length)
            count_ref[size] = count_ref[size] + 1

        return carry

    lax.fori_loop(0, total, tally, 0)
    begin = 0
    for size in range(MAX_SEQ_BLOCKS, 0, -1):
        amount = count_ref[size]
        count_ref[size] = begin
        begin = begin + amount

    def place(spot, carry):
        length = length_at(spot)

        @pl.when(length > 0)
        def _():
            size = blocks_of(length)
            where = count_ref[size]
            order_ref[where] = spot
            count_ref[size] = where + 1

        return carry

    lax.fori_loop(0, total, place, 0)

    def assign(number, carry):
        spot = order_ref[number]
        length = length_at(spot)
        size = blocks_of(length)
        best = jnp.int32(0)
        low = load_ref[0]
        for dev in range(1, 4):
            here = load_ref[dev]
            best = jnp.where(here < low, dev, best)
            low = jnp.minimum(here, low)
        load_ref[best] = low + size

        def put(step, inner):
            slot = best * SLOTS + low + step
            tab_ref[slot] = spot + step
            tab_ref[SEG_AT + slot] = low
            tab_ref[LEN_AT + slot] = jnp.minimum(length - BLK * step, BLK)
            tab_ref[DEST_AT + spot + step] = slot
            return inner

        lax.fori_loop(0, size, put, 0)
        return carry

    lax.fori_loop(0, begin, assign, 0)


def deal_table(lengths):
    micro, per_dev = lengths.shape
    padded = jnp.pad(lengths, ((0, 8 - micro), (0, 128 - per_dev)))
    everyone = pl.pallas_call(
        lens_kernel,
        out_shape=jax.ShapeDtypeStruct((4, 8, 128), jnp.int32),
        in_specs=[VMEM],
        out_specs=VMEM,
        scratch_shapes=[pltpu.SemaphoreType.DMA((3,)), pltpu.SemaphoreType.DMA((3,))],
        compiler_params=pltpu.CompilerParams(collective_id=0, has_side_effects=True),
        name="lens_exchange",
    )(padded)
    return pl.pallas_call(
        partial(table_kernel, micro, per_dev),
        out_shape=jax.ShapeDtypeStruct((TABLE_SIZE,), jnp.int32),
        in_specs=[SMEM],
        out_specs=SMEM,
        scratch_shapes=[
            pltpu.SMEM((4 * micro * per_dev,), jnp.int32),
            pltpu.SMEM((8,), jnp.int32),
            pltpu.SMEM((4,), jnp.int32),
        ],
        name="deal_table",
    )(everyone)


def gather_kernel(
    outer, inner, splits, tab_ref, rows_ref, cots_ref, wa_ref, wb_ref, wc_ref,
    ga_ref, gb_ref, gc_ref, rows_out, cots_out,
    psend, precv, xsend, xrecv,
    z_send, z_recv, y_send, y_recv, c_send, c_recv, own_sem,
    p_send, p_recv, x_send, x_recv,
):
    rank = lax.axis_index("rep")
    spot = lax.axis_index("fsdp")
    core = rank % 2
    row, col = spot // inner, spot % inner
    count = outer * inner
    mate, across = core_of(rank), across_of(rank)
    pieces = [(wa_ref, ga_ref, start, width // 2) for start, width in splits]
    pieces.append((wb_ref, gb_ref, 0, wb_ref.shape[1] // 2))
    pieces.append((wc_ref, gc_ref, 0, None))
    halved = [number for number, piece in enumerate(pieces) if piece[3] is not None]

    barrier = pltpu.get_barrier_semaphore()
    neighbours = (
        (row + 1 < outer, {"fsdp": spot + inner}),
        (row > 0, {"fsdp": spot - inner}),
        (col + 1 < inner, {"fsdp": spot + 1}),
        (col > 0, {"fsdp": spot - 1}),
    )
    amount = jnp.int32(2)
    for there, device in neighbours:
        amount = amount + there.astype(jnp.int32)

        @pl.when(there)
        def _():
            pl.semaphore_signal(barrier, inc=1, device_id=device, device_id_type=MESH)

    for device in (mate, across):
        pl.semaphore_signal(barrier, inc=1, device_id={"rep": device}, device_id_type=MESH)
    pl.semaphore_wait(barrier, amount)

    def cut(ref, number):
        _, _, start, half = pieces[number]
        if half is None:
            return ref
        return ref.at[:, pl.ds(pl.multiple_of(start + core * half, 128), half)]

    def landed(number, shard):
        return cut(pieces[number][1].at[shard], number)

    late = []

    def send(there, src, dst, ssem, rsem, device):
        def describe():
            return pltpu.make_async_remote_copy(
                src_ref=src, dst_ref=dst, send_sem=ssem, recv_sem=rsem,
                device_id=device, device_id_type=MESH,
            )

        if there is None:
            describe().start()
            late.append((None, lambda: describe().wait_send()))
        else:
            @pl.when(there)
            def _():
                describe().start()

            late.append((there, lambda: describe().wait_send()))

    def arrive(number, shard, rsem):
        pltpu.make_async_remote_copy(
            src_ref=landed(number, shard), dst_ref=landed(number, shard),
            send_sem=own_sem.at[0], recv_sem=rsem,
            device_id={"rep": mate}, device_id_type=MESH,
        ).wait_recv()

    def both(first, second):
        return second if first is None else jnp.logical_and(first, second)

    def to_mate(there, number, shard):
        if number not in halved:
            return
        place = landed(number, shard)
        send(there, place, place, c_send.at[number, shard], c_recv.at[number, shard], {"rep": mate})

    def along_row(there, number, line, src):
        shard = line * inner + col
        place = landed(number, shard)
        src = place if src is None else src
        send(both(there, col + 1 < inner), src, place,
             y_send.at[0, 0, line, number], y_recv.at[0, 0, line, number], {"fsdp": spot + 1})
        send(both(there, col > 0), src, place,
             y_send.at[1, 0, line, number], y_recv.at[1, 0, line, number], {"fsdp": spot - 1})

    def from_row(there, number, line):
        for step in range(inner - 1):
            for way, source, onward, target in (
                (0, col - 1 - step, col + 1 < inner, spot + 1),
                (1, col + 1 + step, col > 0, spot - 1),
            ):
                here = jnp.logical_and(source >= 0, source < inner)
                here = both(there, here)
                shard = line * inner + source

                @pl.when(here)
                def _():
                    arrive(number, shard, y_recv.at[way, step, line, number])

                if step + 1 < inner - 1:
                    place = landed(number, shard)
                    send(both(here, onward), place, place,
                         y_send.at[way, step + 1, line, number],
                         y_recv.at[way, step + 1, line, number], {"fsdp": target})
                to_mate(here, number, shard)

    for number, piece in enumerate(pieces):
        src, place = cut(piece[0], number), landed(number, spot)
        send(row + 1 < outer, src, place, z_send.at[0, 0, number], z_recv.at[0, 0, number],
             {"fsdp": spot + inner})
        send(row > 0, src, place, z_send.at[1, 0, number], z_recv.at[1, 0, number],
             {"fsdp": spot - inner})
        along_row(None, number, row, src)
    own = [
        pltpu.make_async_copy(wa_ref, ga_ref.at[spot], own_sem.at[0]),
        pltpu.make_async_copy(wb_ref, gb_ref.at[spot], own_sem.at[1]),
        pltpu.make_async_copy(wc_ref, gc_ref.at[spot], own_sem.at[2]),
    ]
    for copy in own:
        copy.start()

    sources = (rows_ref, cots_ref)
    per_rank = rows_ref.shape[0]

    def picked(kind, target, slot):
        index = tab_ref[target * SLOTS + slot] - rank * per_rank
        mine = jnp.logical_and(index >= 0, index < per_rank)
        value = sources[kind][jnp.clip(index, 0, per_rank - 1)]
        return mine, value

    def mate_copy(kind, part):
        return pltpu.make_async_remote_copy(
            src_ref=psend.at[kind, part], dst_ref=precv.at[kind, part],
            send_sem=p_send.at[kind, part], recv_sem=p_recv.at[kind, part],
            device_id={"rep": mate}, device_id_type=MESH,
        )

    def across_copy(kind):
        return pltpu.make_async_remote_copy(
            src_ref=xsend.at[kind], dst_ref=xrecv.at[kind],
            send_sem=x_send.at[kind], recv_sem=x_recv.at[kind],
            device_id={"rep": across}, device_id_type=MESH,
        )

    for kind, part in ((0, 1), (1, 1), (0, 0), (1, 0)):
        target = mate if part == 0 else across_of(mate)

        def pack(slot, carry):
            mine, value = picked(kind, target, slot)
            psend[kind, part, slot] = jnp.where(mine, value, jnp.zeros_like(value))
            return carry

        lax.fori_loop(0, SLOTS, pack, 0)
        mate_copy(kind, part).start()
    for kind in range(2):
        mate_copy(kind, 1).wait_recv()

        def merge(slot, carry):
            mine, value = picked(kind, across, slot)
            xsend[kind, slot] = jnp.where(mine, value, precv[kind, 1, slot])
            return carry

        lax.fori_loop(0, SLOTS, merge, 0)
        across_copy(kind).start()

    def lines(step):
        return ((row - 1 - step >= 0, row - 1 - step, 0, row + 1 < outer, spot + inner),
                (row + 1 + step < outer, row + 1 + step, 1, row > 0, spot - inner))

    for step in range(outer - 1):
        for number in range(len(pieces)):
            for here, line, way, onward, target in lines(step):
                shard = line * inner + col

                @pl.when(here)
                def _():
                    arrive(number, shard, z_recv.at[way, step, number])

                if step + 1 < outer - 1:
                    place = landed(number, shard)
                    send(jnp.logical_and(here, onward), place, place,
                         z_send.at[way, step + 1, number], z_recv.at[way, step + 1, number],
                         {"fsdp": target})
                along_row(here, number, line, None)
                to_mate(here, number, shard)
        for number in range(len(pieces)):
            if step == 0:
                from_row(None, number, row)
            else:
                for here, line, *_ in lines(step - 1):
                    from_row(here, number, line)
    for number in range(len(pieces)):
        for here, line, *_ in lines(outer - 2):
            from_row(here, number, line)

    outs = (rows_out, cots_out)
    for kind in range(2):
        mate_copy(kind, 0).wait_recv()
        across_copy(kind).wait_recv()

        def finish(slot, carry):
            mine, value = picked(kind, rank, slot)
            outs[kind][slot] = jnp.where(mine, value, precv[kind, 0, slot] + xrecv[kind, slot])
            return carry

        lax.fori_loop(0, SLOTS, finish, 0)

    for shard in range(count):
        @pl.when(shard != spot)
        def _():
            for number in halved:
                other = pieces[number]
                view = other[1].at[shard].at[:, pl.ds(0, other[3])]
                pltpu.make_async_remote_copy(
                    src_ref=view, dst_ref=view, send_sem=own_sem.at[0],
                    recv_sem=c_recv.at[number, shard],
                    device_id={"rep": mate}, device_id_type=MESH,
                ).wait_recv()
    for there, finish_send in late:
        if there is None:
            finish_send()
        else:
            pl.when(there)(finish_send)
    for kind in range(2):
        for part in range(2):
            mate_copy(kind, part).wait_send()
        across_copy(kind).wait_send()
    for copy in own:
        copy.wait()


def gather_weights(count, splits, table, rows, cots, wa, wb, wc):
    outer, inner = grid_of(count)
    block = rows.shape[1:]
    kinds = len(splits) + 2
    dma = pltpu.SemaphoreType.DMA
    bf16 = jnp.bfloat16
    return pl.pallas_call(
        partial(gather_kernel, outer, inner, splits),
        out_shape=(
            jax.ShapeDtypeStruct((count,) + wa.shape, bf16),
            jax.ShapeDtypeStruct((count,) + wb.shape, bf16),
            jax.ShapeDtypeStruct((count,) + wc.shape, bf16),
            jax.ShapeDtypeStruct((SLOTS,) + block, bf16),
            jax.ShapeDtypeStruct((SLOTS,) + block, bf16),
        ),
        in_specs=[SMEM, VMEM, VMEM, VMEM, VMEM, VMEM],
        out_specs=(ANY, ANY, ANY, VMEM, VMEM),
        scratch_shapes=[
            pltpu.VMEM((2, 2, SLOTS) + block, bf16),
            pltpu.VMEM((2, 2, SLOTS) + block, bf16),
            pltpu.VMEM((2, SLOTS) + block, bf16),
            pltpu.VMEM((2, SLOTS) + block, bf16),
            dma((2, outer - 1, kinds)), dma((2, outer - 1, kinds)),
            dma((2, inner - 1, outer, kinds)), dma((2, inner - 1, outer, kinds)),
            dma((kinds, count)), dma((kinds, count)), dma((3,)),
            dma((2, 2)), dma((2, 2)), dma((2,)), dma((2,)),
        ],
        compiler_params=pltpu.CompilerParams(
            collective_id=1, has_side_effects=True, vmem_limit_bytes=VMEM_LIMIT
        ),
        name="gather_and_deal",
    )(table, rows, cots, wa, wb, wc)


def reduce_kernel(
    outer, inner, splits, ga_ref, gb_ref, gc_ref, y_ref, g_ref,
    oa_ref, ob_ref, oc_ref, ry_ref, rg_ref, *scratch,
):
    kinds = len(splits) + 2
    mines, crecvs, yrecvs, zrecvs, xrecvs = (
        scratch[kinds * i : kinds * (i + 1)] for i in range(5)
    )
    (c_send, c_recv, m_sem, y_send, y_recv, z_send, z_recv, x_send, x_recv, f_send, f_recv,
     r_send, r_recv, q_sem) = scratch[5 * kinds :]
    rank = lax.axis_index("rep")
    spot = lax.axis_index("fsdp")
    core = rank % 2
    row, col = spot // inner, spot % inner
    mate, across = core_of(rank), across_of(rank)
    pieces = [(ga_ref, oa_ref, start, width // 2) for start, width in splits]
    pieces.append((gb_ref, ob_ref, 0, gb_ref.shape[3] // 2))
    pieces.append((gc_ref, oc_ref, 0, None))

    barrier = pltpu.get_barrier_semaphore()
    neighbours = (
        (row + 1 < outer, {"fsdp": spot + inner}),
        (row > 0, {"fsdp": spot - inner}),
        (col + 1 < inner, {"fsdp": spot + 1}),
        (col > 0, {"fsdp": spot - 1}),
    )
    amount = jnp.int32(2)
    for there, device in neighbours:
        amount = amount + there.astype(jnp.int32)

        @pl.when(there)
        def _():
            pl.semaphore_signal(barrier, inc=1, device_id=device, device_id_type=MESH)

    for device in (mate, across):
        pl.semaphore_signal(barrier, inc=1, device_id={"rep": device}, device_id_type=MESH)
    pl.semaphore_wait(barrier, amount)

    late = []

    def send(there, src, dst, ssem, rsem, device):
        def describe():
            return pltpu.make_async_remote_copy(
                src_ref=src, dst_ref=dst, send_sem=ssem, recv_sem=rsem,
                device_id=device, device_id_type=MESH,
            )

        if there is None:
            describe().start()
            late.append((None, lambda: describe().wait_send()))
        else:
            @pl.when(there)
            def _():
                describe().start()

            late.append((there, lambda: describe().wait_send()))

    def arrive(place, rsem):
        pltpu.make_async_remote_copy(
            src_ref=place, dst_ref=place, send_sem=q_sem.at[0], recv_sem=rsem,
            device_id={"rep": mate}, device_id_type=MESH,
        ).wait_recv()

    def columns(ref, number, which):
        _, _, start, half = pieces[number]
        if half is None:
            return ref
        cols = pl.ds(pl.multiple_of(start + which * half, 128), half)
        return ref.at[:, :, :, cols] if len(ref.shape) == 4 else ref.at[:, cols]

    order = list(range(kinds))
    loads = []
    for number in order:
        src = columns(pieces[number][0], number, 1 - core)
        send(None, src, crecvs[number], c_send.at[number], c_recv.at[number], {"rep": mate})
        load = pltpu.make_async_copy(
            columns(pieces[number][0], number, core), mines[number], m_sem.at[number]
        )
        load.start()
        loads.append(load)

    for kind, (src, dst) in enumerate(((y_ref, ry_ref), (g_ref, rg_ref))):
        send(None, src, dst.at[rank], r_send.at[kind, 0], r_recv.at[kind, 0], {"rep": across})
        send(None, src, dst.at[rank], r_send.at[kind, 1], r_recv.at[kind, 1], {"rep": mate})
        pltpu.make_async_copy(src, dst.at[rank], q_sem.at[kind + 1]).start()

    def slot_of(way, size, place, dest):
        if size == 2:
            return 0
        return dest - place if way == 0 else size - place + dest

    def line_sum(number, size, place, stride, buffer, view, ssem, rsem):
        for far in range(size - 1, 0, -1):
            for way in range(2):
                dest = far if way == 0 else size - 1 - far
                step = 1 if way == 0 else -1
                passes = place < dest if way == 0 else place > dest
                first = place == 0 if way == 0 else place == size - 1
                mine = view(dest)
                got = slot_of(way, size, place, dest)

                @pl.when(jnp.logical_and(passes, jnp.logical_not(first)))
                def _():
                    arrive(buffer.at[got], rsem.at[got, number])
                    mine[...] = mine[...] + buffer[got]

                put = slot_of(way, size, place + step, dest)
                send(passes, mine, buffer.at[put], ssem.at[way, dest, number], rsem.at[put, number],
                     {"fsdp": spot + step * stride})
        for way in range(2):
            has = place > 0 if way == 0 else place < size - 1
            got = slot_of(way, size, place, place)
            mine = view(place)

            @pl.when(has)
            def _():
                arrive(buffer.at[got], rsem.at[got, number])
                mine[...] = mine[...] + buffer[got]

    for number in order:
        loads[number].wait()
        arrive(crecvs[number], c_recv.at[number])
        mine, other = mines[number], crecvs[number]

        def add(index, carry):
            mine[index // inner, index % inner] = (
                mine[index // inner, index % inner] + other[index // inner, index % inner]
            )
            return carry

        lax.fori_loop(0, outer * inner, add, 0)
        if inner == 2:
            send(None, mine.at[:, 1 - col], yrecvs[number].at[0], y_send.at[0, 0, number],
                 y_recv.at[0, number], {"fsdp": spot + 1 - 2 * col})
    for kind, dst in enumerate((ry_ref, rg_ref)):
        place = dst.at[across]
        arrive(place, r_recv.at[kind, 0])
        send(None, place, place, r_send.at[kind, 2], r_recv.at[kind, 2], {"rep": mate})
    for number in order:
        mine = mines[number]
        if inner == 2:
            arrive(yrecvs[number].at[0], y_recv.at[0, number])
            buffer = yrecvs[number]

            def add(index, carry):
                mine[index, col] = mine[index, col] + buffer[0, index]
                return carry

            lax.fori_loop(0, outer, add, 0)
        else:
            line_sum(number, inner, col, 1, yrecvs[number], lambda dest: mine.at[:, dest],
                     y_send, y_recv)
        line_sum(number, outer, row, inner, zrecvs[number], lambda dest: mine.at[dest, col],
                 z_send, z_recv)
        send(None, mine.at[row, col], xrecvs[number], x_send.at[number], x_recv.at[number],
             {"rep": across})
    for number in order:
        arrive(xrecvs[number], x_recv.at[number])
        total = mines[number][row, col].astype(jnp.float32) + xrecvs[number][...].astype(jnp.float32)
        out, half = pieces[number][1], pieces[number][3]
        place = columns(out, number, core)
        place[...] = total
        if half is not None:
            send(None, place, place, f_send.at[number], f_recv.at[number], {"rep": mate})
    for number in order:
        if pieces[number][3] is not None:
            arrive(columns(pieces[number][1], number, 1 - core), f_recv.at[number])
    for kind, dst in enumerate((ry_ref, rg_ref)):
        arrive(dst.at[mate], r_recv.at[kind, 1])
        arrive(dst.at[across_of(mate)], r_recv.at[kind, 2])
        src = y_ref if kind == 0 else g_ref
        pltpu.make_async_copy(src, dst.at[rank], q_sem.at[kind + 1]).wait()
    for there, finish_send in late:
        if there is None:
            finish_send()
        else:
            pl.when(there)(finish_send)


def reduce_grads(count, splits, ga, gb, gc, y_rows, g_rows):
    outer, inner = grid_of(count)
    kinds = len(splits) + 2
    rows_a, rows_b, rows_c = ga.shape[1], gb.shape[1], gc.shape[1]
    shapes = [(rows_a, width // 2, ga.dtype) for _, width in splits]
    shapes.append((rows_b, gb.shape[2] // 2, gb.dtype))
    shapes.append((rows_c, gc.shape[2], gc.dtype))
    dma = pltpu.SemaphoreType.DMA
    y_slots = 1 if inner == 2 else inner + 1
    z_slots = 1 if outer == 2 else outer + 1
    scratch = []
    for lead in ((outer, inner), (outer, inner), (y_slots, outer), (z_slots,), ()):
        scratch += [pltpu.VMEM(lead + (a, b), dtype) for a, b, dtype in shapes]
    scratch += [
        dma((kinds,)), dma((kinds,)), dma((kinds,)),
        dma((2, inner, kinds)), dma((y_slots, kinds)),
        dma((2, outer, kinds)), dma((z_slots, kinds)),
        dma((kinds,)), dma((kinds,)), dma((kinds,)), dma((kinds,)),
        dma((2, 3)), dma((2, 3)), dma((3,)),
    ]
    f32 = jnp.float32
    return pl.pallas_call(
        partial(reduce_kernel, outer, inner, splits),
        out_shape=(
            jax.ShapeDtypeStruct((rows_a, ga.shape[2]), f32),
            jax.ShapeDtypeStruct((rows_b, gb.shape[2]), f32),
            jax.ShapeDtypeStruct((rows_c, gc.shape[2]), f32),
            jax.ShapeDtypeStruct((4,) + y_rows.shape, y_rows.dtype),
            jax.ShapeDtypeStruct((4,) + g_rows.shape, g_rows.dtype),
        ),
        in_specs=[ANY] * 5,
        out_specs=(VMEM, VMEM, VMEM, ANY, ANY),
        scratch_shapes=scratch,
        compiler_params=pltpu.CompilerParams(
            collective_id=2, has_side_effects=True, vmem_limit_bytes=VMEM_LIMIT
        ),
        name="reduce_and_return",
    )(
        ga.reshape((outer, inner) + ga.shape[1:]),
        gb.reshape((outer, inner) + gb.shape[1:]),
        gc.reshape((outer, inner) + gc.shape[1:]),
        y_rows, g_rows,
    )


def home_kernel(tab_ref, ry_ref, rg_ref, y_ref, g_ref):
    base = lax.axis_index("rep") * y_ref.shape[0]

    def fetch(block, carry):
        index = tab_ref[DEST_AT + base + block]
        safe = jnp.maximum(index, 0)
        for src, dst in ((ry_ref, y_ref), (rg_ref, g_ref)):
            value = src[safe // SLOTS, safe % SLOTS]
            dst[block] = jnp.where(index >= 0, value, jnp.zeros_like(value))
        return carry

    lax.fori_loop(0, y_ref.shape[0], fetch, 0)


def bring_home(table, ry, rg, blocks):
    shape = jax.ShapeDtypeStruct((blocks,) + ry.shape[2:], ry.dtype)
    return pl.pallas_call(
        home_kernel,
        out_shape=(shape, shape),
        in_specs=[SMEM, VMEM, VMEM],
        out_specs=(VMEM, VMEM),
        compiler_params=pltpu.CompilerParams(vmem_limit_bytes=VMEM_LIMIT),
        name="place_rows",
    )(table, ry, rg)


def contract_rows(left_op, right_op):
    return lax.dot_general(
        left_op, right_op, (((0,), (0,)), ((), ())), preferred_element_type=jnp.float32
    )


def contract_cols(left_op, right_op):
    return lax.dot_general(
        left_op, right_op, (((1,), (1,)), ((), ())), preferred_element_type=jnp.float32
    )


def rms_norm(row_data, gain_vec):
    return (
        row_data
        * lax.rsqrt(jnp.mean(row_data * row_data, axis=-1, keepdims=True) + EPSILON)
        * gain_vec
    )


QB = 128
KPAD = 128


def band_table():
    query_pos = jnp.arange(QB, dtype=jnp.int32)[:, None] + KPAD
    key_pos = jnp.arange(QB + 2 * KPAD, dtype=jnp.int32)[None, :]
    return jnp.abs(query_pos - key_pos) <= RADIUS


def block_terms(row_start, queries, keys_pad, values_pad, global_keys, seg_query, seg_key_pad, seg_global):
    key_width = QB + 2 * KPAD
    query_blk = queries[row_start : row_start + QB].reshape(QB, H, DH)
    key_win = keys_pad[row_start : row_start + key_width]
    value_win = values_pad[row_start : row_start + key_width]
    local_scores = jnp.einsum("qhd,khd->hqk", query_blk, key_win, preferred_element_type=jnp.float32)
    global_scores = jnp.einsum("qhd,ghd->hqg", query_blk, global_keys, preferred_element_type=jnp.float32)
    seg_rows = seg_query[row_start : row_start + QB]
    allow_local = band_table() & (
        seg_rows[:, None] == seg_key_pad[row_start : row_start + key_width][None, :]
    )
    allow_global = seg_rows[:, None] == seg_global[None, :]
    masked_local = jnp.where(allow_local[None], local_scores, MASKED_SCORE)
    masked_global = jnp.where(allow_global[None], global_scores, MASKED_SCORE)
    return (query_blk, key_win, value_win, masked_local, masked_global)


def attend_forward(queries, keys_pad, values_pad, global_keys, global_values, seg_query, seg_key_pad, seg_global):
    mixed_blocks, kept = [], []
    for row_start in range(0, queries.shape[0], QB):
        query_blk, key_win, value_win, masked_local, masked_global = block_terms(
            row_start, queries, keys_pad, values_pad, global_keys, seg_query, seg_key_pad, seg_global
        )
        row_peak = jnp.maximum(
            jnp.max(masked_local, axis=-1, keepdims=True), jnp.max(masked_global, axis=-1, keepdims=True)
        )
        local_exp = jnp.exp(masked_local - row_peak)
        global_exp = jnp.exp(masked_global - row_peak)
        denominator = jnp.sum(local_exp, axis=-1, keepdims=True) + jnp.sum(global_exp, axis=-1, keepdims=True)
        local_low = (local_exp / denominator).astype(jnp.bfloat16)
        global_low = (global_exp / denominator).astype(jnp.bfloat16)
        mixed_rows = jnp.einsum("hqk,khd->qhd", local_low, value_win, preferred_element_type=jnp.float32)
        mixed_rows = mixed_rows + jnp.einsum(
            "hqg,ghd->qhd", global_low, global_values, preferred_element_type=jnp.float32
        )
        mixed_blocks.append(mixed_rows.reshape(QB, H * DH).astype(jnp.bfloat16))
        kept.append((row_peak, denominator))
    return (jnp.concatenate(mixed_blocks, axis=0), kept)


def attend_backward(grad_mixed, kept, queries, keys_pad, values_pad, global_keys, global_values, seg_query, seg_key_pad, seg_global):
    key_width = QB + 2 * KPAD
    row_count = queries.shape[0]
    grad_keys = jnp.zeros(keys_pad.shape, jnp.float32)
    grad_values = jnp.zeros(values_pad.shape, jnp.float32)
    grad_gkeys = jnp.zeros(global_keys.shape, jnp.float32)
    grad_gvalues = jnp.zeros(global_values.shape, jnp.float32)
    grad_query_blocks = []
    for number, row_start in enumerate(range(0, row_count, QB)):
        row_peak, denominator = kept[number]
        query_blk, key_win, value_win, masked_local, masked_global = block_terms(
            row_start, queries, keys_pad, values_pad, global_keys, seg_query, seg_key_pad, seg_global
        )
        local_probs = jnp.exp(masked_local - row_peak) / denominator
        global_probs = jnp.exp(masked_global - row_peak) / denominator
        grad_blk = grad_mixed[row_start : row_start + QB].reshape(QB, H, DH)
        local_dp = jnp.einsum("qhd,khd->hqk", grad_blk, value_win, preferred_element_type=jnp.float32)
        global_dp = jnp.einsum("qhd,ghd->hqg", grad_blk, global_values, preferred_element_type=jnp.float32)
        centre = jnp.sum(local_probs * local_dp, axis=-1, keepdims=True) + jnp.sum(
            global_probs * global_dp, axis=-1, keepdims=True
        )
        local_ds = (local_probs * (local_dp - centre)).astype(jnp.bfloat16)
        global_ds = (global_probs * (global_dp - centre)).astype(jnp.bfloat16)
        grad_query_rows = jnp.einsum("hqk,khd->qhd", local_ds, key_win, preferred_element_type=jnp.float32)
        grad_query_rows = grad_query_rows + jnp.einsum(
            "hqg,ghd->qhd", global_ds, global_keys, preferred_element_type=jnp.float32
        )
        grad_query_blocks.append(grad_query_rows.reshape(QB, H * DH).astype(jnp.bfloat16))
        grad_keys = grad_keys.at[row_start : row_start + key_width].add(
            jnp.einsum("hqk,qhd->khd", local_ds, query_blk, preferred_element_type=jnp.float32)
        )
        grad_values = grad_values.at[row_start : row_start + key_width].add(
            jnp.einsum("hqk,qhd->khd", local_probs.astype(jnp.bfloat16), grad_blk, preferred_element_type=jnp.float32)
        )
        grad_gkeys = grad_gkeys + jnp.einsum("hqg,qhd->ghd", global_ds, query_blk, preferred_element_type=jnp.float32)
        grad_gvalues = grad_gvalues + jnp.einsum(
            "hqg,qhd->ghd", global_probs.astype(jnp.bfloat16), grad_blk, preferred_element_type=jnp.float32
        )
    slot_count = global_keys.shape[0]
    grad_k = grad_keys[KPAD : KPAD + row_count].reshape(row_count, H * DH).astype(jnp.bfloat16)
    grad_v = grad_values[KPAD : KPAD + row_count].reshape(row_count, H * DH).astype(jnp.bfloat16)
    grad_gk = grad_gkeys.reshape(slot_count, H * DH).astype(jnp.bfloat16)
    grad_gv = grad_gvalues.reshape(slot_count, H * DH).astype(jnp.bfloat16)
    return (jnp.concatenate(grad_query_blocks, axis=0), grad_k, grad_v, grad_gk, grad_gv)


def layer_pass(row_data, cot_data, seg_tok, valid_tok, weights):
    (attn_gain, global_gain, query_weight, key_weight, value_weight, out_weight, ffn_gain,
     gate_weight, up_weight, down_weight) = weights
    row_count = row_data.shape[0]
    slot_count = row_count // GBLK
    valid_col = valid_tok.astype(jnp.float32)[:, None]
    inputs_f = row_data.astype(jnp.float32)
    gain_one = attn_gain.astype(jnp.float32)
    gain_side = global_gain.astype(jnp.float32)
    gain_two = ffn_gain.astype(jnp.float32)
    normed_f, norm_back_one = jax.vjp(rms_norm, inputs_f, gain_one)
    normed = normed_f.astype(jnp.bfloat16)
    side_sum = jnp.sum((normed.astype(jnp.float32) * valid_col).reshape(slot_count, GBLK, -1), axis=1)
    side_f, side_back = jax.vjp(rms_norm, side_sum, gain_side)
    side_normed = side_f.astype(jnp.bfloat16)

    def project(left, right):
        return jnp.dot(left, right, preferred_element_type=jnp.float32).astype(jnp.bfloat16)

    queries = project(normed, query_weight)
    keys_all = project(normed, key_weight)
    values_all = project(normed, value_weight)
    global_keys = project(side_normed, key_weight)
    global_values = project(side_normed, value_weight)
    seg_key = jnp.where(valid_tok, seg_tok, -2)
    seg_global = seg_key[::GBLK]
    keys_pad = jnp.pad(keys_all, ((KPAD, KPAD), (0, 0))).reshape(-1, H, DH)
    values_pad = jnp.pad(values_all, ((KPAD, KPAD), (0, 0))).reshape(-1, H, DH)
    seg_key_pad = jnp.pad(seg_key, (KPAD, KPAD), constant_values=-3)
    global_key_heads = global_keys.reshape(slot_count, H, DH)
    global_value_heads = global_values.reshape(slot_count, H, DH)
    attended, kept = attend_forward(
        queries, keys_pad, values_pad, global_key_heads, global_value_heads, seg_tok, seg_key_pad, seg_global
    )
    hidden_one = inputs_f + jnp.dot(attended, out_weight, preferred_element_type=jnp.float32)
    normed_two_f, norm_back_two = jax.vjp(rms_norm, hidden_one, gain_two)
    normed_two = normed_two_f.astype(jnp.bfloat16)
    gate_pre = jnp.dot(normed_two, gate_weight, preferred_element_type=jnp.float32)
    up_pre = jnp.dot(normed_two, up_weight, preferred_element_type=jnp.float32)
    activated, gelu_back = jax.vjp(partial(jax.nn.gelu, approximate=True), gate_pre)
    hidden_two = (activated * up_pre).astype(jnp.bfloat16)
    result = (
        valid_col * (hidden_one + jnp.dot(hidden_two, down_weight, preferred_element_type=jnp.float32))
    ).astype(jnp.bfloat16)
    grad_res = cot_data.astype(jnp.float32) * valid_col
    grad_out = grad_res.astype(jnp.bfloat16)
    grad_hidden = contract_cols(grad_out, down_weight)
    grad_down = contract_rows(hidden_two, grad_out)
    grad_gate = gelu_back(grad_hidden * up_pre)[0].astype(jnp.bfloat16)
    grad_up = (grad_hidden * activated).astype(jnp.bfloat16)
    grad_gate_w = contract_rows(normed_two, grad_gate)
    grad_up_w = contract_rows(normed_two, grad_up)
    grad_normed_two = contract_cols(grad_gate, gate_weight) + contract_cols(grad_up, up_weight)
    grad_norm_part, grad_gain_two = norm_back_two(grad_normed_two)
    grad_hidden_one = grad_res + grad_norm_part
    grad_branch = grad_hidden_one.astype(jnp.bfloat16)
    grad_out_w = contract_rows(attended, grad_branch)
    grad_attended = contract_cols(grad_branch, out_weight).astype(jnp.bfloat16)
    grad_q, grad_k, grad_v, grad_gk, grad_gv = attend_backward(
        grad_attended, kept, queries, keys_pad, values_pad, global_key_heads, global_value_heads,
        seg_tok, seg_key_pad, seg_global,
    )
    grad_query_w = contract_rows(normed, grad_q)
    grad_key_w = contract_rows(normed, grad_k) + contract_rows(side_normed, grad_gk)
    grad_value_w = contract_rows(normed, grad_v) + contract_rows(side_normed, grad_gv)
    grad_normed = (
        contract_cols(grad_q, query_weight) + contract_cols(grad_k, key_weight) + contract_cols(grad_v, value_weight)
    )
    grad_side_normed = contract_cols(grad_gk, key_weight) + contract_cols(grad_gv, value_weight)
    grad_side, grad_gain_side = side_back(grad_side_normed)
    spread_side = grad_side[:, None, :] * valid_col.reshape(slot_count, GBLK, 1)
    grad_normed = grad_normed + spread_side.reshape(row_count, -1)
    grad_inputs, grad_gain_one = norm_back_one(grad_normed)
    grad_rows = (grad_inputs + grad_hidden_one).astype(jnp.bfloat16)
    grads = (grad_gain_one, grad_gain_side, grad_query_w, grad_key_w, grad_value_w, grad_out_w,
             grad_gain_two, grad_gate_w, grad_up_w, grad_down)
    return (result, grad_rows, grads)


def per_device(count, layer_input, cotangent, lengths, attn_gain, global_gain, query_weight, key_weight,
               value_weight, out_weight, ffn_gain, gate_weight, up_weight, down_weight):
    micro, span, width = layer_input.shape
    hidden = gate_weight.shape[1]
    blocks = micro * span // BLK
    rank = lax.axis_index("rep")
    table = deal_table(lengths)
    wa = jnp.concatenate([query_weight, key_weight, value_weight, out_weight, gate_weight, up_weight], axis=1)
    part = attn_gain.shape[0]
    wc = jnp.pad(jnp.stack([attn_gain, global_gain, ffn_gain]), ((0, 13), (0, 128 - part)))
    splits = ((0, 4 * width), (4 * width, 2 * hidden))
    ga, gb, gc, rows, cots = gather_weights(
        count, splits, table,
        layer_input.reshape(blocks, BLK, width), cotangent.reshape(blocks, BLK, width), wa, down_weight, wc,
    )
    full = ga.reshape(width, -1)
    gains = jnp.transpose(gc[:, :3, :part], (1, 0, 2)).reshape(3, width)
    own = lax.dynamic_slice_in_dim(table, SEG_AT + rank * SLOTS, SLOTS)
    lens = lax.dynamic_slice_in_dim(table, LEN_AT + rank * SLOTS, SLOTS)
    seg_tok = jnp.repeat(own, BLK)
    valid_tok = (jnp.arange(BLK, dtype=jnp.int32)[None, :] < lens[:, None]).reshape(-1)
    heads = 4 * width
    weights = (
        gains[0], gains[1], full[:, :width], full[:, width : 2 * width], full[:, 2 * width : 3 * width],
        full[:, 3 * width : heads], gains[2], full[:, heads : heads + hidden],
        full[:, heads + hidden :], gb.reshape(-1, width),
    )
    result, grad_rows, grads = layer_pass(
        rows.reshape(-1, width), cots.reshape(-1, width), seg_tok, valid_tok, weights
    )
    grad_a = jnp.concatenate(
        [grads[2], grads[3], grads[4], grads[5], grads[7], grads[8]], axis=1
    ).astype(jnp.bfloat16).reshape(ga.shape)
    grad_b = grads[9].astype(jnp.bfloat16).reshape(gb.shape)
    grad_c = jnp.transpose(jnp.stack([grads[0], grads[1], grads[6]]).reshape(3, count, part), (1, 0, 2))
    grad_c = jnp.pad(grad_c, ((0, 0), (0, 5), (0, 128 - part)))
    oa, ob, oc, ry, rg = reduce_grads(
        count, splits, grad_a, grad_b, grad_c, result.reshape(SLOTS, BLK, width), grad_rows.reshape(SLOTS, BLK, width)
    )
    y_home, g_home = bring_home(table, ry, rg, blocks)
    return (
        y_home.reshape(layer_input.shape), g_home.reshape(layer_input.shape),
        oc[0, :part], oc[1, :part],
        oa[:, :width], oa[:, width : 2 * width], oa[:, 2 * width : 3 * width], oa[:, 3 * width : heads],
        oc[2, :part], oa[:, heads : heads + hidden], oa[:, heads + hidden :], ob,
    )


def solution(mesh):
    rows = P(None, ("rep", "fsdp"), None)
    vector, matrix = P("fsdp"), P("fsdp", None)
    return jax.shard_map(
        partial(per_device, mesh.shape["fsdp"]),
        mesh=mesh,
        in_specs=(rows, rows, P(None, ("rep", "fsdp")), vector, vector, matrix, matrix, matrix, matrix,
                  vector, matrix, matrix, matrix),
        out_specs=(rows, rows, vector, vector, matrix, matrix, matrix, matrix, vector, matrix, matrix, matrix),
        check_vma=False,
    )
```

time: 1590 us -> 534 us (0.34)
  waiting for transfers between devices: 1040 us -> 0 us
  Pallas kernels: 0 us -> 260 us
  matrix products: 243 us -> 137 us
  blocking collectives: 54.4 us -> 0 us
  local copies, waits for them, and re-layouts: 152 us -> 99.7 us
  other arithmetic: 68.5 us -> 26.2 us
  between operations: 21.1 us -> 3.35 us
    reduce_scatter x7 -> x0, waiting for transfers between devices: 356 us -> none  [the longest x1 77.1 us: per_device(): lax.psum_scatter(running[8].astype(jnp.bfloat16), 'fsdp', scatter_dimensi...]
    all_gather x11 -> x0, waiting for transfers between devices: 346 us -> none  [the longest x1 57.6 us: per_device(): lax.all_gather(gate_weight, 'fsdp', axis=0, tiled=True)]
    unnamed x20 -> x0, waiting for transfers between devices: 334 us -> none
    pallas_call x0 -> x5, Pallas kernels: none -> 260 us  [the longest x1 149 us: reduce_grads(): pl.pallas_call(partial(reduce_kernel, outer, inner, splits), out_shape=(j...]
    unnamed x2 -> x0, blocking collectives: 41.7 us -> none
    reshape x8 -> x0, local copies, waits for them, and re-layouts: 34.6 us -> none  [the longest x2 14.3 us: dealt_pass(): group_cot.reshape(block_count, -1)]
    dot_general x20 -> x9, matrix products: 51 us -> 21.9 us  [contract_rows(): lax.dot_general(left_op, right_op, (((0,), (0,)), ((), ())), preferred_el...]
    unnamed x663 -> x368, local copies, waits for them, and re-layouts: 32.1 us -> 34.1 us
  transfers between devices with their start and end apart: 19 -> 0, of which waited for: 16 -> 0; matrix products, arithmetic and copies ran while one was open for 16% -> 0% of each run, Pallas kernels for 0% -> 0%
where the time goes in v1:
time: 534 us; the launch traced here: 527 us
  Pallas kernels  260 us (49%)
  matrix products  137 us (26%)
  local copies, waits for them, and re-layouts  99.7 us (19%)
  other arithmetic  26.2 us (5%)
    pallas_call x1, Pallas kernels, reduce_grads(): pl.pallas_call(partial(reduce_kernel, outer, inner, splits), out_shape=(j...  149 us
    pallas_call x1, Pallas kernels, gather_weights(): pl.pallas_call(partial(gather_kernel, outer, inner, splits), out_shape=(j...  87.9 us
    unnamed x368, local copies, waits for them, and re-layouts  34.1 us
    dot_general x9, matrix products, contract_cols(): lax.dot_general(left_op, right_op, (((1,), (1,)), ((), ())), preferred_el...  22.8 us
    dot_general x9, matrix products, contract_rows(): lax.dot_general(left_op, right_op, (((0,), (0,)), ((), ())), preferred_el...  21.9 us
    dot_general x5, matrix products, attend_backward(): jnp.einsum('qhd,khd->hqk', grad_blk, value_win, preferred_element_type=jn...  13.3 us

profile of v1, /device:TPU:0, one launch (start us, length us, event | category | flops | bytes accessed | tf_op | source)
XLA Modules:
  0.0 526.6 jit_solution(9265617220769040168)
XLA Ops:
  3.4 5.9 %lens_exchange.1.lens_ref = s32[4,8,128]{2,1,0:T(8,128)} custom-call(s32[8,128]{1,0:T(8,128)} %pad.45.lens_ref), custom_call_target="tpu_custom_call" | custom-call | tf_op jit(solution)/shard_map/lens_exchange/pallas_call | solution.py:147
  9.2 10.5 %deal_table.1.tab_ref = s32[256]{0:T(256)} custom-call(s32[4,8,128]{2,1,0:T(8,128)} %lens_exchange.1.lens_ref), custom_call_target="tpu_custom_call" | custom-call | tf_op jit(solution)/shard_map/deal_table/pallas_call | solution.py:156
  31.2 87.9 %gather_and_deal.1 = (bf16[8,96,7168]{2,1,0:T(8,128)(2,1)}, bf16[8,256,768]{2,1,0:T(8,128)(2,1)}, bf16[8,16,128]{2,1,0:T(8,128)(2,1)}, bf16[10,64,768]{2,1,0:T(8,128)(2,1)}, bf16[10,64,768]{2,1,0:T(8,128)(2,1)}) custom-call(s32[256]{0:T(256)} %deal_table.1.tab_ref, bf16[24,64,768]{2,1,0:T(8,128)(2,1)} %bitcast.349, bf16[24,64,768]{2,1,0:T(8,128)(2,1)} %bitcast.350, ...), custom_call_target="tpu_custom_call" | custom-call | tf_op jit(solution)/shard_map/gather_and_deal/pallas_call | solution.py:412
  120.8 2.8 fusion.23
  132.6 2.2 convolution_convert_fusion.6
  134.8 2.2 convolution_convert_fusion.7
  137.1 2.5 convolution_convert_fusion.8
  157.3 2.2 copy.134
  167.2 2.2 copy.132
  197.0 2.2 fusion.175
  199.2 4.5 fusion.9
  203.7 9.8 %multiply_convert_fusion = (bf16[640,2048]{1,0:T(8,128)(2,1)}, bf16[640,2048]{1,0:T(8,128)(2,1)}, bf16[640,2048]{1,0:T(8,128)(2,1)S(1)}) fusion(f32[640,2048]{1,0:T(8,128)} %fusion.9, f32[640,2048]{1,0:T(8,128)S(1)} %fusion.175, bf16[640,768]{1,0:T(8,128)(2,1)S(1)} %multiply_convert_fusion.8, bf16[768,7168]{1,0:T(8,128)(2,1)S(1)} %bitcast.367), kind=kOutput, calls=%fused_computation.9 | convolution fusion | flops 2047344640 | bytes 22478848 | tf_op jit(solution)/shard_map/dot_general | solution.py:844
  213.5 6.0 %multiply_convert_fusion.7 = bf16[640,768]{1,0:T(8,128)(2,1)} fusion(f32[640,768]{1,0:T(8,128)S(1)} %get-tuple-element.244, bf16[640,2048]{1,0:T(8,128)(2,1)} %get-tuple-element.165, bf16[2048,768]{1,0:T(8,128)(2,1)S(1)} %bitcast.422, f32[640]{0:T(1024)S(1)} %copy-done.155), kind=kOutput, calls=%fused_computation.69 | convolution fusion | flops 2014740480 | bytes 8718848 | tf_op jit(solution)/shard_map/dot_general | solution.py:848
  219.5 2.2 fusion.7
  221.7 4.4 multiply_reduce_fusion.5
  228.2 3.2 fusion.37
  231.4 4.1 convolution_convert_fusion
  237.7 4.2 convolution_convert_fusion.1
  241.9 4.0 convolution_convert_fusion.2
  245.9 2.2 convolution_convert_fusion.5
  264.9 2.7 multiply_reduce_fusion.13
  267.6 2.7 multiply_reduce_fusion.12
  289.9 3.2 multiply_reduce_fusion.1
  298.6 3.2 multiply_reduce_fusion.2
  307.4 3.2 multiply_reduce_fusion.3
  316.1 2.4 multiply_reduce_fusion.4
  339.0 2.3 fusion.84
  345.5 2.3 fusion.74
  347.8 3.3 fusion.26
  353.4 4.1 fusion.38
  366.4 148.9 %reduce_and_return.1 = (f32[96,7168]{1,0:T(8,128)}, f32[256,768]{1,0:T(8,128)}, f32[8,128]{1,0:T(8,128)}, bf16[4,10,64,768]{3,2,1,0:T(8,128)(2,1)}, bf16[4,10,64,768]{3,2,1,0:T(8,128)(2,1)}) custom-call(bf16[4,2,96,7168]{3,2,1,0:T(8,128)(2,1)} %constant_dynamic-update-slice_fusion.16.ga_ref, bf16[4,2,256,768]{3,2,1,0:T(8,128)(2,1)} %bitcast.348, ...), custom_call_target="tpu_custom_call" | custom-call | tf_op jit(solution)/shard_map/reduce_and_return/pallas_call | solution.py:640
  515.3 6.7 %place_rows.1 = (bf16[24,64,768]{2,1,0:T(8,128)(2,1)}, bf16[24,64,768]{2,1,0:T(8,128)(2,1)}) custom-call(s32[256]{0:T(256)} %deal_table.1.tab_ref, bf16[4,10,64,768]{3,2,1,0:T(8,128)(2,1)} %get-tuple-element.149.ry_ref, bf16[4,10,64,768]{3,2,1,0:T(8,128)(2,1)} %get-tuple-element.150.rg_ref), custom_call_target="tpu_custom_call" | custom-call | tf_op jit(solution)/shard_map/place_rows/pallas_call | solution.py:680
  (580 shorter events, 172.9 us)
Async XLA Ops:
  0.6 29.5 %copy-start.109 = (bf16[96,2048]{1,0:T(8,128)(2,1)S(1)}, bf16[96,2048]{1,0:T(8,128)(2,1)}, u32[]{:S(2)}) copy-start(bf16[96,2048]{1,0:T(8,128)(2,1)} %param.44) | copy-start | bytes 1179652
  120.7 10.1 %copy-start.121 = (f32[768]{0:T(1024)}, f32[768]{0:T(1024)S(1)}, u32[]{:S(2)}) copy-start(f32[768]{0:T(1024)S(1)} %reshape.1152) | copy-start | bytes 9220
  120.8 6.1 %copy-start.144 = (f32[768]{0:T(1024)}, f32[768]{0:T(1024)S(1)}, u32[]{:S(2)}) copy-start(f32[768]{0:T(1024)S(1)} %reshape.1154) | copy-start | bytes 9220
  124.3 6.5 %copy-start.142 = (f32[640]{0:T(1024)}, f32[640]{0:T(1024)S(1)}, u32[]{:S(2)}) copy-start(f32[640]{0:T(1024)S(1)} %rsqrt.37) | copy-start | bytes 7684
  125.1 5.7 %copy-start.164 = (f32[40]{0:T(128)}, f32[40]{0:T(128)S(1)}, u32[]{:S(2)}) copy-start(f32[40]{0:T(128)S(1)} %multiply_reduce_fusion.16) | copy-start | bytes 484
  125.2 5.7 %copy-start.162 = (f32[40]{0:T(128)}, f32[40]{0:T(128)S(1)}, u32[]{:S(2)}) copy-start(f32[40]{0:T(128)S(1)} %fusion.141) | copy-start | bytes 484
  140.6 16.7 %copy-start.33 = (bf16[128,768]{0,1:T(8,128)(2,1)}, bf16[128,768]{0,1:T(8,128)(2,1)S(1)}, u32[]{:S(2)}) copy-start(bf16[128,768]{0,1:T(8,128)(2,1)S(1)} %copy.133) | copy-start | bytes 589828
  141.8 15.5 %copy-start.36 = (bf16[128,768]{0,1:T(8,128)(2,1)}, bf16[128,768]{0,1:T(8,128)(2,1)S(1)}, u32[]{:S(2)}) copy-start(bf16[128,768]{0,1:T(8,128)(2,1)S(1)} %copy.128) | copy-start | bytes 589828
  157.3 6.5 %copy-start.52 = (bf16[384,768]{1,0:T(8,128)(2,1)S(1)}, bf16[384,768]{1,0:T(8,128)(2,1)}, u32[]{:S(2)}) copy-start(bf16[384,768]{1,0:T(8,128)(2,1)} %get-tuple-element.184) | copy-start | bytes 1769476
  157.3 7.6 %copy-start.51 = (bf16[384,768]{1,0:T(8,128)(2,1)S(1)}, bf16[384,768]{1,0:T(8,128)(2,1)}, u32[]{:S(2)}) copy-start(bf16[384,768]{1,0:T(8,128)(2,1)} %get-tuple-element.185) | copy-start | bytes 1769476
  194.8 26.9 %copy-start.23 = (f32[640,768]{1,0:T(8,128)}, f32[640,768]{1,0:T(8,128)S(1)}, u32[]{:S(2)}) copy-start(f32[640,768]{1,0:T(8,128)S(1)} %get-tuple-element.244) | copy-start | bytes 5898244
  195.4 26.3 %copy-start.150 = (f32[640]{0:T(1024)}, f32[640]{0:T(1024)S(1)}, u32[]{:S(2)}) copy-start(f32[640]{0:T(1024)S(1)} %fusion.140) | copy-start | bytes 7684
  197.0 6.7 %copy-start.82 = (bf16[640,768]{1,0:T(8,128)(2,1)}, bf16[640,768]{1,0:T(8,128)(2,1)S(1)}, u32[]{:S(2)}) copy-start(bf16[640,768]{1,0:T(8,128)(2,1)S(1)} %multiply_convert_fusion.8) | copy-start | bytes 2949124
  203.7 9.8 %copy-start.155 = (f32[640]{0:T(1024)S(1)}, f32[640]{0:T(1024)}, u32[]{:S(2)}) copy-start(f32[640]{0:T(1024)} %reshape.1156) | copy-start | bytes 7684
  213.5 8.3 %copy-start.167 = (bf16[640,2048]{1,0:T(8,128)(2,1)}, bf16[640,2048]{1,0:T(8,128)(2,1)S(1)}, u32[]{:S(2)}) copy-start(bf16[640,2048]{1,0:T(8,128)(2,1)S(1)} %get-tuple-element.167) | copy-start | bytes 7864324
  213.5 6.0 %copy-start.169 = (bf16[640,2048]{1,0:T(8,128)(2,1)S(1)}, bf16[640,2048]{1,0:T(8,128)(2,1)}, u32[]{:S(2)}) copy-start(bf16[640,2048]{1,0:T(8,128)(2,1)} %get-tuple-element.166) | copy-start | bytes 7864324
  231.4 14.6 %copy-start.21 = (f32[640,768]{1,0:T(8,128)}, f32[640,768]{1,0:T(8,128)S(1)}, u32[]{:S(2)}) copy-start(f32[640,768]{1,0:T(8,128)S(1)} %get-tuple-element.175) | copy-start | bytes 5898244
  264.8 5.5 %copy-start.116 = (bf16[128,768]{0,1:T(8,128)(2,1)S(1)}, bf16[128,768]{0,1:T(8,128)(2,1)}, u32[]{:S(2)}) copy-start(bf16[128,768]{0,1:T(8,128)(2,1)} %copy.143) | copy-start | bytes 589828
  264.8 5.5 %copy-start.124 = (bf16[40,12,64]{2,0,1:T(8,128)(2,1)S(1)}, bf16[40,12,64]{2,0,1:T(8,128)(2,1)}, u32[]{:S(2)}) copy-start(bf16[40,12,64]{2,0,1:T(8,128)(2,1)} %copy.116) | copy-start | bytes 184324
  264.8 5.5 %copy-start.132 = (f32[12,128]{1,0:T(8,128)S(1)}, f32[12,128]{1,0:T(8,128)}, u32[]{:S(2)}) copy-start(f32[12,128]{1,0:T(8,128)} %copy-done.131) | copy-start | bytes 18436
  264.9 6.9 %copy-start.63 = (f32[12,128,40]{1,2,0:T(8,128)S(1)}, f32[12,128,40]{1,2,0:T(8,128)}, u32[]{:S(2)}) copy-start(f32[12,128,40]{1,2,0:T(8,128)} %get-tuple-element.238) | copy-start | bytes 737284
  264.9 6.9 %copy-start.118 = (bf16[128,768]{0,1:T(8,128)(2,1)S(1)}, bf16[128,768]{0,1:T(8,128)(2,1)}, u32[]{:S(2)}) copy-start(bf16[128,768]{0,1:T(8,128)(2,1)} %copy.146) | copy-start | bytes 589828
  264.9 6.9 %copy-start.136 = (f32[12,128]{1,0:T(8,128)S(1)}, f32[12,128]{1,0:T(8,128)}, u32[]{:S(2)}) copy-start(f32[12,128]{1,0:T(8,128)} %copy-done.134) | copy-start | bytes 18436
  264.9 8.4 %copy-start.67 = (f32[12,128,40]{1,2,0:T(8,128)S(1)}, f32[12,128,40]{1,2,0:T(8,128)}, u32[]{:S(2)}) copy-start(f32[12,128,40]{1,2,0:T(8,128)} %get-tuple-element.242) | copy-start | bytes 737284
  264.9 8.4 %copy-start.120 = (bf16[128,768]{0,1:T(8,128)(2,1)S(1)}, bf16[128,768]{0,1:T(8,128)(2,1)}, u32[]{:S(2)}) copy-start(bf16[128,768]{0,1:T(8,128)(2,1)} %copy.149) | copy-start | bytes 589828
  264.9 8.4 %copy-start.141 = (f32[12,128]{1,0:T(8,128)S(1)}, f32[12,128]{1,0:T(8,128)}, u32[]{:S(2)}) copy-start(f32[12,128]{1,0:T(8,128)} %copy-done.139) | copy-start | bytes 18436
  267.6 5.9 %copy-start.114 = (bf16[128,768]{0,1:T(8,128)(2,1)S(1)}, bf16[128,768]{0,1:T(8,128)(2,1)}, u32[]{:S(2)}) copy-start(bf16[128,768]{0,1:T(8,128)(2,1)} %copy.137) | copy-start | bytes 589828
  267.6 5.9 %copy-start.126 = (f32[12,128]{1,0:T(8,128)S(1)}, f32[12,128]{1,0:T(8,128)}, u32[]{:S(2)}) copy-start(f32[12,128]{1,0:T(8,128)} %copy-done.125) | copy-start | bytes 18436
  324.7 8.2 %copy-start.97 = (bf16[128,768]{1,0:T(8,128)(2,1)S(1)}, bf16[128,768]{1,0:T(8,128)(2,1)}, u32[]{:S(2)}) copy-start(bf16[128,768]{1,0:T(8,128)(2,1)} %copy.155) | copy-start | bytes 589828
  325.5 7.5 %copy-start.96 = (bf16[128,768]{1,0:T(8,128)(2,1)S(1)}, bf16[128,768]{1,0:T(8,128)(2,1)}, u32[]{:S(2)}) copy-start(bf16[128,768]{1,0:T(8,128)(2,1)} %copy.156) | copy-start | bytes 589828
  333.0 12.4 %copy-start.148 = (bf16[640,768]{1,0:T(8,128)(2,1)}, bf16[640,768]{1,0:T(8,128)(2,1)S(1)}, u32[]{:S(2)}) copy-start(bf16[640,768]{1,0:T(8,128)(2,1)S(1)} %constant_dynamic-update-slice_fusion.11) | copy-start | bytes 2949124
  515.3 8.0 %copy-start.50 = (f32[96,7168]{1,0:T(8,128)S(1)}, f32[96,7168]{1,0:T(8,128)}, u32[]{:S(2)}) copy-start(f32[96,7168]{1,0:T(8,128)} %get-tuple-element.154) | copy-start | bytes 8257540
  (143 other events, 314.0 us)

commit v2 on v1

--- a/solution.py
+++ b/solution.py
@@ -438,10 +438,11 @@
 
 
 def reduce_kernel(
-    outer, inner, splits, ga_ref, gb_ref, gc_ref, y_ref, g_ref,
-    oa_ref, ob_ref, oc_ref, ry_ref, rg_ref, *scratch,
+    outer, inner, kinds, *refs
 ):
-    kinds = len(splits) + 2
+    grads, (y_ref, g_ref) = refs[:kinds], refs[kinds : kinds + 2]
+    totals, (ry_ref, rg_ref) = refs[kinds + 2 : 2 * kinds + 2], refs[2 * kinds + 2 : 2 * kinds + 4]
+    scratch = refs[2 * kinds + 4 :]
     mines, crecvs, yrecvs, zrecvs, xrecvs = (
         scratch[kinds * i : kinds * (i + 1)] for i in range(5)
     )
@@ -452,9 +453,8 @@
     core = rank % 2
     row, col = spot // inner, spot % inner
     mate, across = core_of(rank), across_of(rank)
-    pieces = [(ga_ref, oa_ref, start, width // 2) for start, width in splits]
-    pieces.append((gb_ref, ob_ref, 0, gb_ref.shape[3] // 2))
-    pieces.append((gc_ref, oc_ref, 0, None))
+    pieces = [(src, dst, 0, src.shape[3] // 2) for src, dst in zip(grads[:-1], totals)]
+    pieces.append((grads[-1], totals[-1], 0, None))
 
     barrier = pltpu.get_barrier_semaphore()
     neighbours = (
@@ -616,13 +616,11 @@
             pl.when(there)(finish_send)
 
 
-def reduce_grads(count, splits, ga, gb, gc, y_rows, g_rows):
+def reduce_grads(count, grads, y_rows, g_rows):
     outer, inner = grid_of(count)
-    kinds = len(splits) + 2
-    rows_a, rows_b, rows_c = ga.shape[1], gb.shape[1], gc.shape[1]
-    shapes = [(rows_a, width // 2, ga.dtype) for _, width in splits]
-    shapes.append((rows_b, gb.shape[2] // 2, gb.dtype))
-    shapes.append((rows_c, gc.shape[2], gc.dtype))
+    kinds = len(grads)
+    shapes = [(grad.shape[1], grad.shape[2] // 2, grad.dtype) for grad in grads[:-1]]
+    shapes.append(grads[-1].shape[1:] + (grads[-1].dtype,))
     dma = pltpu.SemaphoreType.DMA
     y_slots = 1 if inner == 2 else inner + 1
     z_slots = 1 if outer == 2 else outer + 1
@@ -636,29 +634,20 @@
         dma((kinds,)), dma((kinds,)), dma((kinds,)), dma((kinds,)),
         dma((2, 3)), dma((2, 3)), dma((3,)),
     ]
-    f32 = jnp.float32
     return pl.pallas_call(
-        partial(reduce_kernel, outer, inner, splits),
-        out_shape=(
-            jax.ShapeDtypeStruct((rows_a, ga.shape[2]), f32),
-            jax.ShapeDtypeStruct((rows_b, gb.shape[2]), f32),
-            jax.ShapeDtypeStruct((rows_c, gc.shape[2]), f32),
+        partial(reduce_kernel, outer, inner, kinds),
+        out_shape=tuple(jax.ShapeDtypeStruct(grad.shape[1:], jnp.float32) for grad in grads) + (
             jax.ShapeDtypeStruct((4,) + y_rows.shape, y_rows.dtype),
             jax.ShapeDtypeStruct((4,) + g_rows.shape, g_rows.dtype),
         ),
-        in_specs=[ANY] * 5,
-        out_specs=(VMEM, VMEM, VMEM, ANY, ANY),
+        in_specs=[ANY] * (kinds + 2),
+        out_specs=(VMEM,) * kinds + (ANY, ANY),
         scratch_shapes=scratch,
         compiler_params=pltpu.CompilerParams(
             collective_id=2, has_side_effects=True, vmem_limit_bytes=VMEM_LIMIT
         ),
         name="reduce_and_return",
-    )(
-        ga.reshape((outer, inner) + ga.shape[1:]),
-        gb.reshape((outer, inner) + gb.shape[1:]),
-        gc.reshape((outer, inner) + gc.shape[1:]),
-        y_rows, g_rows,
-    )
+    )(*(grad.reshape((outer, inner) + grad.shape[1:]) for grad in grads), y_rows, g_rows)
 
 
 def home_kernel(tab_ref, ry_ref, rg_ref, y_ref, g_ref):
@@ -687,199 +676,441 @@
     )(table, ry, rg)
 
 
-def contract_rows(left_op, right_op):
-    return lax.dot_general(
-        left_op, right_op, (((0,), (0,)), ((), ())), preferred_element_type=jnp.float32
+D = H * DH
+ROWS = SLOTS * BLK
+SIDES = SLOTS * (BLK // GBLK)
+SIDE_ROWS = 48
+ALL_ROWS = ROWS + SIDE_ROWS
+QT = 128
+WIN = 384
+TILES = ROWS // QT
+QUAD = 256
+FF_TILE = 256
+GELU_C = 0.7978845608028654
+GELU_A = 0.044715
+F32, BF16 = jnp.float32, jnp.bfloat16
+
+
+def mm(left, right):
+    return lax.dot_general(left, right, (((1,), (0,)), ((), ())), preferred_element_type=F32)
+
+
+def mm_cols(left, right):
+    return lax.dot_general(left, right, (((1,), (1,)), ((), ())), preferred_element_type=F32)
+
+
+def mm_rows(left, right):
+    return lax.dot_general(left, right, (((0,), (0,)), ((), ())), preferred_element_type=F32)
+
+
+def iota(shape, axis):
+    return lax.broadcasted_iota(jnp.int32, shape, axis)
+
+
+def pick_by(index, values, other):
+    out = jnp.full(index.shape, other, jnp.int32)
+    for number, value in enumerate(values):
+        out = jnp.where(index == number, value, out)
+    return out
+
+
+def slot_info(tab_ref, rank):
+    seg = [tab_ref[SEG_AT + rank * SLOTS + slot] for slot in range(SLOTS)]
+    length = [tab_ref[LEN_AT + rank * SLOTS + slot] for slot in range(SLOTS)]
+    return seg, length
+
+
+def valid_column(tab_ref, rank):
+    _, length = slot_info(tab_ref, rank)
+    row = iota((ROWS, 1), 0)
+    return ((row % BLK) < pick_by(row // BLK, length, 0)).astype(F32)
+
+
+def pooling(tab_ref, rank):
+    _, length = slot_info(tab_ref, rank)
+    row = iota((1, ROWS), 1)
+    block = jnp.where((row % BLK) < pick_by(row // BLK, length, 0), row // GBLK, -1)
+    return jnp.where(iota((SIDE_ROWS, ROWS), 0) == block, 1.0, 0.0).astype(BF16)
+
+
+def key_segments(tab_ref, rank, first_block, index):
+    blocks = WIN // BLK
+    base = rank * SLOTS + first_block
+    seg = [tab_ref[SEG_AT + base + step] for step in range(blocks)]
+    length = [tab_ref[LEN_AT + base + step] for step in range(blocks)]
+    alive = (index % BLK) < pick_by(index // BLK, length, 0)
+    return jnp.where(alive, pick_by(index // BLK, seg, -2), -2)
+
+
+def side_segments(tab_ref, rank, index):
+    seg, length = slot_info(tab_ref, rank)
+    per = BLK // GBLK
+    alive = (index % per) * GBLK < pick_by(index // per, length, 0)
+    return jnp.where(alive, pick_by(index // per, seg, -2), -2)
+
+
+def tile_bias(tab_ref, rank, tile, first_row, keys_axis):
+    qs, ks, gs = ((QT, 1), (1, WIN), (1, SIDE_ROWS)) if keys_axis == 1 else ((1, QT), (WIN, 1), (SIDE_ROWS, 1))
+    q_index = iota(qs, 1 - keys_axis)
+    k_index = iota(ks, keys_axis)
+    g_index = iota(gs, keys_axis)
+    base = SEG_AT + rank * SLOTS + tile * (QT // BLK)
+    q_seg = pick_by(q_index // BLK, [tab_ref[base + step] for step in range(QT // BLK)], -1)
+    k_seg = key_segments(tab_ref, rank, first_row // BLK, k_index)
+    g_seg = side_segments(tab_ref, rank, g_index)
+    gap = (q_index + tile * QT) - (k_index + first_row)
+    local = (jnp.abs(gap) <= RADIUS) & (q_seg == k_seg)
+    return jnp.where(local, 0.0, MASKED_SCORE), jnp.where(q_seg == g_seg, 0.0, MASKED_SCORE)
+
+
+def window_start(tile):
+    return pl.multiple_of(jnp.clip(tile - 1, 0, TILES - WIN // QT) * QT, QT)
+
+
+def head_stack(rows):
+    lane = iota(rows.shape, 1) // DH
+    zero = jnp.zeros_like(rows)
+    return jnp.concatenate([jnp.where(lane == head, rows, zero) for head in range(QUAD // DH)], axis=0)
+
+
+def head_merge(stacked):
+    lane = iota((QT, QUAD), 1) // DH
+    out = stacked[:QT]
+    for head in range(1, QUAD // DH):
+        out = jnp.where(lane == head, stacked[head * QT : (head + 1) * QT], out)
+    return out
+
+
+def gains_of(gc_ref):
+    count = gc_ref.shape[0]
+    part = D // count
+    lane, column = iota((128, D), 0), iota((128, D), 1)
+    total = None
+    for shard in range(count):
+        pick = jnp.where((column == lane + shard * part) & (lane < part), 1.0, 0.0).astype(BF16)
+        term = mm(gc_ref[shard], pick)
+        total = term if total is None else total + term
+    return total
+
+
+def three_way(value):
+    high = value.astype(BF16)
+    rest = value - high.astype(F32)
+    middle = rest.astype(BF16)
+    return high, middle, (rest - middle.astype(F32)).astype(BF16)
+
+
+def spread_gain_grads(value, dc_ref):
+    count = dc_ref.shape[0]
+    part = D // count
+    column, lane = iota((D, 128), 0), iota((D, 128), 1)
+    parts = three_way(value)
+    for shard in range(count):
+        pick = jnp.where((column == lane + shard * part) & (lane < part), 1.0, 0.0).astype(BF16)
+        dc_ref[shard] = mm(parts[0], pick) + mm(parts[1], pick) + mm(parts[2], pick)
+
+
+def mean_square(value):
+    return jnp.mean(value * value, axis=-1, keepdims=True)
+
+
+def forward_norm(tab_ref, rank, x_ref, gains, n_ref):
+    for tile in range(TILES):
+        rows = pl.ds(tile * QT, QT)
+        value = x_ref[rows, :].astype(F32)
+        n_ref[rows, :] = (value * lax.rsqrt(mean_square(value) + EPSILON) * gains[0:1]).astype(BF16)
+    side = mm(pooling(tab_ref, rank), n_ref[:ROWS, :])
+    n_ref[ROWS:, :] = (side * lax.rsqrt(mean_square(side) + EPSILON) * gains[1:2]).astype(BF16)
+
+
+def forward_project(n_ref, w_ref, qkv_ref):
+    def step(tile, carry):
+        cols = pl.ds(pl.multiple_of(tile * QUAD, QUAD), QUAD)
+        qkv_ref[:, cols] = mm(n_ref[...], w_ref[:, cols]).astype(BF16)
+        return carry
+
+    lax.fori_loop(0, 3 * D // QUAD, step, 0)
+
+
+def forward_attention(tab_ref, rank, qkv_ref, att_ref, lse_ref):
+    def step(tile, carry):
+        first = window_start(tile)
+        bias, side_bias = tile_bias(tab_ref, rank, tile, first, 1)
+        rows = pl.ds(pl.multiple_of(tile * QT, QT), QT)
+        window = pl.ds(first, WIN)
+        lse = jnp.zeros((QT, 128), F32)
+        lane = iota((QT, 128), 1)
+        for quad in range(D // QUAD):
+            low = quad * QUAD
+            query = head_stack(qkv_ref[rows, low : low + QUAD])
+            scores = mm_cols(query, qkv_ref[window, D + low : D + low + QUAD])
+            side_scores = mm_cols(query, qkv_ref[ROWS:, D + low : D + low + QUAD])
+            local, sides, scale = [], [], []
+            for head in range(QUAD // DH):
+                part = slice(head * QT, (head + 1) * QT)
+                one = scores[part] + bias
+                two = side_scores[part] + side_bias
+                peak = jnp.maximum(
+                    jnp.max(one, axis=-1, keepdims=True), jnp.max(two, axis=-1, keepdims=True)
+                )
+                one, two = jnp.exp(one - peak), jnp.exp(two - peak)
+                total = jnp.sum(one, axis=-1, keepdims=True) + jnp.sum(two, axis=-1, keepdims=True)
+                local.append(one.astype(BF16))
+                sides.append(two.astype(BF16))
+                scale.append(1.0 / total)
+                lse = jnp.where(lane == quad * (QUAD // DH) + head, peak + jnp.log(total), lse)
+            mixed = mm(jnp.concatenate(local, axis=0), qkv_ref[window, 2 * D + low : 2 * D + low + QUAD])
+            mixed = mixed + mm(
+                jnp.concatenate(sides, axis=0), qkv_ref[ROWS:, 2 * D + low : 2 * D + low + QUAD]
+            )
+            mixed = mixed * jnp.concatenate(scale, axis=0)
+            att_ref[rows, low : low + QUAD] = head_merge(mixed).astype(BF16)
+        lse_ref[tile] = jnp.transpose(lse)[:16]
+        return carry
+
+    lax.fori_loop(0, TILES, step, 0)
+
+
+def feed_forward(tab_ref, rank, x_ref, cot_ref, att_ref, gains, w_ref, wb_ref,
+                 y_ref, gh_ref, ga_ref, dg_ref, db_ref, do_ref,
+                 h1_ref, nt_ref, ntt_ref, gres_ref, h2_ref, gg_ref, gu_ref, gn_ref):
+    hidden = wb_ref.shape[0]
+    gate_at = 4 * D
+    valid = valid_column(tab_ref, rank)
+    gain = gains[2:3]
+    for tile in range(TILES):
+        rows = pl.ds(tile * QT, QT)
+        value = x_ref[rows, :].astype(F32) + mm(att_ref[rows, :], w_ref[:, 3 * D : 4 * D])
+        h1_ref[rows, :] = value
+        normed = (value * lax.rsqrt(mean_square(value) + EPSILON) * gain).astype(BF16)
+        nt_ref[rows, :] = normed
+        ntt_ref[:, tile * QT : (tile + 1) * QT] = jnp.transpose(normed)
+        gres_ref[rows, :] = (cot_ref[rows, :].astype(F32) * valid[tile * QT : (tile + 1) * QT]).astype(BF16)
+
+    def inward(tile, carry):
+        at = pl.multiple_of(tile * FF_TILE, FF_TILE)
+        cols = pl.ds(at, FF_TILE)
+        gate = mm(nt_ref[...], w_ref[:, pl.ds(gate_at + at, FF_TILE)])
+        up = mm(nt_ref[...], w_ref[:, pl.ds(gate_at + hidden + at, FF_TILE)])
+        back = mm_cols(gres_ref[...], wb_ref[cols, :])
+        square = gate * gate
+        bend = jnp.tanh(GELU_C * (gate * (1.0 + GELU_A * square)))
+        half = 0.5 * (1.0 + bend)
+        act = gate * half
+        slope = half + (0.5 * GELU_C) * gate * (1.0 - bend * bend) * (1.0 + (3.0 * GELU_A) * square)
+        h2_ref[:, cols] = (act * up).astype(BF16)
+        gg_ref[:, cols] = (back * up * slope).astype(BF16)
+        gu_ref[:, cols] = (back * act).astype(BF16)
+        return carry
+
+    lax.fori_loop(0, hidden // FF_TILE, inward, 0)
+
+    def outward(tile, carry):
+        cols = pl.ds(pl.multiple_of(tile * QUAD, QUAD), QUAD)
+        value = h1_ref[:, cols] + mm(h2_ref[...], wb_ref[:, cols])
+        y_ref[:, cols] = (value * valid).astype(BF16)
+        gn_ref[:, cols] = mm_cols(gg_ref[...], w_ref[cols, gate_at : gate_at + hidden]) + mm_cols(
+            gu_ref[...], w_ref[cols, gate_at + hidden :]
+        )
+        return carry
+
+    lax.fori_loop(0, D // QUAD, outward, 0)
+
+    def weights(tile, carry):
+        at = pl.multiple_of(tile * FF_TILE, FF_TILE)
+        cols = pl.ds(at, FF_TILE)
+        dg_ref[:, cols] = mm(ntt_ref[...], gg_ref[:, cols]).astype(BF16)
+        dg_ref[:, pl.ds(hidden + at, FF_TILE)] = mm(ntt_ref[...], gu_ref[:, cols]).astype(BF16)
+        db_ref[cols, :] = mm_rows(h2_ref[:, cols], gres_ref[...]).astype(BF16)
+        return carry
+
+    lax.fori_loop(0, hidden // FF_TILE, weights, 0)
+
+    gain_grad = jnp.zeros((1, D), F32)
+    for tile in range(TILES):
+        rows = pl.ds(tile * QT, QT)
+        value, grad = h1_ref[rows, :], gn_ref[rows, :]
+        root = lax.rsqrt(mean_square(value) + EPSILON)
+        unit = value * root
+        gain_grad = gain_grad + jnp.sum(grad * unit, axis=0, keepdims=True)
+        grad = grad * gain
+        grad = gres_ref[rows, :].astype(F32) + root * (
+            grad - unit * jnp.mean(grad * unit, axis=-1, keepdims=True)
+        )
+        gh_ref[rows, :] = grad
+        low = grad.astype(BF16)
+        nt_ref[rows, :] = low
+        ga_ref[rows, :] = mm_cols(low, w_ref[:, 3 * D : 4 * D]).astype(BF16)
+
+    def out_weight(tile, carry):
+        cols = pl.ds(pl.multiple_of(tile * QUAD, QUAD), QUAD)
+        do_ref[cols, :] = mm_rows(att_ref[:, cols], nt_ref[...]).astype(BF16)
+        return carry
+
+    lax.fori_loop(0, D // QUAD, out_weight, 0)
+    return gain_grad
+
+
+def backward_attention(tab_ref, rank, qkv_ref, att_ref, ga_ref, lse_ref, dqkv_ref, dk_ref, dv_ref):
+    dk_ref[...] = jnp.zeros_like(dk_ref)
+    dv_ref[...] = jnp.zeros_like(dv_ref)
+    heads = QUAD // DH
+    marks = jnp.where(iota((16, D), 1) // DH == iota((16, D), 0), 1.0, 0.0).astype(BF16)
+
+    def step(tile, carry):
+        first = window_start(tile)
+        bias, side_bias = tile_bias(tab_ref, rank, tile, first, 0)
+        bias = jnp.concatenate([bias, side_bias], axis=0)
+        rows = pl.ds(pl.multiple_of(tile * QT, QT), QT)
+        window = pl.ds(first, WIN)
+        product = ga_ref[rows, :].astype(F32) * att_ref[rows, :].astype(F32)
+        high = product.astype(BF16)
+        rest = (product - high.astype(F32)).astype(BF16)
+        centre = mm_cols(marks, high) + mm_cols(marks, rest)
+        lse = lse_ref[tile]
+        for quad in range(D // QUAD):
+            low = quad * QUAD
+            query = head_stack(qkv_ref[rows, low : low + QUAD])
+            grad = head_stack(ga_ref[rows, low : low + QUAD])
+            keys = jnp.concatenate(
+                [qkv_ref[window, D + low : D + low + QUAD], qkv_ref[ROWS:, D + low : D + low + QUAD]], axis=0
+            )
+            values = jnp.concatenate(
+                [qkv_ref[window, 2 * D + low : 2 * D + low + QUAD],
+                 qkv_ref[ROWS:, 2 * D + low : 2 * D + low + QUAD]], axis=0
+            )
+            scores = mm_cols(keys, query)
+            slopes = mm_cols(values, grad)
+            probs, grads = [], []
+            for head in range(heads):
+                part = slice(head * QT, (head + 1) * QT)
+                number = quad * heads + head
+                prob = jnp.exp(scores[:, part] + bias - lse[number : number + 1])
+                probs.append(prob.astype(BF16))
+                grads.append((prob * (slopes[:, part] - centre[number : number + 1])).astype(BF16))
+            probs = jnp.concatenate(probs, axis=1)
+            grads = jnp.concatenate(grads, axis=1)
+            dkey = mm(grads, query)
+            dvalue = mm(probs, grad)
+            cols = slice(low, low + QUAD)
+            dk_ref[window, cols] = dk_ref[window, cols] + dkey[:WIN]
+            dk_ref[ROWS:, cols] = dk_ref[ROWS:, cols] + dkey[WIN:]
+            dv_ref[window, cols] = dv_ref[window, cols] + dvalue[:WIN]
+            dv_ref[ROWS:, cols] = dv_ref[ROWS:, cols] + dvalue[WIN:]
+            dqkv_ref[rows, cols] = head_merge(mm_rows(grads, keys)).astype(BF16)
+        return carry
+
+    lax.fori_loop(0, TILES, step, 0)
+    dqkv_ref[ROWS:, :D] = jnp.zeros((SIDE_ROWS, D), BF16)
+    dqkv_ref[:, D : 2 * D] = dk_ref[...].astype(BF16)
+    dqkv_ref[:, 2 * D :] = dv_ref[...].astype(BF16)
+
+
+def backward_project(tab_ref, rank, x_ref, gh_ref, gains, n_ref, dqkv_ref, w_ref, gn_ref, g_ref, dw_ref):
+    def step(tile, carry):
+        cols = pl.ds(pl.multiple_of(tile * QUAD, QUAD), QUAD)
+        gn_ref[:, cols] = mm_cols(dqkv_ref[...], w_ref[cols, : 3 * D])
+        return carry
+
+    lax.fori_loop(0, D // QUAD, step, 0)
+
+    def weights(tile, carry):
+        cols = pl.ds(pl.multiple_of(tile * QUAD, QUAD), QUAD)
+        dw_ref[:, cols] = mm_rows(n_ref[...], dqkv_ref[:, cols]).astype(BF16)
+        return carry
+
+    lax.fori_loop(0, 3 * D // QUAD, weights, 0)
+    pool = pooling(tab_ref, rank)
+    side = mm(pool, n_ref[:ROWS, :])
+    root = lax.rsqrt(mean_square(side) + EPSILON)
+    unit = side * root
+    grad = gn_ref[ROWS:, :]
+    side_gain = jnp.sum(grad * unit, axis=0, keepdims=True)
+    grad = grad * gains[1:2]
+    grad = root * (grad - unit * jnp.mean(grad * unit, axis=-1, keepdims=True))
+    parts = three_way(grad)
+    gain_grad = jnp.zeros((1, D), F32)
+    for tile in range(TILES):
+        rows = pl.ds(tile * QT, QT)
+        spread = pool[:, tile * QT : (tile + 1) * QT]
+        total = gn_ref[rows, :] + mm_rows(spread, parts[0]) + mm_rows(spread, parts[1])
+        value = x_ref[rows, :].astype(F32)
+        root = lax.rsqrt(mean_square(value) + EPSILON)
+        unit = value * root
+        gain_grad = gain_grad + jnp.sum(total * unit, axis=0, keepdims=True)
+        total = total * gains[0:1]
+        g_ref[rows, :] = (
+            gh_ref[rows, :] + root * (total - unit * jnp.mean(total * unit, axis=-1, keepdims=True))
+        ).astype(BF16)
+    return gain_grad, side_gain
+
+
+def first_kernel(tab_ref, x_ref, gc_ref, w_ref, n_ref, qkv_ref, att_ref, lse_ref):
+    rank = lax.axis_index("rep")
+    gains = gains_of(gc_ref)
+    forward_norm(tab_ref, rank, x_ref, gains, n_ref)
+    forward_project(n_ref, w_ref, qkv_ref)
+    forward_attention(tab_ref, rank, qkv_ref, att_ref, lse_ref)
+
+
+def second_kernel(tab_ref, x_ref, cot_ref, att_ref, gc_ref, w_ref, wb_ref,
+                  y_ref, gh_ref, ga_ref, dg_ref, db_ref, do_ref, gain_ref, *scratch):
+    rank = lax.axis_index("rep")
+    gain_ref[...] = feed_forward(tab_ref, rank, x_ref, cot_ref, att_ref, gains_of(gc_ref), w_ref, wb_ref,
+                                 y_ref, gh_ref, ga_ref, dg_ref, db_ref, do_ref, *scratch)
+
+
+def third_kernel(tab_ref, x_ref, gh_ref, ga_ref, att_ref, lse_ref, n_ref, qkv_ref, gain_ref, gc_ref, w_ref,
+                 g_ref, dw_ref, dc_ref, dqkv_ref, dk_ref, dv_ref, gn_ref):
+    rank = lax.axis_index("rep")
+    gains = gains_of(gc_ref)
+    backward_attention(tab_ref, rank, qkv_ref, att_ref, ga_ref, lse_ref, dqkv_ref, dk_ref, dv_ref)
+    one, side = backward_project(
+        tab_ref, rank, x_ref, gh_ref, gains, n_ref, dqkv_ref, w_ref, gn_ref, g_ref, dw_ref
     )
-
-
-def contract_cols(left_op, right_op):
-    return lax.dot_general(
-        left_op, right_op, (((1,), (1,)), ((), ())), preferred_element_type=jnp.float32
-    )
-
-
-def rms_norm(row_data, gain_vec):
-    return (
-        row_data
-        * lax.rsqrt(jnp.mean(row_data * row_data, axis=-1, keepdims=True) + EPSILON)
-        * gain_vec
-    )
-
-
-QB = 128
-KPAD = 128
-
-
-def band_table():
-    query_pos = jnp.arange(QB, dtype=jnp.int32)[:, None] + KPAD
-    key_pos = jnp.arange(QB + 2 * KPAD, dtype=jnp.int32)[None, :]
-    return jnp.abs(query_pos - key_pos) <= RADIUS
-
-
-def block_terms(row_start, queries, keys_pad, values_pad, global_keys, seg_query, seg_key_pad, seg_global):
-    key_width = QB + 2 * KPAD
-    query_blk = queries[row_start : row_start + QB].reshape(QB, H, DH)
-    key_win = keys_pad[row_start : row_start + key_width]
-    value_win = values_pad[row_start : row_start + key_width]
-    local_scores = jnp.einsum("qhd,khd->hqk", query_blk, key_win, preferred_element_type=jnp.float32)
-    global_scores = jnp.einsum("qhd,ghd->hqg", query_blk, global_keys, preferred_element_type=jnp.float32)
-    seg_rows = seg_query[row_start : row_start + QB]
-    allow_local = band_table() & (
-        seg_rows[:, None] == seg_key_pad[row_start : row_start + key_width][None, :]
-    )
-    allow_global = seg_rows[:, None] == seg_global[None, :]
-    masked_local = jnp.where(allow_local[None], local_scores, MASKED_SCORE)
-    masked_global = jnp.where(allow_global[None], global_scores, MASKED_SCORE)
-    return (query_blk, key_win, value_win, masked_local, masked_global)
-
-
-def attend_forward(queries, keys_pad, values_pad, global_keys, global_values, seg_query, seg_key_pad, seg_global):
-    mixed_blocks, kept = [], []
-    for row_start in range(0, queries.shape[0], QB):
-        query_blk, key_win, value_win, masked_local, masked_global = block_terms(
-            row_start, queries, keys_pad, values_pad, global_keys, seg_query, seg_key_pad, seg_global
-        )
-        row_peak = jnp.maximum(
-            jnp.max(masked_local, axis=-1, keepdims=True), jnp.max(masked_global, axis=-1, keepdims=True)
-        )
-        local_exp = jnp.exp(masked_local - row_peak)
-        global_exp = jnp.exp(masked_global - row_peak)
-        denominator = jnp.sum(local_exp, axis=-1, keepdims=True) + jnp.sum(global_exp, axis=-1, keepdims=True)
-        local_low = (local_exp / denominator).astype(jnp.bfloat16)
-        global_low = (global_exp / denominator).astype(jnp.bfloat16)
-        mixed_rows = jnp.einsum("hqk,khd->qhd", local_low, value_win, preferred_element_type=jnp.float32)
-        mixed_rows = mixed_rows + jnp.einsum(
-            "hqg,ghd->qhd", global_low, global_values, preferred_element_type=jnp.float32
-        )
-        mixed_blocks.append(mixed_rows.reshape(QB, H * DH).astype(jnp.bfloat16))
-        kept.append((row_peak, denominator))
-    return (jnp.concatenate(mixed_blocks, axis=0), kept)
-
-
-def attend_backward(grad_mixed, kept, queries, keys_pad, values_pad, global_keys, global_values, seg_query, seg_key_pad, seg_global):
-    key_width = QB + 2 * KPAD
-    row_count = queries.shape[0]
-    grad_keys = jnp.zeros(keys_pad.shape, jnp.float32)
-    grad_values = jnp.zeros(values_pad.shape, jnp.float32)
-    grad_gkeys = jnp.zeros(global_keys.shape, jnp.float32)
-    grad_gvalues = jnp.zeros(global_values.shape, jnp.float32)
-    grad_query_blocks = []
-    for number, row_start in enumerate(range(0, row_count, QB)):
-        row_peak, denominator = kept[number]
-        query_blk, key_win, value_win, masked_local, masked_global = block_terms(
-            row_start, queries, keys_pad, values_pad, global_keys, seg_query, seg_key_pad, seg_global
-        )
-        local_probs = jnp.exp(masked_local - row_peak) / denominator
-        global_probs = jnp.exp(masked_global - row_peak) / denominator
-        grad_blk = grad_mixed[row_start : row_start + QB].reshape(QB, H, DH)
-        local_dp = jnp.einsum("qhd,khd->hqk", grad_blk, value_win, preferred_element_type=jnp.float32)
-        global_dp = jnp.einsum("qhd,ghd->hqg", grad_blk, global_values, preferred_element_type=jnp.float32)
-        centre = jnp.sum(local_probs * local_dp, axis=-1, keepdims=True) + jnp.sum(
-            global_probs * global_dp, axis=-1, keepdims=True
-        )
-        local_ds = (local_probs * (local_dp - centre)).astype(jnp.bfloat16)
-        global_ds = (global_probs * (global_dp - centre)).astype(jnp.bfloat16)
-        grad_query_rows = jnp.einsum("hqk,khd->qhd", local_ds, key_win, preferred_element_type=jnp.float32)
-        grad_query_rows = grad_query_rows + jnp.einsum(
-            "hqg,ghd->qhd", global_ds, global_keys, preferred_element_type=jnp.float32
-        )
-        grad_query_blocks.append(grad_query_rows.reshape(QB, H * DH).astype(jnp.bfloat16))
-        grad_keys = grad_keys.at[row_start : row_start + key_width].add(
-            jnp.einsum("hqk,qhd->khd", local_ds, query_blk, preferred_element_type=jnp.float32)
-        )
-        grad_values = grad_values.at[row_start : row_start + key_width].add(
-            jnp.einsum("hqk,qhd->khd", local_probs.astype(jnp.bfloat16), grad_blk, preferred_element_type=jnp.float32)
-        )
-        grad_gkeys = grad_gkeys + jnp.einsum("hqg,qhd->ghd", global_ds, query_blk, preferred_element_type=jnp.float32)
-        grad_gvalues = grad_gvalues + jnp.einsum(
-            "hqg,qhd->ghd", global_probs.astype(jnp.bfloat16), grad_blk, preferred_element_type=jnp.float32
-        )
-    slot_count = global_keys.shape[0]
-    grad_k = grad_keys[KPAD : KPAD + row_count].reshape(row_count, H * DH).astype(jnp.bfloat16)
-    grad_v = grad_values[KPAD : KPAD + row_count].reshape(row_count, H * DH).astype(jnp.bfloat16)
-    grad_gk = grad_gkeys.reshape(slot_count, H * DH).astype(jnp.bfloat16)
-    grad_gv = grad_gvalues.reshape(slot_count, H * DH).astype(jnp.bfloat16)
-    return (jnp.concatenate(grad_query_blocks, axis=0), grad_k, grad_v, grad_gk, grad_gv)
-
-
-def layer_pass(row_data, cot_data, seg_tok, valid_tok, weights):
-    (attn_gain, global_gain, query_weight, key_weight, value_weight, out_weight, ffn_gain,
-     gate_weight, up_weight, down_weight) = weights
-    row_count = row_data.shape[0]
-    slot_count = row_count // GBLK
-    valid_col = valid_tok.astype(jnp.float32)[:, None]
-    inputs_f = row_data.astype(jnp.float32)
-    gain_one = attn_gain.astype(jnp.float32)
-    gain_side = global_gain.astype(jnp.float32)
-    gain_two = ffn_gain.astype(jnp.float32)
-    normed_f, norm_back_one = jax.vjp(rms_norm, inputs_f, gain_one)
-    normed = normed_f.astype(jnp.bfloat16)
-    side_sum = jnp.sum((normed.astype(jnp.float32) * valid_col).reshape(slot_count, GBLK, -1), axis=1)
-    side_f, side_back = jax.vjp(rms_norm, side_sum, gain_side)
-    side_normed = side_f.astype(jnp.bfloat16)
-
-    def project(left, right):
-        return jnp.dot(left, right, preferred_element_type=jnp.float32).astype(jnp.bfloat16)
-
-    queries = project(normed, query_weight)
-    keys_all = project(normed, key_weight)
-    values_all = project(normed, value_weight)
-    global_keys = project(side_normed, key_weight)
-    global_values = project(side_normed, value_weight)
-    seg_key = jnp.where(valid_tok, seg_tok, -2)
-    seg_global = seg_key[::GBLK]
-    keys_pad = jnp.pad(keys_all, ((KPAD, KPAD), (0, 0))).reshape(-1, H, DH)
-    values_pad = jnp.pad(values_all, ((KPAD, KPAD), (0, 0))).reshape(-1, H, DH)
-    seg_key_pad = jnp.pad(seg_key, (KPAD, KPAD), constant_values=-3)
-    global_key_heads = global_keys.reshape(slot_count, H, DH)
-    global_value_heads = global_values.reshape(slot_count, H, DH)
-    attended, kept = attend_forward(
-        queries, keys_pad, values_pad, global_key_heads, global_value_heads, seg_tok, seg_key_pad, seg_global
-    )
-    hidden_one = inputs_f + jnp.dot(attended, out_weight, preferred_element_type=jnp.float32)
-    normed_two_f, norm_back_two = jax.vjp(rms_norm, hidden_one, gain_two)
-    normed_two = normed_two_f.astype(jnp.bfloat16)
-    gate_pre = jnp.dot(normed_two, gate_weight, preferred_element_type=jnp.float32)
-    up_pre = jnp.dot(normed_two, up_weight, preferred_element_type=jnp.float32)
-    activated, gelu_back = jax.vjp(partial(jax.nn.gelu, approximate=True), gate_pre)
-    hidden_two = (activated * up_pre).astype(jnp.bfloat16)
-    result = (
-        valid_col * (hidden_one + jnp.dot(hidden_two, down_weight, preferred_element_type=jnp.float32))
-    ).astype(jnp.bfloat16)
-    grad_res = cot_data.astype(jnp.float32) * valid_col
-    grad_out = grad_res.astype(jnp.bfloat16)
-    grad_hidden = contract_cols(grad_out, down_weight)
-    grad_down = contract_rows(hidden_two, grad_out)
-    grad_gate = gelu_back(grad_hidden * up_pre)[0].astype(jnp.bfloat16)
-    grad_up = (grad_hidden * activated).astype(jnp.bfloat16)
-    grad_gate_w = contract_rows(normed_two, grad_gate)
-    grad_up_w = contract_rows(normed_two, grad_up)
-    grad_normed_two = contract_cols(grad_gate, gate_weight) + contract_cols(grad_up, up_weight)
-    grad_norm_part, grad_gain_two = norm_back_two(grad_normed_two)
-    grad_hidden_one = grad_res + grad_norm_part
-    grad_branch = grad_hidden_one.astype(jnp.bfloat16)
-    grad_out_w = contract_rows(attended, grad_branch)
-    grad_attended = contract_cols(grad_branch, out_weight).astype(jnp.bfloat16)
-    grad_q, grad_k, grad_v, grad_gk, grad_gv = attend_backward(
-        grad_attended, kept, queries, keys_pad, values_pad, global_key_heads, global_value_heads,
-        seg_tok, seg_key_pad, seg_global,
-    )
-    grad_query_w = contract_rows(normed, grad_q)
-    grad_key_w = contract_rows(normed, grad_k) + contract_rows(side_normed, grad_gk)
-    grad_value_w = contract_rows(normed, grad_v) + contract_rows(side_normed, grad_gv)
-    grad_normed = (
-        contract_cols(grad_q, query_weight) + contract_cols(grad_k, key_weight) + contract_cols(grad_v, value_weight)
-    )
-    grad_side_normed = contract_cols(grad_gk, key_weight) + contract_cols(grad_gv, value_weight)
-    grad_side, grad_gain_side = side_back(grad_side_normed)
-    spread_side = grad_side[:, None, :] * valid_col.reshape(slot_count, GBLK, 1)
-    grad_normed = grad_normed + spread_side.reshape(row_count, -1)
-    grad_inputs, grad_gain_one = norm_back_one(grad_normed)
-    grad_rows = (grad_inputs + grad_hidden_one).astype(jnp.bfloat16)
-    grads = (grad_gain_one, grad_gain_side, grad_query_w, grad_key_w, grad_value_w, grad_out_w,
-             grad_gain_two, grad_gate_w, grad_up_w, grad_down)
-    return (result, grad_rows, grads)
+    grads = jnp.concatenate([one, side, gain_ref[...], jnp.zeros((5, D), F32)], axis=0)
+    spread_gain_grads(grads, dc_ref)
+
+
+def layer(tab, x, cot, gc, w, wb):
+    hidden = wb.shape[0]
+    shape = jax.ShapeDtypeStruct
+    params = pltpu.CompilerParams(vmem_limit_bytes=VMEM_LIMIT)
+    n, qkv, att, lse = pl.pallas_call(
+        first_kernel,
+        out_shape=(shape((ALL_ROWS, D), BF16), shape((ALL_ROWS, 3 * D), BF16), shape((ROWS, D), BF16),
+                   shape((TILES, 16, QT), F32)),
+        in_specs=[SMEM, VMEM, VMEM, pl.BlockSpec((D, 3 * D), lambda step: (0, 0))],
+        grid=(1,),
+        out_specs=(VMEM,) * 4,
+        compiler_params=params,
+        name="attend",
+    )(tab, x, gc, w)
+    y, gh, ga, dg, db, do, gain = pl.pallas_call(
+        second_kernel,
+        out_shape=(shape((ROWS, D), BF16), shape((ROWS, D), F32), shape((ROWS, D), BF16),
+                   shape((D, 2 * hidden), BF16), shape((hidden, D), BF16), shape((D, D), BF16), shape((1, D), F32)),
+        in_specs=[SMEM] + [VMEM] * 6,
+        out_specs=(VMEM,) * 7,
+        scratch_shapes=[pltpu.VMEM((ROWS, D), F32), pltpu.VMEM((ROWS, D), BF16), pltpu.VMEM((D, ROWS), BF16),
+                        pltpu.VMEM((ROWS, D), BF16), pltpu.VMEM((ROWS, hidden), BF16),
+                        pltpu.VMEM((ROWS, hidden), BF16), pltpu.VMEM((ROWS, hidden), BF16),
+                        pltpu.VMEM((ROWS, D), F32)],
+        compiler_params=params,
+        name="feed_forward",
+    )(tab, x, cot, att, gc, w, wb)
+    g, dw, dc = pl.pallas_call(
+        third_kernel,
+        out_shape=(shape((ROWS, D), BF16), shape((D, 3 * D), BF16), shape((gc.shape[0], 8, 128), F32)),
+        in_specs=[SMEM] + [VMEM] * 9 + [pl.BlockSpec((D, 3 * D), lambda step: (0, 0))],
+        grid=(1,),
+        out_specs=(VMEM,) * 3,
+        scratch_shapes=[pltpu.VMEM((ALL_ROWS, 3 * D), BF16), pltpu.VMEM((ALL_ROWS, D), F32),
+                        pltpu.VMEM((ALL_ROWS, D), F32), pltpu.VMEM((ALL_ROWS, D), F32)],
+        compiler_params=params,
+        name="attend_back",
+    )(tab, x, gh, ga, att, lse, n, qkv, gain, gc, w)
+    return y, g, dg, db, do, dw, dc
 
 
 def per_device(count, layer_input, cotangent, lengths, attn_gain, global_gain, query_weight, key_weight,
@@ -887,7 +1118,6 @@
     micro, span, width = layer_input.shape
     hidden = gate_weight.shape[1]
     blocks = micro * span // BLK
-    rank = lax.axis_index("rep")
     table = deal_table(lengths)
     wa = jnp.concatenate([query_weight, key_weight, value_weight, out_weight, gate_weight, up_weight], axis=1)
     part = attn_gain.shape[0]
@@ -897,36 +1127,18 @@
         count, splits, table,
         layer_input.reshape(blocks, BLK, width), cotangent.reshape(blocks, BLK, width), wa, down_weight, wc,
     )
-    full = ga.reshape(width, -1)
-    gains = jnp.transpose(gc[:, :3, :part], (1, 0, 2)).reshape(3, width)
-    own = lax.dynamic_slice_in_dim(table, SEG_AT + rank * SLOTS, SLOTS)
-    lens = lax.dynamic_slice_in_dim(table, LEN_AT + rank * SLOTS, SLOTS)
-    seg_tok = jnp.repeat(own, BLK)
-    valid_tok = (jnp.arange(BLK, dtype=jnp.int32)[None, :] < lens[:, None]).reshape(-1)
-    heads = 4 * width
-    weights = (
-        gains[0], gains[1], full[:, :width], full[:, width : 2 * width], full[:, 2 * width : 3 * width],
-        full[:, 3 * width : heads], gains[2], full[:, heads : heads + hidden],
-        full[:, heads + hidden :], gb.reshape(-1, width),
+    y, g, dg, db, do, dw, dc = layer(
+        table, rows.reshape(ROWS, width), cots.reshape(ROWS, width), gc, ga.reshape(width, -1), gb.reshape(-1, width)
     )
-    result, grad_rows, grads = layer_pass(
-        rows.reshape(-1, width), cots.reshape(-1, width), seg_tok, valid_tok, weights
-    )
-    grad_a = jnp.concatenate(
-        [grads[2], grads[3], grads[4], grads[5], grads[7], grads[8]], axis=1
-    ).astype(jnp.bfloat16).reshape(ga.shape)
-    grad_b = grads[9].astype(jnp.bfloat16).reshape(gb.shape)
-    grad_c = jnp.transpose(jnp.stack([grads[0], grads[1], grads[6]]).reshape(3, count, part), (1, 0, 2))
-    grad_c = jnp.pad(grad_c, ((0, 0), (0, 5), (0, 128 - part)))
-    oa, ob, oc, ry, rg = reduce_grads(
-        count, splits, grad_a, grad_b, grad_c, result.reshape(SLOTS, BLK, width), grad_rows.reshape(SLOTS, BLK, width)
+    grads = [grad.reshape(count, -1, grad.shape[-1]) for grad in (dg, db, do, dw, dc)]
+    og, ob, oo, ow, oc, ry, rg = reduce_grads(
+        count, grads, y.reshape(SLOTS, BLK, width), g.reshape(SLOTS, BLK, width)
     )
     y_home, g_home = bring_home(table, ry, rg, blocks)
     return (
         y_home.reshape(layer_input.shape), g_home.reshape(layer_input.shape),
-        oc[0, :part], oc[1, :part],
-        oa[:, :width], oa[:, width : 2 * width], oa[:, 2 * width : 3 * width], oa[:, 3 * width : heads],
-        oc[2, :part], oa[:, heads : heads + hidden], oa[:, heads + hidden :], ob,
+        oc[0, :part], oc[1, :part], ow[:, :width], ow[:, width : 2 * width], ow[:, 2 * width :], oo,
+        oc[2, :part], og[:, :hidden], og[:, hidden:], ob,
     )
 
 

time: 534 us -> 372 us (0.70); the launches traced: 527 us -> 372 us
  matrix products: 137 us -> 0 us
  Pallas kernels: 260 us -> 358 us
  local copies, waits for them, and re-layouts: 99.7 us -> 11.3 us
  other arithmetic: 26.2 us -> 1.29 us
    dot_general x87 -> x0, matrix products: 137 us -> none  [the longest x9 22.8 us: contract_cols(): lax.dot_general(left_op, right_op, (((1,), (1,)), ((), ())), preferred_el...]
    pallas_call x1 -> x4, Pallas kernels: 149 us -> 247 us  [the longest x1 156 us: reduce_grads(): pl.pallas_call(partial(reduce_kernel, outer, inner, kinds), out_shape=tup...]
    slice x35 -> x2, local copies, waits for them, and re-layouts: 40.1 us -> 2.17 us  [the longest x1 1.24 us: per_device(): og[:, hidden:]]
    unnamed x368 -> x21, local copies, waits for them, and re-layouts: 34.1 us -> 6.41 us
    convert_element_type x20 -> x0, other arithmetic: 12.6 us -> none  [the longest x5 4.88 us: attend_backward(): local_ds = (local_probs * (local_dp - centre)).astype(jnp.bfloat16)]
    convert_element_type x11 -> x0, local copies, waits for them, and re-layouts: 11.7 us -> none  [the longest x5 7.81 us: attend_backward(): grad_query_rows.reshape(QB, H * DH).astype(jnp.bfloat16)]
    reduce_sum x13 -> x0, other arithmetic: 9.12 us -> none  [the longest x5 4.34 us: attend_forward(): jnp.sum(local_exp, axis=-1, keepdims=True)]
where the time goes in v2:
time: 372 us
  Pallas kernels  358 us (96%)
  local copies, waits for them, and re-layouts  11.3 us (3%)
    pallas_call x1, Pallas kernels, reduce_grads(): pl.pallas_call(partial(reduce_kernel, outer, inner, kinds), out_shape=tup...  156 us
    pallas_call x1, Pallas kernels, gather_weights(): pl.pallas_call(partial(gather_kernel, outer, inner, splits), out_shape=(j...  88 us
    pallas_call x1, Pallas kernels, layer(): pl.pallas_call(second_kernel, out_shape=(shape((ROWS, D), BF16), shape((R...  39.7 us
    pallas_call x1, Pallas kernels, layer(): pl.pallas_call(third_kernel, out_shape=(shape((ROWS, D), BF16), shape((D,...  27.8 us
    pallas_call x1, Pallas kernels, layer(): pl.pallas_call(first_kernel, out_shape=(shape((ALL_ROWS, D), BF16), shape...  23.9 us
    pallas_call x1, Pallas kernels, deal_table(): pl.pallas_call(partial(table_kernel, micro, per_dev), out_shape=jax.Shape...  10.4 us

profile of v2, /device:TPU:0, one launch (start us, length us, event | category | flops | bytes accessed | tf_op | source)
XLA Modules:
  0.0 371.7 jit_solution(10070707582578019769)
XLA Ops:
  0.6 0.0 copy-start.5
  0.7 0.0 copy-start.4
  0.7 1.3 pad.8.lens_ref
  2.0 1.3 fusion.8.wc_ref
  3.3 5.9 %lens_exchange.1.lens_ref = s32[4,8,128]{2,1,0:T(8,128)} custom-call(s32[8,128]{1,0:T(8,128)} %pad.8.lens_ref), custom_call_target="tpu_custom_call" | custom-call | tf_op jit(solution)/shard_map/lens_exchange/pallas_call | solution.py:147
  9.2 10.4 %deal_table.1.tab_ref = s32[256]{0:T(256)} custom-call(s32[4,8,128]{2,1,0:T(8,128)} %lens_exchange.1.lens_ref), custom_call_target="tpu_custom_call" | custom-call | tf_op jit(solution)/shard_map/deal_table/pallas_call | solution.py:156
  19.6 0.9 constant_dynamic-update-slice_fusion.5
  20.5 0.9 constant_dynamic-update-slice_fusion.4
  21.5 0.9 constant_dynamic-update-slice_fusion.3
  22.4 0.9 constant_dynamic-update-slice_fusion.2
  23.3 0.0 copy-done.4
  23.4 0.0 copy-done.5
  23.4 0.0 copy-start
  23.4 1.1 copy-done
  24.5 88.0 %gather_and_deal.1 = (bf16[8,96,7168]{2,1,0:T(8,128)(2,1)}, bf16[8,256,768]{2,1,0:T(8,128)(2,1)}, bf16[8,16,128]{2,1,0:T(8,128)(2,1)}, bf16[10,64,768]{2,1,0:T(8,128)(2,1)}, bf16[10,64,768]{2,1,0:T(8,128)(2,1)}) custom-call(s32[256]{0:T(256)} %deal_table.1.tab_ref, bf16[24,64,768]{2,1,0:T(8,128)(2,1)} %bitcast.34, bf16[24,64,768]{2,1,0:T(8,128)(2,1)} %bitcast.35, ...), custom_call_target="tpu_custom_call" | custom-call | tf_op jit(solution)/shard_map/gather_and_deal/pallas_call | solution.py:412
  112.5 23.9 %attend.1 = (bf16[688,768]{1,0:T(8,128)(2,1)}, bf16[688,2304]{1,0:T(8,128)(2,1)}, bf16[640,768]{1,0:T(8,128)(2,1)}, f32[5,16,128]{2,1,0:T(8,128)}) custom-call(s32[256]{0:T(256)} %deal_table.1.tab_ref, bf16[640,768]{1,0:T(8,128)(2,1)} %bitcast.27, bf16[8,16,128]{2,1,0:T(8,128)(2,1)} %get-tuple-element.42.gc_ref, bf16[768,7168]{1,0:T(8,128)(2,1)} %bitcast.24), custom_call_target="tpu_custom_call" | custom-call | tf_op jit(solution)/shard_map/attend/pallas_call | solution.py:1079
  136.4 39.7 %feed_forward.1 = (bf16[640,768]{1,0:T(8,128)(2,1)}, f32[640,768]{1,0:T(8,128)}, bf16[640,768]{1,0:T(8,128)(2,1)}, bf16[768,4096]{1,0:T(8,128)(2,1)}, bf16[2048,...) custom-call(s32[256]{0:T(256)} %deal_table.1.tab_ref, bf16[640,768]{1,0:T(8,128)(2,1)} %bitcast.28, ...), custom_call_target="tpu_custom_call" | custom-call | tf_op jit(solution)/shard_map/feed_forward/pallas_call | solution.py:1089
  176.1 27.8 %attend_back.1 = (bf16[640,768]{1,0:T(8,128)(2,1)}, bf16[768,2304]{1,0:T(8,128)(2,1)}, f32[8,8,128]{2,1,0:T(8,128)}) custom-call(s32[256]{0:T(256)} %deal_table.1.tab_ref, bf16[640,768]{1,0:T(8,128)(2,1)} %bitcast.29, f32[640,768]{1,0:T(8,128)} %get-tuple-element.49.gh_ref, bf16[640,768]{1,0:T(8,128)(2,1)} %get-tuple-element.50.ga_ref, ...), custom_call_target="tpu_custom_call" | custom-call | tf_op jit(solution)/shard_map/attend_back/pallas_call | solution.py:1102
  204.0 156.0 %reduce_and_return.1 = (f32[96,4096]{1,0:T(8,128)}, f32[256,768]{1,0:T(8,128)}, f32[96,768]{1,0:T(8,128)}, f32[96,2304]{1,0:T(8,128)}, f32[8,128]{1,0:T(8,128)},...) custom-call(bf16[4,2,96,4096]{3,2,1,0:T(8,128)(2,1)} %bitcast.30, bf16[4,2,256,768]{3,2,1,0:T(8,128)(2,1)} %bitcast.33, ...), custom_call_target="tpu_custom_call" | custom-call | tf_op jit(solution)/shard_map/reduce_and_return/pallas_call | solution.py:637
  360.0 0.0 copy-start.2
  360.0 6.6 %place_rows.1 = (bf16[24,64,768]{2,1,0:T(8,128)(2,1)}, bf16[24,64,768]{2,1,0:T(8,128)(2,1)}) custom-call(s32[256]{0:T(256)} %deal_table.1.tab_ref, bf16[4,10,64,768]{3,2,1,0:T(8,128)(2,1)} %get-tuple-element.59.ry_ref, bf16[4,10,64,768]{3,2,1,0:T(8,128)(2,1)} %get-tuple-element.60.rg_ref), custom_call_target="tpu_custom_call" | custom-call | tf_op jit(solution)/shard_map/place_rows/pallas_call | solution.py:669
  366.6 0.0 copy-start.1
  366.6 1.3 slice_bitcast_fusion
  368.0 0.0 copy-done.2
  368.0 0.9 fusion.10
  368.9 0.0 copy-done.1
  368.9 0.0 copy-start.6
  368.9 1.2 fusion.9
  370.1 0.0 copy-done.6
  370.1 0.7 copy.32
  370.9 0.0 copy-done.3
  370.9 0.9 copy.33
  (3 shorter events, 0.1 us)
Async XLA Ops:
  0.6 22.7 %copy-start.5 = (bf16[96,2048]{1,0:T(8,128)(2,1)S(1)}, bf16[96,2048]{1,0:T(8,128)(2,1)}, u32[]{:S(2)}) copy-start(bf16[96,2048]{1,0:T(8,128)(2,1)} %param.24) | copy-start | bytes 1179652
  0.7 22.7 %copy-start.4 = (bf16[96,2048]{1,0:T(8,128)(2,1)S(1)}, bf16[96,2048]{1,0:T(8,128)(2,1)}, u32[]{:S(2)}) copy-start(bf16[96,2048]{1,0:T(8,128)(2,1)} %param.23) | copy-start | bytes 1179652
  23.4 1.1 copy-start
  360.0 8.0 %copy-start.2 = (f32[96,2304]{1,0:T(8,128)S(1)}, f32[96,2304]{1,0:T(8,128)}, u32[]{:S(2)}) copy-start(f32[96,2304]{1,0:T(8,128)} %get-tuple-element.64) | copy-start | bytes 2654212
  366.6 2.3 copy-start.1
  368.9 1.2 copy-start.6
  368.9 2.0 copy-start.3

commit v3 on v2

--- a/solution.py
+++ b/solution.py
@@ -801,13 +801,14 @@
 
 
 def spread_gain_grads(value, dc_ref):
-    count = dc_ref.shape[0]
+    count = dc_ref.shape[0] if len(dc_ref.shape) == 3 else dc_ref.shape[0] * dc_ref.shape[1]
     part = D // count
     column, lane = iota((D, 128), 0), iota((D, 128), 1)
     parts = three_way(value)
     for shard in range(count):
         pick = jnp.where((column == lane + shard * part) & (lane < part), 1.0, 0.0).astype(BF16)
-        dc_ref[shard] = mm(parts[0], pick) + mm(parts[1], pick) + mm(parts[2], pick)
+        place = dc_ref.at[shard] if len(dc_ref.shape) == 3 else dc_ref.at[shard // dc_ref.shape[1], shard % dc_ref.shape[1]]
+        place[...] = mm(parts[0], pick) + mm(parts[1], pick) + mm(parts[2], pick)
 
 
 def mean_square(value):
@@ -872,7 +873,7 @@
 
 
 def feed_forward(tab_ref, rank, x_ref, cot_ref, att_ref, gains, w_ref, wb_ref,
-                 y_ref, gh_ref, ga_ref, dg_ref, db_ref, do_ref,
+                 y_ref, gh_ref, ga_ref, dg_ref, du_ref, db_ref, do_ref,
                  h1_ref, nt_ref, ntt_ref, gres_ref, h2_ref, gg_ref, gu_ref, gn_ref):
     hidden = wb_ref.shape[0]
     gate_at = 4 * D
@@ -920,7 +921,7 @@
         at = pl.multiple_of(tile * FF_TILE, FF_TILE)
         cols = pl.ds(at, FF_TILE)
         dg_ref[:, cols] = mm(ntt_ref[...], gg_ref[:, cols]).astype(BF16)
-        dg_ref[:, pl.ds(hidden + at, FF_TILE)] = mm(ntt_ref[...], gu_ref[:, cols]).astype(BF16)
+        du_ref[:, cols] = mm(ntt_ref[...], gu_ref[:, cols]).astype(BF16)
         db_ref[cols, :] = mm_rows(h2_ref[:, cols], gres_ref[...]).astype(BF16)
         return carry
 
@@ -951,9 +952,12 @@
     return gain_grad
 
 
-def backward_attention(tab_ref, rank, qkv_ref, att_ref, ga_ref, lse_ref, dqkv_ref, dk_ref, dv_ref):
+def backward_attention_start(dk_ref, dv_ref):
     dk_ref[...] = jnp.zeros_like(dk_ref)
     dv_ref[...] = jnp.zeros_like(dv_ref)
+
+
+def backward_attention_tiles(tab_ref, rank, qkv_ref, att_ref, ga_ref, lse_ref, dqkv_ref, dk_ref, dv_ref, begin, end):
     heads = QUAD // DH
     marks = jnp.where(iota((16, D), 1) // DH == iota((16, D), 0), 1.0, 0.0).astype(BF16)
 
@@ -1000,26 +1004,36 @@
             dqkv_ref[rows, cols] = head_merge(mm_rows(grads, keys)).astype(BF16)
         return carry
 
-    lax.fori_loop(0, TILES, step, 0)
+    lax.fori_loop(begin, end, step, 0)
+
+
+def backward_attention_end(dqkv_ref, dk_ref, dv_ref):
     dqkv_ref[ROWS:, :D] = jnp.zeros((SIDE_ROWS, D), BF16)
     dqkv_ref[:, D : 2 * D] = dk_ref[...].astype(BF16)
     dqkv_ref[:, 2 * D :] = dv_ref[...].astype(BF16)
 
 
-def backward_project(tab_ref, rank, x_ref, gh_ref, gains, n_ref, dqkv_ref, w_ref, gn_ref, g_ref, dw_ref):
+def weight_grads(n_ref, dqkv_ref, refs):
+    for number, ref in enumerate(refs):
+        def weights(tile, carry):
+            at = pl.multiple_of(tile * QUAD, QUAD)
+            value = mm_rows(n_ref[...], dqkv_ref[:, pl.ds(number * D + at, QUAD)]).astype(BF16)
+            if len(ref.shape) == 4:
+                ref[:, :, :, pl.ds(at, QUAD)] = value.reshape(ref.shape[:3] + (QUAD,))
+            else:
+                ref[:, pl.ds(at, QUAD)] = value
+            return carry
+
+        lax.fori_loop(0, D // QUAD, weights, 0)
+
+
+def backward_project(tab_ref, rank, x_ref, gh_ref, gains, n_ref, dqkv_ref, w_ref, gn_ref, g_ref):
     def step(tile, carry):
         cols = pl.ds(pl.multiple_of(tile * QUAD, QUAD), QUAD)
         gn_ref[:, cols] = mm_cols(dqkv_ref[...], w_ref[cols, : 3 * D])
         return carry
 
     lax.fori_loop(0, D // QUAD, step, 0)
-
-    def weights(tile, carry):
-        cols = pl.ds(pl.multiple_of(tile * QUAD, QUAD), QUAD)
-        dw_ref[:, cols] = mm_rows(n_ref[...], dqkv_ref[:, cols]).astype(BF16)
-        return carry
-
-    lax.fori_loop(0, 3 * D // QUAD, weights, 0)
     pool = pooling(tab_ref, rank)
     side = mm(pool, n_ref[:ROWS, :])
     root = lax.rsqrt(mean_square(side) + EPSILON)
@@ -1039,9 +1053,13 @@
         unit = value * root
         gain_grad = gain_grad + jnp.sum(total * unit, axis=0, keepdims=True)
         total = total * gains[0:1]
-        g_ref[rows, :] = (
+        value = (
             gh_ref[rows, :] + root * (total - unit * jnp.mean(total * unit, axis=-1, keepdims=True))
         ).astype(BF16)
+        if len(g_ref.shape) == 3:
+            g_ref[pl.ds(tile * (QT // BLK), QT // BLK)] = value.reshape(QT // BLK, BLK, D)
+        else:
+            g_ref[rows, :] = value
     return gain_grad, side_gain
 
 
@@ -1054,25 +1072,26 @@
 
 
 def second_kernel(tab_ref, x_ref, cot_ref, att_ref, gc_ref, w_ref, wb_ref,
-                  y_ref, gh_ref, ga_ref, dg_ref, db_ref, do_ref, gain_ref, *scratch):
+                  y_ref, gh_ref, ga_ref, dg_ref, du_ref, db_ref, do_ref, gain_ref, *scratch):
     rank = lax.axis_index("rep")
     gain_ref[...] = feed_forward(tab_ref, rank, x_ref, cot_ref, att_ref, gains_of(gc_ref), w_ref, wb_ref,
-                                 y_ref, gh_ref, ga_ref, dg_ref, db_ref, do_ref, *scratch)
+                                 y_ref, gh_ref, ga_ref, dg_ref, du_ref, db_ref, do_ref, *scratch)
 
 
 def third_kernel(tab_ref, x_ref, gh_ref, ga_ref, att_ref, lse_ref, n_ref, qkv_ref, gain_ref, gc_ref, w_ref,
                  g_ref, dw_ref, dc_ref, dqkv_ref, dk_ref, dv_ref, gn_ref):
     rank = lax.axis_index("rep")
     gains = gains_of(gc_ref)
-    backward_attention(tab_ref, rank, qkv_ref, att_ref, ga_ref, lse_ref, dqkv_ref, dk_ref, dv_ref)
-    one, side = backward_project(
-        tab_ref, rank, x_ref, gh_ref, gains, n_ref, dqkv_ref, w_ref, gn_ref, g_ref, dw_ref
-    )
+    backward_attention_start(dk_ref, dv_ref)
+    backward_attention_tiles(tab_ref, rank, qkv_ref, att_ref, ga_ref, lse_ref, dqkv_ref, dk_ref, dv_ref, 0, TILES)
+    backward_attention_end(dqkv_ref, dk_ref, dv_ref)
+    weight_grads(n_ref, dqkv_ref, [dw_ref.at[:, i * D : (i + 1) * D] for i in range(3)])
+    one, side = backward_project(tab_ref, rank, x_ref, gh_ref, gains, n_ref, dqkv_ref, w_ref, gn_ref, g_ref)
     grads = jnp.concatenate([one, side, gain_ref[...], jnp.zeros((5, D), F32)], axis=0)
     spread_gain_grads(grads, dc_ref)
 
 
-def layer(tab, x, cot, gc, w, wb):
+def forward_layer(tab, x, cot, gc, w, wb):
     hidden = wb.shape[0]
     shape = jax.ShapeDtypeStruct
     params = pltpu.CompilerParams(vmem_limit_bytes=VMEM_LIMIT)
@@ -1086,12 +1105,13 @@
         compiler_params=params,
         name="attend",
     )(tab, x, gc, w)
-    y, gh, ga, dg, db, do, gain = pl.pallas_call(
+    outs = pl.pallas_call(
         second_kernel,
         out_shape=(shape((ROWS, D), BF16), shape((ROWS, D), F32), shape((ROWS, D), BF16),
-                   shape((D, 2 * hidden), BF16), shape((hidden, D), BF16), shape((D, D), BF16), shape((1, D), F32)),
+                   shape((D, hidden), BF16), shape((D, hidden), BF16), shape((hidden, D), BF16), shape((D, D), BF16),
+                   shape((1, D), F32)),
         in_specs=[SMEM] + [VMEM] * 6,
-        out_specs=(VMEM,) * 7,
+        out_specs=(VMEM,) * 8,
         scratch_shapes=[pltpu.VMEM((ROWS, D), F32), pltpu.VMEM((ROWS, D), BF16), pltpu.VMEM((D, ROWS), BF16),
                         pltpu.VMEM((ROWS, D), BF16), pltpu.VMEM((ROWS, hidden), BF16),
                         pltpu.VMEM((ROWS, hidden), BF16), pltpu.VMEM((ROWS, hidden), BF16),
@@ -1099,7 +1119,12 @@
         compiler_params=params,
         name="feed_forward",
     )(tab, x, cot, att, gc, w, wb)
-    g, dw, dc = pl.pallas_call(
+    return (n, qkv, att, lse) + outs
+
+
+def backward_layer(tab, x, gh, ga, att, lse, n, qkv, gain, gc, w):
+    shape = jax.ShapeDtypeStruct
+    return pl.pallas_call(
         third_kernel,
         out_shape=(shape((ROWS, D), BF16), shape((D, 3 * D), BF16), shape((gc.shape[0], 8, 128), F32)),
         in_specs=[SMEM] + [VMEM] * 9 + [pl.BlockSpec((D, 3 * D), lambda step: (0, 0))],
@@ -1107,10 +1132,306 @@
         out_specs=(VMEM,) * 3,
         scratch_shapes=[pltpu.VMEM((ALL_ROWS, 3 * D), BF16), pltpu.VMEM((ALL_ROWS, D), F32),
                         pltpu.VMEM((ALL_ROWS, D), F32), pltpu.VMEM((ALL_ROWS, D), F32)],
-        compiler_params=params,
+        compiler_params=pltpu.CompilerParams(vmem_limit_bytes=VMEM_LIMIT),
         name="attend_back",
     )(tab, x, gh, ga, att, lse, n, qkv, gain, gc, w)
-    return y, g, dg, db, do, dw, dc
+
+
+class Links:
+    def __init__(self, outer, inner):
+        self.outer, self.inner = outer, inner
+        self.rank, self.spot = lax.axis_index("rep"), lax.axis_index("fsdp")
+        self.core = self.rank % 2
+        self.row, self.col = self.spot // inner, self.spot % inner
+        self.mate, self.across = core_of(self.rank), across_of(self.rank)
+        self.late = []
+
+    def greet(self):
+        barrier = pltpu.get_barrier_semaphore()
+        neighbours = (
+            (self.row + 1 < self.outer, {"fsdp": self.spot + self.inner}),
+            (self.row > 0, {"fsdp": self.spot - self.inner}),
+            (self.col + 1 < self.inner, {"fsdp": self.spot + 1}),
+            (self.col > 0, {"fsdp": self.spot - 1}),
+        )
+        amount = jnp.int32(2)
+        for there, device in neighbours:
+            amount = amount + there.astype(jnp.int32)
+
+            @pl.when(there)
+            def _():
+                pl.semaphore_signal(barrier, inc=1, device_id=device, device_id_type=MESH)
+
+        for device in (self.mate, self.across):
+            pl.semaphore_signal(barrier, inc=1, device_id={"rep": device}, device_id_type=MESH)
+        pl.semaphore_wait(barrier, amount)
+
+    def send(self, there, src, dst, ssem, rsem, device):
+        def describe():
+            return pltpu.make_async_remote_copy(
+                src_ref=src, dst_ref=dst, send_sem=ssem, recv_sem=rsem,
+                device_id=device, device_id_type=MESH,
+            )
+
+        if there is None:
+            describe().start()
+        else:
+            @pl.when(there)
+            def _():
+                describe().start()
+
+        self.late.append((there, lambda: describe().wait_send()))
+
+    def arrive(self, place, rsem, spare):
+        pltpu.make_async_remote_copy(
+            src_ref=place, dst_ref=place, send_sem=spare, recv_sem=rsem,
+            device_id={"rep": self.mate}, device_id_type=MESH,
+        ).wait_recv()
+
+    def drain(self):
+        for there, finish in self.late:
+            if there is None:
+                finish()
+            else:
+                pl.when(there)(finish)
+
+
+def halves(ref, which):
+    half = ref.shape[-1] // 2
+    cols = pl.ds(pl.multiple_of(which * half, 128), half)
+    return ref.at[:, :, :, cols] if len(ref.shape) == 4 else ref.at[:, cols]
+
+
+class Reduction:
+    def __init__(self, links, source, total, mine, crecv, yrecv, zrecv, xrecv, sems, number):
+        self.links, self.source, self.total, self.mine = links, source, total, mine
+        self.crecv, self.yrecv, self.zrecv, self.xrecv = crecv, yrecv, zrecv, xrecv
+        self.sems, self.number = sems, number
+        self.whole = total.shape[-1] % 256 != 0
+        self.load = None
+
+    def sem(self, name, *index):
+        return self.sems[name].at[index + (self.number,)]
+
+    def begin(self):
+        links = self.links
+        other = self.source if self.whole else halves(self.source, 1 - links.core)
+        links.send(None, other, self.crecv, self.sem("c_send"), self.sem("c_recv"), {"rep": links.mate})
+        if self.mine is None:
+            self.mine = self.source if self.whole else halves(self.source, links.core)
+        else:
+            own = self.source if self.whole else halves(self.source, links.core)
+            self.load = pltpu.make_async_copy(own, self.mine, self.sem("m_sem"))
+            self.load.start()
+
+    def pair(self):
+        links = self.links
+        if self.load is not None:
+            self.load.wait()
+        links.arrive(self.crecv, self.sem("c_recv"), self.sems["spare"].at[0])
+        inner = links.inner
+
+        def add(index, carry):
+            row, col = index // inner, index % inner
+            self.mine[row, col] = self.mine[row, col] + self.crecv[row, col]
+            return carry
+
+        lax.fori_loop(0, links.outer * inner, add, 0)
+        links.send(None, self.mine.at[:, 1 - links.col], self.yrecv, self.sem("y_send"), self.sem("y_recv"),
+                   {"fsdp": links.spot + 1 - 2 * links.col})
+
+    def slot(self, way, place, dest):
+        return dest - place if way == 0 else self.links.outer - place + dest
+
+    def pass_on(self, way, dest, first):
+        links = self.links
+        step = 1 if way == 0 else -1
+        place, size = links.row, links.outer
+        passes = place < dest if way == 0 else place > dest
+        start = place == 0 if way == 0 else place == size - 1
+        mine = self.mine.at[dest, links.col]
+        put = self.slot(way, place + step, dest)
+        there = jnp.logical_and(passes, start if first else jnp.logical_not(start))
+        if not first:
+            got = self.slot(way, place, dest)
+
+            @pl.when(there)
+            def _():
+                links.arrive(self.zrecv.at[got], self.sem("z_recv", got), self.sems["spare"].at[0])
+                mine[...] = mine[...] + self.zrecv[got]
+
+        links.send(there, mine, self.zrecv.at[put], self.sem("z_send", way, dest), self.sem("z_recv", put),
+                   {"fsdp": links.spot + step * links.inner})
+
+    def column(self):
+        links = self.links
+        links.arrive(self.yrecv, self.sem("y_recv"), self.sems["spare"].at[0])
+
+        def add(index, carry):
+            self.mine[index, links.col] = self.mine[index, links.col] + self.yrecv[index]
+            return carry
+
+        lax.fori_loop(0, links.outer, add, 0)
+        for far in range(links.outer - 1, 0, -1):
+            self.pass_on(0, far, True)
+            self.pass_on(1, links.outer - 1 - far, True)
+
+    def line(self):
+        links = self.links
+        size, place = links.outer, links.row
+        for far in range(size - 1, 0, -1):
+            self.pass_on(0, far, False)
+            self.pass_on(1, size - 1 - far, False)
+        mine = self.mine.at[place, links.col]
+        for way in range(2):
+            got = self.slot(way, place, place)
+
+            @pl.when(place > 0 if way == 0 else place < size - 1)
+            def _():
+                links.arrive(self.zrecv.at[got], self.sem("z_recv", got), self.sems["spare"].at[0])
+                mine[...] = mine[...] + self.zrecv[got]
+
+        links.send(None, mine, self.xrecv, self.sem("x_send"), self.sem("x_recv"), {"rep": links.across})
+
+    def finish(self):
+        links = self.links
+        links.arrive(self.xrecv, self.sem("x_recv"), self.sems["spare"].at[0])
+        value = self.mine[links.row, links.col].astype(F32) + self.xrecv[...].astype(F32)
+        if self.whole:
+            self.total[...] = value
+            return
+        place = halves(self.total, links.core)
+        place[...] = value
+        links.send(None, place, place, self.sem("f_send"), self.sem("f_recv"), {"rep": links.mate})
+
+    def settle(self):
+        if not self.whole:
+            self.links.arrive(
+                halves(self.total, 1 - self.links.core), self.sem("f_recv"), self.sems["spare"].at[0]
+            )
+
+
+SEM_NAMES = ("c_send", "c_recv", "m_sem", "y_send", "y_recv", "z_send", "z_recv", "x_send", "x_recv",
+             "f_send", "f_recv", "r_send", "r_recv", "own", "spare")
+
+
+class Return:
+    def __init__(self, links, source, home, sems, kind):
+        self.links, self.source, self.home, self.sems, self.kind = links, source, home, sems, kind
+
+    def begin(self):
+        links = self.links
+        dst = self.home.at[links.rank]
+        for way, device in enumerate((links.across, links.mate)):
+            links.send(None, self.source, dst, self.sems["r_send"].at[self.kind, way],
+                       self.sems["r_recv"].at[self.kind, way], {"rep": device})
+        self.copy = pltpu.make_async_copy(self.source, dst, self.sems["own"].at[self.kind])
+        self.copy.start()
+
+    def relay(self):
+        links = self.links
+        place = self.home.at[links.across]
+        links.arrive(place, self.sems["r_recv"].at[self.kind, 0], self.sems["spare"].at[0])
+        links.send(None, place, place, self.sems["r_send"].at[self.kind, 2],
+                   self.sems["r_recv"].at[self.kind, 2], {"rep": links.mate})
+
+    def settle(self):
+        links, sem = self.links, self.sems["r_recv"]
+        links.arrive(self.home.at[links.mate], sem.at[self.kind, 1], self.sems["spare"].at[0])
+        links.arrive(self.home.at[across_of(links.mate)], sem.at[self.kind, 2], self.sems["spare"].at[0])
+        self.copy.wait()
+
+
+def back_kernel(outer, inner, early, *refs):
+    (tab_ref, x_ref, gh_ref, ga_ref, att_ref, lse_ref, n_ref, qkv_ref, gain_ref, gc_ref, w_ref), refs = refs[:11], refs[11:]
+    grads, (y_ref,), refs = refs[:early], refs[early : early + 1], refs[early + 1 :]
+    kinds = early + 4
+    totals, (ry_ref, rg_ref), refs = refs[:kinds], refs[kinds : kinds + 2], refs[kinds + 2 :]
+    (dq_ref, dkw_ref, dvw_ref, dc_ref), refs = refs[:4], refs[4:]
+    (g_ref, dqkv_ref, dk_ref, dv_ref), refs = refs[:4], refs[4:]
+    mines, refs = list(refs[:early]) + [None] * 3 + [refs[early]], refs[early + 1 :]
+    crecv, yrecv, zrecv, xrecv = (refs[kinds * i : kinds * (i + 1)] for i in range(4))
+    sems = dict(zip(SEM_NAMES, refs[4 * kinds :]))
+    links = Links(outer, inner)
+    rank = links.rank
+    sources = list(grads) + [dq_ref, dkw_ref, dvw_ref, dc_ref]
+    tasks = [
+        Reduction(links, sources[i], totals[i], mines[i], crecv[i], yrecv[i], zrecv[i], xrecv[i], sems, i)
+        for i in range(kinds)
+    ]
+    rows_y, rows_g = Return(links, y_ref, ry_ref, sems, 0), Return(links, g_ref, rg_ref, sems, 1)
+
+    links.greet()
+    for task in tasks[:early]:
+        task.begin()
+    rows_y.begin()
+    gains = gains_of(gc_ref)
+    for task in tasks[:early]:
+        task.pair()
+    backward_attention_start(dk_ref, dv_ref)
+    backward_attention_tiles(tab_ref, rank, qkv_ref, att_ref, ga_ref, lse_ref, dqkv_ref, dk_ref, dv_ref, 0, TILES)
+    tasks[0].column()
+    backward_attention_end(dqkv_ref, dk_ref, dv_ref)
+    weight_grads(n_ref, dqkv_ref, (dq_ref, dkw_ref, dvw_ref))
+    for task in tasks[early : early + 3]:
+        task.begin()
+    rows_y.relay()
+    one, side = backward_project(tab_ref, rank, x_ref, gh_ref, gains, n_ref, dqkv_ref, w_ref, dk_ref, g_ref)
+    spread_gain_grads(jnp.concatenate([one, side, gain_ref[...], jnp.zeros((5, D), F32)], axis=0), dc_ref)
+    rows_g.begin()
+    tasks[kinds - 1].begin()
+    for task in tasks[early:]:
+        task.pair()
+    for number in range(kinds):
+        if number + 1 < kinds:
+            tasks[number + 1].column()
+        tasks[number].line()
+        if number == 2:
+            rows_g.relay()
+        if number > 0:
+            tasks[number - 1].finish()
+    tasks[-1].finish()
+    rows_y.settle()
+    rows_g.settle()
+    for task in tasks:
+        task.settle()
+    links.drain()
+
+
+def attend_back(count, table, x, gh, ga, att, lse, n, qkv, gain, gc, w, grads, y):
+    outer, inner = grid_of(count)
+    part = D // count
+    early = len(grads)
+    kinds = early + 4
+    grads = [grad.reshape((outer, inner, -1) + grad.shape[1:]) for grad in grads]
+    shapes = [grad.shape[2:] for grad in grads] + [(part, D)] * 3 + [(8, 128)]
+    dtypes = [BF16] * (kinds - 1) + [F32]
+    halved = [(a, b // 2 if b % 256 == 0 else b) for a, b in shapes]
+    dma = pltpu.SemaphoreType.DMA
+    scratch = [pltpu.VMEM((outer, inner) + shape, dtype) for shape, dtype in zip(shapes[early:], dtypes[early:])]
+    scratch += [pltpu.VMEM((SLOTS, BLK, D), BF16), pltpu.VMEM((ALL_ROWS, 3 * D), BF16),
+                pltpu.VMEM((ALL_ROWS, D), F32), pltpu.VMEM((ALL_ROWS, D), F32)]
+    scratch += [pltpu.VMEM((outer, inner) + shape, BF16) for shape in halved[:early]]
+    scratch += [pltpu.VMEM((outer, inner) + halved[-1], F32)]
+    for lead in ((outer, inner), (outer,), (outer + 1,), ()):
+        scratch += [pltpu.VMEM(lead + shape, dtype) for shape, dtype in zip(halved, dtypes)]
+    one = dma((kinds,))
+    scratch += [one, one, one, one, one, dma((2, outer, kinds)), dma((outer + 1, kinds)), one, one, one, one,
+                dma((2, 3)), dma((2, 3)), dma((2,)), dma((1,))]
+    rows = jax.ShapeDtypeStruct((4, SLOTS, BLK, D), BF16)
+    outs = pl.pallas_call(
+        partial(back_kernel, outer, inner, early),
+        out_shape=tuple(jax.ShapeDtypeStruct(shape, F32) for shape in shapes) + (rows, rows),
+        grid=(1,),
+        in_specs=[SMEM] + [VMEM] * 9 + [pl.BlockSpec((D, 3 * D), lambda step: (0, 0))] + [ANY] * early + [VMEM],
+        out_specs=(VMEM,) * kinds + (ANY, ANY),
+        scratch_shapes=scratch,
+        compiler_params=pltpu.CompilerParams(
+            collective_id=2, has_side_effects=True, vmem_limit_bytes=VMEM_LIMIT
+        ),
+        name="attend_back_and_reduce",
+    )(table, x, gh, ga, att, lse, n, qkv, gain, gc, w, *grads, y.reshape(SLOTS, BLK, D))
+    return outs[:kinds], outs[kinds], outs[kinds + 1]
 
 
 def per_device(count, layer_input, cotangent, lengths, attn_gain, global_gain, query_weight, key_weight,
@@ -1127,18 +1448,24 @@
         count, splits, table,
         layer_input.reshape(blocks, BLK, width), cotangent.reshape(blocks, BLK, width), wa, down_weight, wc,
     )
-    y, g, dg, db, do, dw, dc = layer(
-        table, rows.reshape(ROWS, width), cots.reshape(ROWS, width), gc, ga.reshape(width, -1), gb.reshape(-1, width)
+    x, full = rows.reshape(ROWS, width), ga.reshape(width, -1)
+    n, qkv, att, lse, y, gh, gatt, dg, du, db, do, gain = forward_layer(
+        table, x, cots.reshape(ROWS, width), gc, full, gb.reshape(-1, width)
     )
-    grads = [grad.reshape(count, -1, grad.shape[-1]) for grad in (dg, db, do, dw, dc)]
-    og, ob, oo, ow, oc, ry, rg = reduce_grads(
-        count, grads, y.reshape(SLOTS, BLK, width), g.reshape(SLOTS, BLK, width)
-    )
+    if grid_of(count)[1] == 2 and part % 16 == 0:
+        totals, ry, rg = attend_back(count, table, x, gh, gatt, att, lse, n, qkv, gain, gc, full, (dg, du, db, do), y)
+        og, ou, ob, oo, oq, ok, ov, oc = totals
+    else:
+        g, dw, dc = backward_layer(table, x, gh, gatt, att, lse, n, qkv, gain, gc, full)
+        grads = [grad.reshape(count, -1, grad.shape[-1]) for grad in (dg, du, db, do, dw, dc)]
+        og, ou, ob, oo, ow, oc, ry, rg = reduce_grads(
+            count, grads, y.reshape(SLOTS, BLK, width), g.reshape(SLOTS, BLK, width)
+        )
+        oq, ok, ov = ow[:, :width], ow[:, width : 2 * width], ow[:, 2 * width :]
     y_home, g_home = bring_home(table, ry, rg, blocks)
     return (
         y_home.reshape(layer_input.shape), g_home.reshape(layer_input.shape),
-        oc[0, :part], oc[1, :part], ow[:, :width], ow[:, width : 2 * width], ow[:, 2 * width :], oo,
-        oc[2, :part], og[:, :hidden], og[:, hidden:], ob,
+        oc[0, :part], oc[1, :part], oq, ok, ov, oo, oc[2, :part], og, ou, ob,
     )
 
 

time: 372 us -> 332 us (0.89)
  Pallas kernels: 358 us -> 316 us
    pallas_call x4 -> x3, Pallas kernels: 247 us -> 205 us  [the longest x1 142 us: attend_back(): pl.pallas_call(partial(back_kernel, outer, inner, early), out_shape=tuple...]
    unnamed x21 -> x32, local copies, waits for them, and re-layouts: 6.41 us -> 10.3 us
where the time goes in v3:
time: 332 us; the launch traced here: 331 us
  Pallas kernels  316 us (95%)
  local copies, waits for them, and re-layouts  13 us (4%)
    pallas_call x1, Pallas kernels, attend_back(): pl.pallas_call(partial(back_kernel, outer, inner, early), out_shape=tuple...  142 us
    pallas_call x1, Pallas kernels, gather_weights(): pl.pallas_call(partial(gather_kernel, outer, inner, splits), out_shape=(j...  88 us
    pallas_call x1, Pallas kernels, forward_layer(): pl.pallas_call(second_kernel, out_shape=(shape((ROWS, D), BF16), shape((R...  39.5 us
    pallas_call x1, Pallas kernels, forward_layer(): pl.pallas_call(first_kernel, out_shape=(shape((ALL_ROWS, D), BF16), shape...  23.9 us
    pallas_call x1, Pallas kernels, deal_table(): pl.pallas_call(partial(table_kernel, micro, per_dev), out_shape=jax.Shape...  10.4 us
    unnamed x32, local copies, waits for them, and re-layouts  10.3 us

profile of v3, /device:TPU:0, one launch (start us, length us, event | category | flops | bytes accessed | tf_op | source)
XLA Modules:
  0.0 331.3 jit_solution(17554426601751563578)
XLA Ops:
  0.6 0.0 copy-start.5
  0.7 0.0 copy-start.4
  0.7 1.3 pad.8.lens_ref
  2.0 1.3 fusion.8.wc_ref
  3.3 5.9 %lens_exchange.1.lens_ref = s32[4,8,128]{2,1,0:T(8,128)} custom-call(s32[8,128]{1,0:T(8,128)} %pad.8.lens_ref), custom_call_target="tpu_custom_call" | custom-call | tf_op jit(solution)/shard_map/lens_exchange/pallas_call | solution.py:147
  9.2 10.4 %deal_table.1.tab_ref.refs_0_ = s32[256]{0:T(256)} custom-call(s32[4,8,128]{2,1,0:T(8,128)} %lens_exchange.1.lens_ref), custom_call_target="tpu_custom_call" | custom-call | tf_op jit(solution)/shard_map/deal_table/pallas_call | solution.py:156
  19.6 0.9 constant_dynamic-update-slice_fusion.5
  20.5 0.9 constant_dynamic-update-slice_fusion.4
  21.5 0.9 constant_dynamic-update-slice_fusion.3
  22.4 0.9 constant_dynamic-update-slice_fusion.2
  23.3 0.0 copy-done.4
  23.4 0.0 copy-done.5
  23.4 0.0 copy-start
  23.4 1.1 copy-done
  24.5 88.0 %gather_and_deal.1 = (bf16[8,96,7168]{2,1,0:T(8,128)(2,1)}, bf16[8,256,768]{2,1,0:T(8,128)(2,1)}, bf16[8,16,128]{2,1,0:T(8,128)(2,1)}, bf16[10,64,768]{2,1,0:T(8,128)(2,1)}, bf16[10,64,768]{2,1,0:T(8,128)(2,1)}) custom-call(s32[256]{0:T(256)} %deal_table.1.tab_ref.refs_0_, bf16[24,64,768]{2,1,0:T(8,128)(2,1)} %bitcast.32, bf16[24,64,768]{2,1,0:T(8,128)(2,1)} %bitcast.33, ...), custom_call_target="tpu_custom_call" | custom-call | tf_op jit(solution)/shard_map/gather_and_deal/pallas_call | solution.py:412
  112.5 23.9 %attend.1 = (bf16[688,768]{1,0:T(8,128)(2,1)}, bf16[688,2304]{1,0:T(8,128)(2,1)}, bf16[640,768]{1,0:T(8,128)(2,1)}, f32[5,16,128]{2,1,0:T(8,128)}) custom-call(s32[256]{0:T(256)} %deal_table.1.tab_ref.refs_0_, bf16[640,768]{1,0:T(8,128)(2,1)} %bitcast.25, bf16[8,16,128]{2,1,0:T(8,128)(2,1)} %get-tuple-element.43.gc_ref.refs_9_, bf16[768,7168]{1,0:T(8,128)(2,1)} %bitcast.22), custom_call_target="tpu_custom_call" | custom-call | tf_op jit(solution)/shard_map/attend/pallas_call | solution.py:1098
  136.5 39.5 %feed_forward.1 = (bf16[640,768]{1,0:T(8,128)(2,1)}, f32[640,768]{1,0:T(8,128)}, bf16[640,768]{1,0:T(8,128)(2,1)}, bf16[768,2048]{1,0:T(8,128)(2,1)}, bf16[768,2...) custom-call(s32[256]{0:T(256)} %deal_table.1.tab_ref.refs_0_, ...), custom_call_target="tpu_custom_call" | custom-call | tf_op jit(solution)/shard_map/feed_forward/pallas_call | solution.py:1108
  176.0 141.8 %attend_back_and_reduce.1 = (f32[96,2048]{1,0:T(8,128)}, f32[96,2048]{1,0:T(8,128)}, f32[256,768]{1,0:T(8,128)}, f32[96,768]{1,0:T(8,128)}, f32[96,768]{1,0:T(8,...) custom-call(s32[256]{0:T(256)} %deal_table.1.tab_ref.refs_0_, ...), custom_call_target="tpu_custom_call" | custom-call | tf_op jit(solution)/shard_map/attend_back_and_reduce/pallas_call | solution.py:1422
  317.9 0.0 copy-start.9
  317.9 0.0 copy-start.8
  317.9 0.0 copy-start.7
  317.9 6.6 %place_rows.1 = (bf16[24,64,768]{2,1,0:T(8,128)(2,1)}, bf16[24,64,768]{2,1,0:T(8,128)(2,1)}) custom-call(s32[256]{0:T(256)} %deal_table.1.tab_ref.refs_0_, bf16[4,10,64,768]{3,2,1,0:T(8,128)(2,1)} %get-tuple-element.58.ry_ref, bf16[4,10,64,768]{3,2,1,0:T(8,128)(2,1)} %get-tuple-element.59.rg_ref), custom_call_target="tpu_custom_call" | custom-call | tf_op jit(solution)/shard_map/place_rows/pallas_call | solution.py:669
  324.5 1.3 slice_bitcast_fusion
  325.8 0.7 copy.37
  326.5 0.7 copy.38
  327.3 0.7 copy.39
  328.0 0.0 copy-done.6
  328.0 0.7 copy.40
  328.7 0.9 copy.41
  329.6 0.0 copy-done.2
  329.6 0.9 copy.42
  330.5 0.9 copy.43
  (11 shorter events, 0.1 us)
Async XLA Ops:
  0.6 22.7 %copy-start.5 = (bf16[96,2048]{1,0:T(8,128)(2,1)S(1)}, bf16[96,2048]{1,0:T(8,128)(2,1)}, u32[]{:S(2)}) copy-start(bf16[96,2048]{1,0:T(8,128)(2,1)} %param.24) | copy-start | bytes 1179652
  0.7 22.7 %copy-start.4 = (bf16[96,2048]{1,0:T(8,128)(2,1)S(1)}, bf16[96,2048]{1,0:T(8,128)(2,1)}, u32[]{:S(2)}) copy-start(bf16[96,2048]{1,0:T(8,128)(2,1)} %param.23) | copy-start | bytes 1179652
  23.4 1.1 copy-start
  317.9 8.0 %copy-start.9 = (f32[96,768]{1,0:T(8,128)S(1)}, f32[96,768]{1,0:T(8,128)}, u32[]{:S(2)}) copy-start(f32[96,768]{1,0:T(8,128)} %get-tuple-element.89) | copy-start | bytes 884740
  317.9 8.7 %copy-start.8 = (f32[96,768]{1,0:T(8,128)S(1)}, f32[96,768]{1,0:T(8,128)}, u32[]{:S(2)}) copy-start(f32[96,768]{1,0:T(8,128)} %get-tuple-element.90) | copy-start | bytes 884740
  317.9 9.4 %copy-start.7 = (f32[96,768]{1,0:T(8,128)S(1)}, f32[96,768]{1,0:T(8,128)}, u32[]{:S(2)}) copy-start(f32[96,768]{1,0:T(8,128)} %get-tuple-element.91) | copy-start | bytes 884740
  324.5 3.5 %copy-start.6 = (f32[96,768]{1,0:T(8,128)S(1)}, f32[96,768]{1,0:T(8,128)}, u32[]{:S(2)}) copy-start(f32[96,768]{1,0:T(8,128)} %get-tuple-element.92) | copy-start | bytes 884740
  324.5 4.2 %copy-start.3 = (f32[96,2048]{1,0:T(8,128)S(1)}, f32[96,2048]{1,0:T(8,128)}, u32[]{:S(2)}) copy-start(f32[96,2048]{1,0:T(8,128)} %get-tuple-element.94) | copy-start | bytes 2359300
  327.3 2.3 copy-start.2
  328.7 1.8 copy-start.1

commit v4 on v3

--- a/solution.py
+++ b/solution.py
@@ -1243,17 +1243,13 @@
     def slot(self, way, place, dest):
         return dest - place if way == 0 else self.links.outer - place + dest
 
-    def pass_on(self, way, dest, first):
+    def pass_on(self, way, dest, there, first):
         links = self.links
         step = 1 if way == 0 else -1
-        place, size = links.row, links.outer
-        passes = place < dest if way == 0 else place > dest
-        start = place == 0 if way == 0 else place == size - 1
         mine = self.mine.at[dest, links.col]
-        put = self.slot(way, place + step, dest)
-        there = jnp.logical_and(passes, start if first else jnp.logical_not(start))
+        put = self.slot(way, links.row + step, dest)
         if not first:
-            got = self.slot(way, place, dest)
+            got = self.slot(way, links.row, dest)
 
             @pl.when(there)
             def _():
@@ -1265,32 +1261,38 @@
 
     def column(self):
         links = self.links
+        size = links.outer
         links.arrive(self.yrecv, self.sem("y_recv"), self.sems["spare"].at[0])
 
         def add(index, carry):
             self.mine[index, links.col] = self.mine[index, links.col] + self.yrecv[index]
             return carry
 
-        lax.fori_loop(0, links.outer, add, 0)
-        for far in range(links.outer - 1, 0, -1):
-            self.pass_on(0, far, True)
-            self.pass_on(1, links.outer - 1 - far, True)
-
-    def line(self):
+        lax.fori_loop(0, size, add, 0)
+        for far in range(size - 1, 0, -1):
+            self.pass_on(0, far, links.row == 0, True)
+            self.pass_on(1, size - 1 - far, links.row == size - 1, True)
+
+    def hop(self, turn):
         links = self.links
-        size, place = links.outer, links.row
-        for far in range(size - 1, 0, -1):
-            self.pass_on(0, far, False)
-            self.pass_on(1, size - 1 - far, False)
-        mine = self.mine.at[place, links.col]
+        size = links.outer
         for way in range(2):
+            place = turn if way == 0 else size - 1 - turn
+            here = links.row == place
+            rest = range(size - 1, place, -1) if way == 0 else range(0, place)
+            for dest in rest:
+                self.pass_on(way, dest, here, False)
+            mine = self.mine.at[place, links.col]
             got = self.slot(way, place, place)
 
-            @pl.when(place > 0 if way == 0 else place < size - 1)
+            @pl.when(here)
             def _():
                 links.arrive(self.zrecv.at[got], self.sem("z_recv", got), self.sems["spare"].at[0])
                 mine[...] = mine[...] + self.zrecv[got]
 
+    def cross(self):
+        links = self.links
+        mine = self.mine.at[links.row, links.col]
         links.send(None, mine, self.xrecv, self.sem("x_send"), self.sem("x_recv"), {"rep": links.across})
 
     def finish(self):
@@ -1382,15 +1384,18 @@
     tasks[kinds - 1].begin()
     for task in tasks[early:]:
         task.pair()
-    for number in range(kinds):
-        if number + 1 < kinds:
-            tasks[number + 1].column()
-        tasks[number].line()
+    for number in range(1, kinds + outer):
+        if number < kinds:
+            tasks[number].column()
         if number == 2:
             rows_g.relay()
-        if number > 0:
-            tasks[number - 1].finish()
-    tasks[-1].finish()
+        for turn in range(1, outer):
+            if 0 <= number - turn < kinds:
+                tasks[number - turn].hop(turn)
+        if 0 <= number - outer + 1 < kinds:
+            tasks[number - outer + 1].cross()
+        if 0 <= number - outer < kinds:
+            tasks[number - outer].finish()
     rows_y.settle()
     rows_g.settle()
     for task in tasks:

time: 332 us -> 301 us (0.907)
  Pallas kernels: 316 us -> 286 us
    pallas_call x1, Pallas kernels: 142 us -> 112 us  [attend_back(): pl.pallas_call(partial(back_kernel, outer, inner, early), out_shape=tuple...]
where the time goes in v4:
time: 301 us
  Pallas kernels  286 us (95%)
  local copies, waits for them, and re-layouts  13 us (4%)
    pallas_call x1, Pallas kernels, attend_back(): pl.pallas_call(partial(back_kernel, outer, inner, early), out_shape=tuple...  112 us
    pallas_call x1, Pallas kernels, gather_weights(): pl.pallas_call(partial(gather_kernel, outer, inner, splits), out_shape=(j...  87.9 us
    pallas_call x1, Pallas kernels, forward_layer(): pl.pallas_call(second_kernel, out_shape=(shape((ROWS, D), BF16), shape((R...  39.5 us
    pallas_call x1, Pallas kernels, forward_layer(): pl.pallas_call(first_kernel, out_shape=(shape((ALL_ROWS, D), BF16), shape...  23.9 us
    pallas_call x1, Pallas kernels, deal_table(): pl.pallas_call(partial(table_kernel, micro, per_dev), out_shape=jax.Shape...  10.5 us
    unnamed x32, local copies, waits for them, and re-layouts  10.3 us
    pallas_call x1, Pallas kernels, bring_home(): pl.pallas_call(home_kernel, out_shape=(shape, shape), in_specs=[SMEM, VME...  6.61 us

profile of v4, /device:TPU:0, one launch (start us, length us, event | category | flops | bytes accessed | tf_op | source)
XLA Modules:
  0.0 301.0 jit_solution(11609129954972804479)
XLA Ops:
  0.6 0.0 copy-start.5
  0.7 0.0 copy-start.4
  0.7 1.3 pad.8.lens_ref
  2.0 1.3 fusion.8.wc_ref
  3.3 5.9 %lens_exchange.1.lens_ref = s32[4,8,128]{2,1,0:T(8,128)} custom-call(s32[8,128]{1,0:T(8,128)} %pad.8.lens_ref), custom_call_target="tpu_custom_call" | custom-call | tf_op jit(solution)/shard_map/lens_exchange/pallas_call | solution.py:147
  9.2 10.5 %deal_table.1.tab_ref.refs_0_ = s32[256]{0:T(256)} custom-call(s32[4,8,128]{2,1,0:T(8,128)} %lens_exchange.1.lens_ref), custom_call_target="tpu_custom_call" | custom-call | tf_op jit(solution)/shard_map/deal_table/pallas_call | solution.py:156
  19.7 0.9 constant_dynamic-update-slice_fusion.5
  20.6 0.9 constant_dynamic-update-slice_fusion.4
  21.5 0.9 constant_dynamic-update-slice_fusion.3
  22.4 0.9 constant_dynamic-update-slice_fusion.2
  23.4 0.0 copy-done.4
  23.4 0.0 copy-done.5
  23.5 0.0 copy-start
  23.5 1.1 copy-done
  24.5 87.9 %gather_and_deal.1 = (bf16[8,96,7168]{2,1,0:T(8,128)(2,1)}, bf16[8,256,768]{2,1,0:T(8,128)(2,1)}, bf16[8,16,128]{2,1,0:T(8,128)(2,1)}, bf16[10,64,768]{2,1,0:T(8,128)(2,1)}, bf16[10,64,768]{2,1,0:T(8,128)(2,1)}) custom-call(s32[256]{0:T(256)} %deal_table.1.tab_ref.refs_0_, bf16[24,64,768]{2,1,0:T(8,128)(2,1)} %bitcast.32, bf16[24,64,768]{2,1,0:T(8,128)(2,1)} %bitcast.33, ...), custom_call_target="tpu_custom_call" | custom-call | tf_op jit(solution)/shard_map/gather_and_deal/pallas_call | solution.py:412
  112.5 23.9 %attend.1 = (bf16[688,768]{1,0:T(8,128)(2,1)}, bf16[688,2304]{1,0:T(8,128)(2,1)}, bf16[640,768]{1,0:T(8,128)(2,1)}, f32[5,16,128]{2,1,0:T(8,128)}) custom-call(s32[256]{0:T(256)} %deal_table.1.tab_ref.refs_0_, bf16[640,768]{1,0:T(8,128)(2,1)} %bitcast.25, bf16[8,16,128]{2,1,0:T(8,128)(2,1)} %get-tuple-element.43.gc_ref.refs_9_, bf16[768,7168]{1,0:T(8,128)(2,1)} %bitcast.22), custom_call_target="tpu_custom_call" | custom-call | tf_op jit(solution)/shard_map/attend/pallas_call | solution.py:1098
  136.4 39.5 %feed_forward.1 = (bf16[640,768]{1,0:T(8,128)(2,1)}, f32[640,768]{1,0:T(8,128)}, bf16[640,768]{1,0:T(8,128)(2,1)}, bf16[768,2048]{1,0:T(8,128)(2,1)}, bf16[768,2...) custom-call(s32[256]{0:T(256)} %deal_table.1.tab_ref.refs_0_, ...), custom_call_target="tpu_custom_call" | custom-call | tf_op jit(solution)/shard_map/feed_forward/pallas_call | solution.py:1108
  176.0 111.6 %attend_back_and_reduce.1 = (f32[96,2048]{1,0:T(8,128)}, f32[96,2048]{1,0:T(8,128)}, f32[256,768]{1,0:T(8,128)}, f32[96,768]{1,0:T(8,128)}, f32[96,768]{1,0:T(8,...) custom-call(s32[256]{0:T(256)} %deal_table.1.tab_ref.refs_0_, ...), custom_call_target="tpu_custom_call" | custom-call | tf_op jit(solution)/shard_map/attend_back_and_reduce/pallas_call | solution.py:1427
  287.5 0.0 copy-start.9
  287.6 0.0 copy-start.8
  287.6 6.6 %place_rows.1 = (bf16[24,64,768]{2,1,0:T(8,128)(2,1)}, bf16[24,64,768]{2,1,0:T(8,128)(2,1)}) custom-call(s32[256]{0:T(256)} %deal_table.1.tab_ref.refs_0_, bf16[4,10,64,768]{3,2,1,0:T(8,128)(2,1)} %get-tuple-element.58.ry_ref, bf16[4,10,64,768]{3,2,1,0:T(8,128)(2,1)} %get-tuple-element.59.rg_ref), custom_call_target="tpu_custom_call" | custom-call | tf_op jit(solution)/shard_map/place_rows/pallas_call | solution.py:669
  294.2 1.3 slice_bitcast_fusion
  295.5 0.7 copy.37
  296.2 0.7 copy.38
  296.9 0.7 copy.39
  297.6 0.0 copy-done.6
  297.7 0.7 copy.40
  298.4 0.0 copy-done.3
  298.4 0.9 copy.41
  299.3 0.0 copy-done.2
  299.3 0.9 copy.42
  300.1 0.9 copy.43
  (11 shorter events, 0.1 us)
Async XLA Ops:
  0.6 22.8 %copy-start.5 = (bf16[96,2048]{1,0:T(8,128)(2,1)S(1)}, bf16[96,2048]{1,0:T(8,128)(2,1)}, u32[]{:S(2)}) copy-start(bf16[96,2048]{1,0:T(8,128)(2,1)} %param.24) | copy-start | bytes 1179652
  0.7 22.7 %copy-start.4 = (bf16[96,2048]{1,0:T(8,128)(2,1)S(1)}, bf16[96,2048]{1,0:T(8,128)(2,1)}, u32[]{:S(2)}) copy-start(bf16[96,2048]{1,0:T(8,128)(2,1)} %param.23) | copy-start | bytes 1179652
  23.5 1.1 copy-start
  287.5 8.0 %copy-start.9 = (f32[96,768]{1,0:T(8,128)S(1)}, f32[96,768]{1,0:T(8,128)}, u32[]{:S(2)}) copy-start(f32[96,768]{1,0:T(8,128)} %get-tuple-element.89) | copy-start | bytes 884740
  287.6 8.7 %copy-start.8 = (f32[96,768]{1,0:T(8,128)S(1)}, f32[96,768]{1,0:T(8,128)}, u32[]{:S(2)}) copy-start(f32[96,768]{1,0:T(8,128)} %get-tuple-element.90) | copy-start | bytes 884740
  287.6 9.4 %copy-start.7 = (f32[96,768]{1,0:T(8,128)S(1)}, f32[96,768]{1,0:T(8,128)}, u32[]{:S(2)}) copy-start(f32[96,768]{1,0:T(8,128)} %get-tuple-element.91) | copy-start | bytes 884740
  294.2 3.5 %copy-start.6 = (f32[96,768]{1,0:T(8,128)S(1)}, f32[96,768]{1,0:T(8,128)}, u32[]{:S(2)}) copy-start(f32[96,768]{1,0:T(8,128)} %get-tuple-element.92) | copy-start | bytes 884740
  294.2 4.2 %copy-start.3 = (f32[96,2048]{1,0:T(8,128)S(1)}, f32[96,2048]{1,0:T(8,128)}, u32[]{:S(2)}) copy-start(f32[96,2048]{1,0:T(8,128)} %get-tuple-element.94) | copy-start | bytes 2359300
  296.9 2.3 copy-start.2
  298.4 1.8 copy-start.1

commit v5 on v4

--- a/solution.py
+++ b/solution.py
@@ -654,7 +654,7 @@
     base = lax.axis_index("rep") * y_ref.shape[0]
 
     def fetch(block, carry):
-        index = tab_ref[DEST_AT + base + block]
+        index = tab_ref[DEST_AT + base + block] if len(tab_ref.shape) == 1 else tab_ref[48, base + block]
         safe = jnp.maximum(index, 0)
         for src, dst in ((ry_ref, y_ref), (rg_ref, g_ref)):
             value = src[safe // SLOTS, safe % SLOTS]
@@ -714,9 +714,25 @@
     return out
 
 
+def block_at(tab_ref, slot):
+    return lax.rem(tab_ref[slot, 0], 128) - 1
+
+
+def seg_at(tab_ref, slot):
+    if len(tab_ref.shape) == 1:
+        return tab_ref[SEG_AT + slot]
+    return lax.div(tab_ref[slot, 0], 16384) - 1
+
+
+def len_at(tab_ref, slot):
+    if len(tab_ref.shape) == 1:
+        return tab_ref[LEN_AT + slot]
+    return lax.rem(lax.div(tab_ref[slot, 0], 128), 128)
+
+
 def slot_info(tab_ref, rank):
-    seg = [tab_ref[SEG_AT + rank * SLOTS + slot] for slot in range(SLOTS)]
-    length = [tab_ref[LEN_AT + rank * SLOTS + slot] for slot in range(SLOTS)]
+    seg = [seg_at(tab_ref, rank * SLOTS + slot) for slot in range(SLOTS)]
+    length = [len_at(tab_ref, rank * SLOTS + slot) for slot in range(SLOTS)]
     return seg, length
 
 
@@ -736,8 +752,8 @@
 def key_segments(tab_ref, rank, first_block, index):
     blocks = WIN // BLK
     base = rank * SLOTS + first_block
-    seg = [tab_ref[SEG_AT + base + step] for step in range(blocks)]
-    length = [tab_ref[LEN_AT + base + step] for step in range(blocks)]
+    seg = [seg_at(tab_ref, base + step) for step in range(blocks)]
+    length = [len_at(tab_ref, base + step) for step in range(blocks)]
     alive = (index % BLK) < pick_by(index // BLK, length, 0)
     return jnp.where(alive, pick_by(index // BLK, seg, -2), -2)
 
@@ -754,8 +770,8 @@
     q_index = iota(qs, 1 - keys_axis)
     k_index = iota(ks, keys_axis)
     g_index = iota(gs, keys_axis)
-    base = SEG_AT + rank * SLOTS + tile * (QT // BLK)
-    q_seg = pick_by(q_index // BLK, [tab_ref[base + step] for step in range(QT // BLK)], -1)
+    base = rank * SLOTS + tile * (QT // BLK)
+    q_seg = pick_by(q_index // BLK, [seg_at(tab_ref, base + step) for step in range(QT // BLK)], -1)
     k_seg = key_segments(tab_ref, rank, first_row // BLK, k_index)
     g_seg = side_segments(tab_ref, rank, g_index)
     gap = (q_index + tile * QT) - (k_index + first_row)
@@ -833,7 +849,7 @@
     lax.fori_loop(0, 3 * D // QUAD, step, 0)
 
 
-def forward_attention(tab_ref, rank, qkv_ref, att_ref, lse_ref):
+def forward_attention(tab_ref, rank, qkv_ref, att_ref, lse_ref, begin, end):
     def step(tile, carry):
         first = window_start(tile)
         bias, side_bias = tile_bias(tab_ref, rank, tile, first, 1)
@@ -869,19 +885,20 @@
         lse_ref[tile] = jnp.transpose(lse)[:16]
         return carry
 
-    lax.fori_loop(0, TILES, step, 0)
+    lax.fori_loop(begin, end, step, 0)
 
 
 def feed_forward(tab_ref, rank, x_ref, cot_ref, att_ref, gains, w_ref, wb_ref,
                  y_ref, gh_ref, ga_ref, dg_ref, du_ref, db_ref, do_ref,
                  h1_ref, nt_ref, ntt_ref, gres_ref, h2_ref, gg_ref, gu_ref, gn_ref):
     hidden = wb_ref.shape[0]
-    gate_at = 4 * D
+    gate_at = w_ref.shape[1] - 2 * hidden
+    out_at = gate_at - D
     valid = valid_column(tab_ref, rank)
     gain = gains[2:3]
     for tile in range(TILES):
         rows = pl.ds(tile * QT, QT)
-        value = x_ref[rows, :].astype(F32) + mm(att_ref[rows, :], w_ref[:, 3 * D : 4 * D])
+        value = x_ref[rows, :].astype(F32) + mm(att_ref[rows, :], w_ref[:, out_at:gate_at])
         h1_ref[rows, :] = value
         normed = (value * lax.rsqrt(mean_square(value) + EPSILON) * gain).astype(BF16)
         nt_ref[rows, :] = normed
@@ -941,7 +958,7 @@
         gh_ref[rows, :] = grad
         low = grad.astype(BF16)
         nt_ref[rows, :] = low
-        ga_ref[rows, :] = mm_cols(low, w_ref[:, 3 * D : 4 * D]).astype(BF16)
+        ga_ref[rows, :] = mm_cols(low, w_ref[:, out_at:gate_at]).astype(BF16)
 
     def out_weight(tile, carry):
         cols = pl.ds(pl.multiple_of(tile * QUAD, QUAD), QUAD)
@@ -1068,7 +1085,7 @@
     gains = gains_of(gc_ref)
     forward_norm(tab_ref, rank, x_ref, gains, n_ref)
     forward_project(n_ref, w_ref, qkv_ref)
-    forward_attention(tab_ref, rank, qkv_ref, att_ref, lse_ref)
+    forward_attention(tab_ref, rank, qkv_ref, att_ref, lse_ref, 0, TILES)
 
 
 def second_kernel(tab_ref, x_ref, cot_ref, att_ref, gc_ref, w_ref, wb_ref,
@@ -1091,21 +1108,24 @@
     spread_gain_grads(grads, dc_ref)
 
 
-def forward_layer(tab, x, cot, gc, w, wb):
-    hidden = wb.shape[0]
+def attend(tab, x, gc, w):
     shape = jax.ShapeDtypeStruct
-    params = pltpu.CompilerParams(vmem_limit_bytes=VMEM_LIMIT)
-    n, qkv, att, lse = pl.pallas_call(
+    return pl.pallas_call(
         first_kernel,
         out_shape=(shape((ALL_ROWS, D), BF16), shape((ALL_ROWS, 3 * D), BF16), shape((ROWS, D), BF16),
                    shape((TILES, 16, QT), F32)),
         in_specs=[SMEM, VMEM, VMEM, pl.BlockSpec((D, 3 * D), lambda step: (0, 0))],
         grid=(1,),
         out_specs=(VMEM,) * 4,
-        compiler_params=params,
+        compiler_params=pltpu.CompilerParams(vmem_limit_bytes=VMEM_LIMIT),
         name="attend",
     )(tab, x, gc, w)
-    outs = pl.pallas_call(
+
+
+def feed(tab, x, cot, att, gc, w, wb):
+    hidden = wb.shape[0]
+    shape = jax.ShapeDtypeStruct
+    return pl.pallas_call(
         second_kernel,
         out_shape=(shape((ROWS, D), BF16), shape((ROWS, D), F32), shape((ROWS, D), BF16),
                    shape((D, hidden), BF16), shape((D, hidden), BF16), shape((hidden, D), BF16), shape((D, D), BF16),
@@ -1116,10 +1136,9 @@
                         pltpu.VMEM((ROWS, D), BF16), pltpu.VMEM((ROWS, hidden), BF16),
                         pltpu.VMEM((ROWS, hidden), BF16), pltpu.VMEM((ROWS, hidden), BF16),
                         pltpu.VMEM((ROWS, D), F32)],
-        compiler_params=params,
+        compiler_params=pltpu.CompilerParams(vmem_limit_bytes=VMEM_LIMIT),
         name="feed_forward",
     )(tab, x, cot, att, gc, w, wb)
-    return (n, qkv, att, lse) + outs
 
 
 def backward_layer(tab, x, gh, ga, att, lse, n, qkv, gain, gc, w):
@@ -1146,7 +1165,7 @@
         self.mate, self.across = core_of(self.rank), across_of(self.rank)
         self.late = []
 
-    def greet(self):
+    def greet(self, everyone=False):
         barrier = pltpu.get_barrier_semaphore()
         neighbours = (
             (self.row + 1 < self.outer, {"fsdp": self.spot + self.inner}),
@@ -1154,7 +1173,8 @@
             (self.col + 1 < self.inner, {"fsdp": self.spot + 1}),
             (self.col > 0, {"fsdp": self.spot - 1}),
         )
-        amount = jnp.int32(2)
+        group = (self.mate, self.across) + ((across_of(self.mate),) if everyone else ())
+        amount = jnp.int32(len(group))
         for there, device in neighbours:
             amount = amount + there.astype(jnp.int32)
 
@@ -1162,7 +1182,7 @@
             def _():
                 pl.semaphore_signal(barrier, inc=1, device_id=device, device_id_type=MESH)
 
-        for device in (self.mate, self.across):
+        for device in group:
             pl.semaphore_signal(barrier, inc=1, device_id={"rep": device}, device_id_type=MESH)
         pl.semaphore_wait(barrier, amount)
 
@@ -1439,28 +1459,385 @@
     return outs[:kinds], outs[kinds], outs[kinds + 1]
 
 
+TABLE_ROWS = 56
+
+
+def packed_table(lens, tabv_ref):
+    lane = iota((8, 128), 1)
+    blocks = lax.div(lens + (BLK - 1), BLK)
+    key = jnp.where(blocks > 0, blocks * 128 + (127 - lane), 0)
+    wide = jnp.broadcast_to(key[:1], (128, 128))
+    other = jnp.sum(jnp.where(iota((128, 128), 0) == iota((128, 128), 1), wide, 0), axis=1, keepdims=True)
+    order = jnp.sum(jnp.where(other > wide, 1, 0), axis=0, keepdims=True)
+    order = jnp.broadcast_to(order, (8, 128))
+    edges, below = [], jnp.zeros((8, 1), jnp.int32)
+    for size in range(MAX_SEQ_BLOCKS, 0, -1):
+        below = below + jnp.sum(jnp.where(blocks == size, 1, 0), axis=1, keepdims=True)
+        edges.append(jnp.broadcast_to(below, (8, 128)))
+
+    def assign(number, carry):
+        loads, slot, first = carry[:4], carry[4], carry[5]
+        size = jnp.zeros((8, 128), jnp.int32)
+        for step, edge in enumerate(edges):
+            size = size + jnp.where(number < edge, 1, 0)
+        low = jnp.minimum(jnp.minimum(loads[0], loads[1]), jnp.minimum(loads[2], loads[3]))
+        best = jnp.full((8, 128), 3, jnp.int32)
+        for dev in (2, 1, 0):
+            best = jnp.where(loads[dev] == low, dev, best)
+        mine = order == number
+        slot = jnp.where(mine, best * SLOTS + low, slot)
+        first = jnp.where(mine, low, first)
+        loads = tuple(loads[dev] + jnp.where(best == dev, size, 0) for dev in range(4))
+        return loads + (slot, first)
+
+    zero = jnp.zeros((8, 128), jnp.int32)
+    carry = lax.fori_loop(0, 32, assign, (zero,) * 6)
+    slot, first = carry[4], carry[5]
+    where, tokens, segment = zero - 1, zero, zero
+    for step in range(MAX_SEQ_BLOCKS):
+        def shifted(value):
+            return value if step == 0 else pltpu.roll(value, step, 1)
+
+        covers = shifted(blocks) > step
+        where = jnp.where(covers, shifted(slot) + step, where)
+        tokens = jnp.where(covers, jnp.minimum(shifted(lens) - BLK * step, BLK), tokens)
+        segment = jnp.where(covers, shifted(first) + 1, segment)
+    packed = jnp.where(where >= 0, (lane + 1) + 128 * tokens + 16384 * segment, 0)
+    spots = jnp.broadcast_to(where[:1], (48, 128))
+    values = jnp.broadcast_to(packed[:1], (48, 128))
+    column = jnp.sum(jnp.where(spots == iota((48, 128), 0), values, 0), axis=1, keepdims=True)
+    tabv_ref[:48] = jnp.broadcast_to(column, (48, 128))
+    tabv_ref[48:] = where
+
+
+def front_kernel(outer, inner, *refs):
+    (lens_ref, rows_ref, cots_ref, *weights), refs = refs[:9], refs[9:]
+    (wd_ref, wc_ref), refs = refs[:2], refs[2:]
+    (tab_ref, x_ref, cot_ref, n_ref, qkv_ref, att_ref, lse_ref, wqkv_ref, gc_ref, ga_ref, gb_ref), refs = refs[:11], refs[11:]
+    (stage, lens_all, tabs, psend, precv, xsend, xrecv), refs = refs[:7], refs[7:]
+    (l_send, l_recv, t_sem, w_sem, z_send, z_recv, y_send, y_recv, c_send, c_recv, d_send, d_recv, own_sem,
+     p_send, p_recv, x_send, x_recv, spare) = refs
+    links = Links(outer, inner)
+    rank, spot, core, mate, across = links.rank, links.spot, links.core, links.mate, links.across
+    row, col = links.row, links.col
+    side = rank // 2
+    count = outer * inner
+    part = stage.shape[0]
+    per_rank = rows_ref.shape[0]
+    width = 3 * D
+    tall = wd_ref.shape[0]
+    hidden = weights[-1].shape[1]
+    gate_half, up_half = (D + hidden) // 2, hidden // 2
+
+    at = 0
+    loads = []
+    for number, ref in enumerate(weights):
+        cols = slice(at, at + ref.shape[1])
+        loads.append(pltpu.make_async_copy(ref, stage.at[:, cols], w_sem.at[number]))
+        loads[-1].start()
+        at += ref.shape[1]
+
+    links.greet(True)
+    lens_all[rank] = lens_ref[...]
+    for step in range(1, 4):
+        links.send(None, lens_ref, lens_all.at[rank], l_send.at[step - 1], l_recv.at[step - 1],
+                   {"rep": (rank + step) % 4})
+
+    def cols_of(start, half, which):
+        return pl.ds(pl.multiple_of(start + which * half, 128), half)
+
+    down_half = D // 2
+
+    def tall_rows(which):
+        return pl.ds(pl.multiple_of(which * (tall // 2), 16), tall // 2)
+
+    def source(number):
+        return (
+            lambda: stage.at[:, cols_of(0, width // 2, core)],
+            lambda: stage.at[:, cols_of(width, gate_half, core)],
+            lambda: stage.at[:, cols_of(width + 2 * gate_half, up_half, core)],
+            lambda: wd_ref.at[tall_rows(side), cols_of(0, down_half, core)],
+            lambda: wc_ref,
+        )[number]()
+
+    def place(number, shard, which=None):
+        which = core if which is None else which
+        return (
+            lambda: wqkv_ref.at[pl.ds(pl.multiple_of(shard * part, 16), part), cols_of(0, width // 2, which)],
+            lambda: ga_ref.at[shard, :, cols_of(0, gate_half, which)],
+            lambda: ga_ref.at[shard, :, cols_of(2 * gate_half, up_half, which)],
+            lambda: gb_ref.at[shard, tall_rows(side), cols_of(0, down_half, which)],
+            lambda: gc_ref.at[shard],
+            lambda: gb_ref.at[shard, tall_rows(1 - side), cols_of(0, down_half, which)],
+        )[number]()
+
+    nobody = spare.at[0]
+
+    def both(first, second):
+        return second if first is None else jnp.logical_and(first, second)
+
+    def guarded(there, action):
+        if there is None:
+            action()
+        else:
+            pl.when(there)(action)
+
+    def share(there, number, shard):
+        if number == 4:
+            return
+        here = place(number, shard)
+        links.send(there, here, here, c_send.at[number, shard], c_recv.at[number, shard], {"rep": mate})
+        if number == 3:
+            links.send(there, here, here, d_send.at[shard], d_recv.at[shard], {"rep": across})
+
+    other_column = {"fsdp": spot + 1 - 2 * col}
+
+    def along_row(there, number, line, src):
+        here = place(number, line * inner + col)
+        links.send(there, here if src is None else src, here, y_send.at[line, number], y_recv.at[line, number],
+                   other_column)
+
+    def lines(step):
+        return ((row - 1 - step >= 0, row - 1 - step, 0, row + 1 < outer, spot + inner),
+                (row + 1 + step < outer, row + 1 + step, 1, row > 0, spot - inner))
+
+    def own(number):
+        src, dst = source(number), place(number, spot)
+        links.send(row + 1 < outer, src, dst, z_send.at[0, 0, number], z_recv.at[0, 0, number],
+                   {"fsdp": spot + inner})
+        links.send(row > 0, src, dst, z_send.at[1, 0, number], z_recv.at[1, 0, number], {"fsdp": spot - inner})
+        along_row(None, number, row, src)
+
+    def hop(number, step):
+        for here, line, way, onward, target in lines(step):
+            shard = line * inner + col
+            guarded(here, lambda: links.arrive(place(number, shard), z_recv.at[way, step, number], nobody))
+            if step + 1 < outer - 1:
+                view = place(number, shard)
+                links.send(both(here, onward), view, view, z_send.at[way, step + 1, number],
+                           z_recv.at[way, step + 1, number], {"fsdp": target})
+            along_row(here, number, line, None)
+            share(here, number, shard)
+
+    def from_row(number):
+        def one(there, line):
+            shard = line * inner + 1 - col
+            guarded(there, lambda: links.arrive(place(number, shard), y_recv.at[line, number], nobody))
+            share(there, number, shard)
+
+        one(None, row)
+        for step in range(outer - 1):
+            for here, line, *_ in lines(step):
+                one(here, line)
+
+    def gathered(*numbers):
+        for shard in range(count):
+            @pl.when(shard != spot)
+            def _():
+                for number in numbers:
+                    links.arrive(place(number, shard, 1 - core), c_recv.at[number, shard], nobody)
+
+    def from_across():
+        for shard in range(count):
+            there = shard != spot
+            guarded(there, lambda: links.arrive(place(5, shard), d_recv.at[shard], nobody))
+            here = place(5, shard)
+            links.send(there, here, here, c_send.at[5, shard], c_recv.at[5, shard], {"rep": mate})
+
+    for load in loads:
+        load.wait()
+    own(0)
+    own(4)
+    own(1)
+    keep = [
+        pltpu.make_async_copy(stage.at[:, :width], wqkv_ref.at[pl.ds(pl.multiple_of(spot * part, 16), part)], own_sem.at[0]),
+        pltpu.make_async_copy(stage.at[:, width:], ga_ref.at[spot], own_sem.at[1]),
+        pltpu.make_async_copy(wd_ref, gb_ref.at[spot], own_sem.at[2]),
+        pltpu.make_async_copy(wc_ref, gc_ref.at[spot], own_sem.at[3]),
+    ]
+    for copy in keep:
+        copy.start()
+
+    for step in range(1, 4):
+        links.arrive(lens_all.at[(rank + 4 - step) % 4], l_recv.at[step - 1], nobody)
+    lens = lens_all[0] + lens_all[1] + lens_all[2] + lens_all[3]
+    packed_table(jnp.broadcast_to(lens[:1], (8, 128)), tab_ref)
+    to_scalar = pltpu.make_async_copy(tab_ref, tabs, t_sem.at[0])
+    to_scalar.start()
+    to_scalar.wait()
+
+    sources = (rows_ref, cots_ref)
+    outs = (x_ref, cot_ref)
+
+    def picked(kind, target, slot):
+        index = block_at(tabs, target * SLOTS + slot) - rank * per_rank
+        mine = jnp.logical_and(index >= 0, index < per_rank)
+        return mine, sources[kind][jnp.clip(index, 0, per_rank - 1)]
+
+    def mate_copy(kind, piece):
+        return pltpu.make_async_remote_copy(
+            src_ref=psend.at[kind, piece], dst_ref=precv.at[kind, piece],
+            send_sem=p_send.at[kind, piece], recv_sem=p_recv.at[kind, piece],
+            device_id={"rep": mate}, device_id_type=MESH,
+        )
+
+    def across_copy(kind):
+        return pltpu.make_async_remote_copy(
+            src_ref=xsend.at[kind], dst_ref=xrecv.at[kind],
+            send_sem=x_send.at[kind], recv_sem=x_recv.at[kind],
+            device_id={"rep": across}, device_id_type=MESH,
+        )
+
+    def pack_rows(kind, piece):
+        target = mate if piece == 0 else across_of(mate)
+
+        def pack(slot, carry):
+            mine, value = picked(kind, target, slot)
+            psend[kind, piece, slot] = jnp.where(mine, value, jnp.zeros_like(value))
+            return carry
+
+        lax.fori_loop(0, SLOTS, pack, 0)
+        mate_copy(kind, piece).start()
+
+    def cross_rows(kind):
+        mate_copy(kind, 1).wait_recv()
+
+        def merge(slot, carry):
+            mine, value = picked(kind, across, slot)
+            xsend[kind, slot] = jnp.where(mine, value, precv[kind, 1, slot])
+            return carry
+
+        lax.fori_loop(0, SLOTS, merge, 0)
+        across_copy(kind).start()
+
+    def finish_rows(kind):
+        mate_copy(kind, 0).wait_recv()
+        across_copy(kind).wait_recv()
+
+        def finish(slot, carry):
+            mine, value = picked(kind, rank, slot)
+            rows = pl.ds(pl.multiple_of(slot * BLK, BLK), BLK)
+            outs[kind][rows, :] = jnp.where(mine, value, precv[kind, 0, slot] + xrecv[kind, slot])
+            return carry
+
+        lax.fori_loop(0, SLOTS, finish, 0)
+
+    pack_rows(0, 1)
+    pack_rows(1, 1)
+    cross_rows(0)
+    pack_rows(0, 0)
+    cross_rows(1)
+    pack_rows(1, 0)
+    for step in range(outer - 1):
+        hop(0, step)
+    for step in range(outer - 1):
+        hop(4, step)
+    hop(1, 0)
+    own(2)
+    from_row(0)
+    from_row(4)
+    for step in range(1, outer - 1):
+        hop(1, step)
+    keep[3].wait()
+    gains = gains_of(gc_ref)
+    finish_rows(0)
+    forward_norm(tabs, rank, x_ref, gains, n_ref)
+    hop(2, 0)
+    own(3)
+    keep[0].wait()
+    gathered(0)
+    forward_project(n_ref, wqkv_ref, qkv_ref)
+    hop(2, 1)
+    forward_attention(tabs, rank, qkv_ref, att_ref, lse_ref, 0, 2)
+    from_row(1)
+    for step in range(2, outer - 1):
+        hop(2, step)
+    hop(3, 0)
+    forward_attention(tabs, rank, qkv_ref, att_ref, lse_ref, 2, 4)
+    from_row(2)
+    for step in range(1, outer - 1):
+        hop(3, step)
+    forward_attention(tabs, rank, qkv_ref, att_ref, lse_ref, 4, TILES)
+    from_row(3)
+    finish_rows(1)
+    from_across()
+    gathered(1, 2, 3, 5)
+    links.drain()
+    for kind in range(2):
+        for piece in range(2):
+            mate_copy(kind, piece).wait_send()
+        across_copy(kind).wait_send()
+    for copy in keep[1:3]:
+        copy.wait()
+
+
+def gather_and_attend(count, lens, rows, cots, weights, wd, wc):
+    outer, inner = grid_of(count)
+    block = rows.shape[1:]
+    part, hidden = wd.shape[0], weights[-1].shape[1]
+    part = weights[0].shape[0]
+    dma, shape = pltpu.SemaphoreType.DMA, jax.ShapeDtypeStruct
+    total = sum(weight.shape[1] for weight in weights)
+    kinds = 5
+    return pl.pallas_call(
+        partial(front_kernel, outer, inner),
+        out_shape=(
+            shape((TABLE_ROWS, 128), jnp.int32), shape((ROWS, D), BF16), shape((ROWS, D), BF16),
+            shape((ALL_ROWS, D), BF16), shape((ALL_ROWS, 3 * D), BF16), shape((ROWS, D), BF16),
+            shape((TILES, 16, QT), F32), shape((D, 3 * D), BF16), shape((count,) + wc.shape, BF16),
+            shape((count, part, total - 3 * D), BF16), shape((count,) + wd.shape, BF16),
+        ),
+        in_specs=[VMEM] * 3 + [ANY] * 6 + [VMEM] * 2,
+        out_specs=(VMEM,) * 9 + (ANY,) * 2,
+        scratch_shapes=[
+            pltpu.VMEM((part, total), BF16), pltpu.VMEM((4, 8, 128), jnp.int32), pltpu.SMEM((TABLE_ROWS, 128), jnp.int32),
+            pltpu.VMEM((2, 2, SLOTS) + block, BF16), pltpu.VMEM((2, 2, SLOTS) + block, BF16),
+            pltpu.VMEM((2, SLOTS) + block, BF16), pltpu.VMEM((2, SLOTS) + block, BF16),
+            dma((3,)), dma((3,)), dma((1,)), dma((6,)),
+            dma((2, outer - 1, kinds)), dma((2, outer - 1, kinds)), dma((outer, kinds)), dma((outer, kinds)),
+            dma((kinds + 1, count)), dma((kinds + 1, count)), dma((count,)), dma((count,)), dma((4,)),
+            dma((2, 2)), dma((2, 2)), dma((2,)), dma((2,)), dma((1,)),
+        ],
+        compiler_params=pltpu.CompilerParams(
+            collective_id=1, has_side_effects=True, vmem_limit_bytes=VMEM_LIMIT
+        ),
+        name="gather_and_attend",
+    )(lens, rows, cots, *weights, wd, wc)
+
+
 def per_device(count, layer_input, cotangent, lengths, attn_gain, global_gain, query_weight, key_weight,
                value_weight, out_weight, ffn_gain, gate_weight, up_weight, down_weight):
     micro, span, width = layer_input.shape
     hidden = gate_weight.shape[1]
     blocks = micro * span // BLK
-    table = deal_table(lengths)
-    wa = jnp.concatenate([query_weight, key_weight, value_weight, out_weight, gate_weight, up_weight], axis=1)
     part = attn_gain.shape[0]
+    rows_in = layer_input.reshape(blocks, BLK, width)
+    cots_in = cotangent.reshape(blocks, BLK, width)
+    weights = (query_weight, key_weight, value_weight, out_weight, gate_weight, up_weight)
     wc = jnp.pad(jnp.stack([attn_gain, global_gain, ffn_gain]), ((0, 13), (0, 128 - part)))
-    splits = ((0, 4 * width), (4 * width, 2 * hidden))
-    ga, gb, gc, rows, cots = gather_weights(
-        count, splits, table,
-        layer_input.reshape(blocks, BLK, width), cotangent.reshape(blocks, BLK, width), wa, down_weight, wc,
-    )
-    x, full = rows.reshape(ROWS, width), ga.reshape(width, -1)
-    n, qkv, att, lse, y, gh, gatt, dg, du, db, do, gain = forward_layer(
-        table, x, cots.reshape(ROWS, width), gc, full, gb.reshape(-1, width)
-    )
     if grid_of(count)[1] == 2 and part % 16 == 0:
-        totals, ry, rg = attend_back(count, table, x, gh, gatt, att, lse, n, qkv, gain, gc, full, (dg, du, db, do), y)
+        lens = lax.dynamic_update_slice(
+            jnp.zeros((8, 128), jnp.int32), lengths.reshape(1, blocks), (0, lax.axis_index("rep") * blocks)
+        )
+        table, x, cot, n, qkv, att, lse, wqkv, gc, ga, gb = gather_and_attend(
+            count, lens, rows_in, cots_in, weights, down_weight, wc
+        )
+        y, gh, gatt, dg, du, db, do, gain = feed(
+            table, x, cot, att, gc, ga.reshape(width, -1), gb.reshape(-1, width)
+        )
+        totals, ry, rg = attend_back(count, table, x, gh, gatt, att, lse, n, qkv, gain, gc, wqkv, (dg, du, db, do), y)
         og, ou, ob, oo, oq, ok, ov, oc = totals
     else:
+        table = deal_table(lengths)
+        splits = ((0, 4 * width), (4 * width, 2 * hidden))
+        ga, gb, gc, rows, cots = gather_weights(
+            count, splits, table, rows_in, cots_in, jnp.concatenate(weights, axis=1), down_weight, wc
+        )
+        x, full = rows.reshape(ROWS, width), ga.reshape(width, -1)
+        n, qkv, att, lse = attend(table, x, gc, full)
+        y, gh, gatt, dg, du, db, do, gain = feed(
+            table, x, cots.reshape(ROWS, width), att, gc, full, gb.reshape(-1, width)
+        )
         g, dw, dc = backward_layer(table, x, gh, gatt, att, lse, n, qkv, gain, gc, full)
         grads = [grad.reshape(count, -1, grad.shape[-1]) for grad in (dg, du, db, do, dw, dc)]
         og, ou, ob, oo, ow, oc, ry, rg = reduce_grads(

time: 301 us -> 262 us (0.87)
  Pallas kernels: 286 us -> 251 us
  local copies, waits for them, and re-layouts: 13 us -> 8.29 us
    pallas_call x5 -> x2, Pallas kernels: 168 us -> 133 us  [the longest x1 95.1 us: gather_and_attend(): pl.pallas_call(partial(front_kernel, outer, inner), out_shape=(shape((TAB...]
    unnamed x32 -> x23, local copies, waits for them, and re-layouts: 10.3 us -> 6.11 us
where the time goes in v5:
time: 262 us; the launch traced here: 261 us
  Pallas kernels  251 us (96%)
  local copies, waits for them, and re-layouts  8.29 us (3%)
    pallas_call x1, Pallas kernels, attend_back(): pl.pallas_call(partial(back_kernel, outer, inner, early), out_shape=tuple...  111 us
    pallas_call x1, Pallas kernels, gather_and_attend(): pl.pallas_call(partial(front_kernel, outer, inner), out_shape=(shape((TAB...  95.1 us
    pallas_call x1, Pallas kernels, feed(): pl.pallas_call(second_kernel, out_shape=(shape((ROWS, D), BF16), shape((R...  38.1 us
    pallas_call x1, Pallas kernels, bring_home(): pl.pallas_call(home_kernel, out_shape=(shape, shape), in_specs=[SMEM, VME...  6.72 us
    unnamed x23, local copies, waits for them, and re-layouts  6.11 us

profile of v5, /device:TPU:0, one launch (start us, length us, event | category | flops | bytes accessed | tf_op | source)
XLA Modules:
  0.0 261.4 jit_solution(8193134104155907915)
XLA Ops:
  0.6 0.8 reshape.60
  1.4 1.3 fusion.8.refs_10_
  2.7 0.1 dynamic_update_slice.3.refs_0_
  2.8 0.0 copy-start.7
  2.8 0.6 copy-done.7
  3.4 95.1 %gather_and_attend.1 = (s32[56,128]{1,0:T(8,128)}, bf16[640,768]{1,0:T(8,128)(2,1)}, bf16[640,768]{1,0:T(8,128)(2,1)}, bf16[688,768]{1,0:T(8,128)(2,1)}, bf16[68...) custom-call(s32[8,128]{1,0:T(8,128)} %copy-done.7, ...), custom_call_target="tpu_custom_call" | custom-call | tf_op jit(solution)/shard_map/gather_and_attend/pallas_call | solution.py:1782
  98.5 38.1 %feed_forward.1 = (bf16[640,768]{1,0:T(8,128)(2,1)}, f32[640,768]{1,0:T(8,128)}, bf16[640,768]{1,0:T(8,128)(2,1)}, bf16[768,2048]{1,0:T(8,128)(2,1)}, bf16[768,2...) custom-call(s32[56,128]{1,0:T(8,128)} %get-tuple-element.43.tab_ref.refs_0_, ...), custom_call_target="tpu_custom_call" | custom-call | tf_op jit(solution)/shard_map/feed_forward/pallas_call | solution.py:1128
  136.6 111.2 %attend_back_and_reduce.1 = (f32[96,2048]{1,0:T(8,128)}, f32[96,2048]{1,0:T(8,128)}, f32[256,768]{1,0:T(8,128)}, f32[96,768]{1,0:T(8,128)}, f32[96,768]{1,0:T(8,...) custom-call(s32[56,128]{1,0:T(8,128)} %get-tuple-element.43.tab_ref., ...), custom_call_target="tpu_custom_call" | custom-call | tf_op jit(solution)/shard_map/attend_back_and_reduce/pallas_call | solution.py:1447
  247.8 0.0 copy-start.6
  247.8 0.0 copy-start.5
  247.8 0.0 copy-start.4
  247.9 0.0 copy-start.3
  247.9 0.0 copy-start.2
  247.9 6.7 %place_rows.1 = (bf16[24,64,768]{2,1,0:T(8,128)(2,1)}, bf16[24,64,768]{2,1,0:T(8,128)(2,1)}) custom-call(s32[56,128]{1,0:T(8,128)} %get-tuple-element.43.tab_ref.refs_0_, bf16[4,10,64,768]{3,2,1,0:T(8,128)(2,1)} %get-tuple-element.62.ry_ref, bf16[4,10,64,768]{3,2,1,0:T(8,128)(2,1)} %get-tuple-element.63.rg_ref), custom_call_target="tpu_custom_call" | custom-call | tf_op jit(solution)/shard_map/place_rows/pallas_call | solution.py:669
  254.6 0.0 copy-start.1
  254.6 0.0 copy-start
  254.6 1.3 slice_bitcast_fusion
  255.9 0.0 copy-done.6
  255.9 0.7 copy.33
  256.6 0.0 copy-done.5
  256.6 0.7 copy.34
  257.4 0.0 copy-done.4
  257.4 0.7 copy.35
  258.1 0.0 copy-done.3
  258.1 0.7 copy.36
  258.8 0.0 copy-done.2
  258.8 0.9 copy.37
  259.7 0.0 copy-done.1
  259.7 0.9 copy.38
  260.6 0.0 copy-done
  260.6 0.9 copy.39
  (1 shorter events, 0.0 us)
Async XLA Ops:
  2.8 0.6 copy-start.7
  247.8 8.1 %copy-start.6 = (f32[96,768]{1,0:T(8,128)S(1)}, f32[96,768]{1,0:T(8,128)}, u32[]{:S(2)}) copy-start(f32[96,768]{1,0:T(8,128)} %get-tuple-element.93) | copy-start | bytes 884740
  247.8 8.8 %copy-start.5 = (f32[96,768]{1,0:T(8,128)S(1)}, f32[96,768]{1,0:T(8,128)}, u32[]{:S(2)}) copy-start(f32[96,768]{1,0:T(8,128)} %get-tuple-element.94) | copy-start | bytes 884740
  247.8 9.5 %copy-start.4 = (f32[96,768]{1,0:T(8,128)S(1)}, f32[96,768]{1,0:T(8,128)}, u32[]{:S(2)}) copy-start(f32[96,768]{1,0:T(8,128)} %get-tuple-element.95) | copy-start | bytes 884740
  247.9 10.2 %copy-start.3 = (f32[96,768]{1,0:T(8,128)S(1)}, f32[96,768]{1,0:T(8,128)}, u32[]{:S(2)}) copy-start(f32[96,768]{1,0:T(8,128)} %get-tuple-element.96) | copy-start | bytes 884740
  247.9 10.9 %copy-start.2 = (f32[96,2048]{1,0:T(8,128)S(1)}, f32[96,2048]{1,0:T(8,128)}, u32[]{:S(2)}) copy-start(f32[96,2048]{1,0:T(8,128)} %get-tuple-element.98) | copy-start | bytes 2359300
  254.6 5.1 %copy-start.1 = (f32[96,2048]{1,0:T(8,128)S(1)}, f32[96,2048]{1,0:T(8,128)}, u32[]{:S(2)}) copy-start(f32[96,2048]{1,0:T(8,128)} %get-tuple-element.99) | copy-start | bytes 2359300
  254.6 6.0 %copy-start = (f32[256,768]{1,0:T(8,128)S(1)}, f32[256,768]{1,0:T(8,128)}, u32[]{:S(2)}) copy-start(f32[256,768]{1,0:T(8,128)} %get-tuple-element.100) | copy-start | bytes 2359300

commit v6 on v5

--- a/solution.py
+++ b/solution.py
@@ -1223,8 +1223,8 @@
 
 
 class Reduction:
-    def __init__(self, links, source, total, mine, crecv, yrecv, zrecv, xrecv, sems, number):
-        self.links, self.source, self.total, self.mine = links, source, total, mine
+    def __init__(self, links, source, total, mine, crecv, yrecv, zrecv, xrecv, stage, sems, number):
+        self.links, self.source, self.total, self.mine, self.stage = links, source, total, mine, stage
         self.crecv, self.yrecv, self.zrecv, self.xrecv = crecv, yrecv, zrecv, xrecv
         self.sems, self.number = sems, number
         self.whole = total.shape[-1] % 256 != 0
@@ -1318,15 +1318,15 @@
     def finish(self):
         links = self.links
         links.arrive(self.xrecv, self.sem("x_recv"), self.sems["spare"].at[0])
-        value = self.mine[links.row, links.col].astype(F32) + self.xrecv[...].astype(F32)
-        if self.whole:
-            self.total[...] = value
-            return
-        place = halves(self.total, links.core)
-        place[...] = value
-        links.send(None, place, place, self.sem("f_send"), self.sem("f_recv"), {"rep": links.mate})
+        self.stage[...] = self.mine[links.row, links.col].astype(F32) + self.xrecv[...].astype(F32)
+        place = self.total if self.whole else halves(self.total, links.core)
+        self.keep = pltpu.make_async_copy(self.stage, place, self.sem("m_sem"))
+        self.keep.start()
+        if not self.whole:
+            links.send(None, self.stage, place, self.sem("f_send"), self.sem("f_recv"), {"rep": links.mate})
 
     def settle(self):
+        self.keep.wait()
         if not self.whole:
             self.links.arrive(
                 halves(self.total, 1 - self.links.core), self.sem("f_recv"), self.sems["spare"].at[0]
@@ -1362,101 +1362,6 @@
         links.arrive(self.home.at[links.mate], sem.at[self.kind, 1], self.sems["spare"].at[0])
         links.arrive(self.home.at[across_of(links.mate)], sem.at[self.kind, 2], self.sems["spare"].at[0])
         self.copy.wait()
-
-
-def back_kernel(outer, inner, early, *refs):
-    (tab_ref, x_ref, gh_ref, ga_ref, att_ref, lse_ref, n_ref, qkv_ref, gain_ref, gc_ref, w_ref), refs = refs[:11], refs[11:]
-    grads, (y_ref,), refs = refs[:early], refs[early : early + 1], refs[early + 1 :]
-    kinds = early + 4
-    totals, (ry_ref, rg_ref), refs = refs[:kinds], refs[kinds : kinds + 2], refs[kinds + 2 :]
-    (dq_ref, dkw_ref, dvw_ref, dc_ref), refs = refs[:4], refs[4:]
-    (g_ref, dqkv_ref, dk_ref, dv_ref), refs = refs[:4], refs[4:]
-    mines, refs = list(refs[:early]) + [None] * 3 + [refs[early]], refs[early + 1 :]
-    crecv, yrecv, zrecv, xrecv = (refs[kinds * i : kinds * (i + 1)] for i in range(4))
-    sems = dict(zip(SEM_NAMES, refs[4 * kinds :]))
-    links = Links(outer, inner)
-    rank = links.rank
-    sources = list(grads) + [dq_ref, dkw_ref, dvw_ref, dc_ref]
-    tasks = [
-        Reduction(links, sources[i], totals[i], mines[i], crecv[i], yrecv[i], zrecv[i], xrecv[i], sems, i)
-        for i in range(kinds)
-    ]
-    rows_y, rows_g = Return(links, y_ref, ry_ref, sems, 0), Return(links, g_ref, rg_ref, sems, 1)
-
-    links.greet()
-    for task in tasks[:early]:
-        task.begin()
-    rows_y.begin()
-    gains = gains_of(gc_ref)
-    for task in tasks[:early]:
-        task.pair()
-    backward_attention_start(dk_ref, dv_ref)
-    backward_attention_tiles(tab_ref, rank, qkv_ref, att_ref, ga_ref, lse_ref, dqkv_ref, dk_ref, dv_ref, 0, TILES)
-    tasks[0].column()
-    backward_attention_end(dqkv_ref, dk_ref, dv_ref)
-    weight_grads(n_ref, dqkv_ref, (dq_ref, dkw_ref, dvw_ref))
-    for task in tasks[early : early + 3]:
-        task.begin()
-    rows_y.relay()
-    one, side = backward_project(tab_ref, rank, x_ref, gh_ref, gains, n_ref, dqkv_ref, w_ref, dk_ref, g_ref)
-    spread_gain_grads(jnp.concatenate([one, side, gain_ref[...], jnp.zeros((5, D), F32)], axis=0), dc_ref)
-    rows_g.begin()
-    tasks[kinds - 1].begin()
-    for task in tasks[early:]:
-        task.pair()
-    for number in range(1, kinds + outer):
-        if number < kinds:
-            tasks[number].column()
-        if number == 2:
-            rows_g.relay()
-        for turn in range(1, outer):
-            if 0 <= number - turn < kinds:
-                tasks[number - turn].hop(turn)
-        if 0 <= number - outer + 1 < kinds:
-            tasks[number - outer + 1].cross()
-        if 0 <= number - outer < kinds:
-            tasks[number - outer].finish()
-    rows_y.settle()
-    rows_g.settle()
-    for task in tasks:
-        task.settle()
-    links.drain()
-
-
-def attend_back(count, table, x, gh, ga, att, lse, n, qkv, gain, gc, w, grads, y):
-    outer, inner = grid_of(count)
-    part = D // count
-    early = len(grads)
-    kinds = early + 4
-    grads = [grad.reshape((outer, inner, -1) + grad.shape[1:]) for grad in grads]
-    shapes = [grad.shape[2:] for grad in grads] + [(part, D)] * 3 + [(8, 128)]
-    dtypes = [BF16] * (kinds - 1) + [F32]
-    halved = [(a, b // 2 if b % 256 == 0 else b) for a, b in shapes]
-    dma = pltpu.SemaphoreType.DMA
-    scratch = [pltpu.VMEM((outer, inner) + shape, dtype) for shape, dtype in zip(shapes[early:], dtypes[early:])]
-    scratch += [pltpu.VMEM((SLOTS, BLK, D), BF16), pltpu.VMEM((ALL_ROWS, 3 * D), BF16),
-                pltpu.VMEM((ALL_ROWS, D), F32), pltpu.VMEM((ALL_ROWS, D), F32)]
-    scratch += [pltpu.VMEM((outer, inner) + shape, BF16) for shape in halved[:early]]
-    scratch += [pltpu.VMEM((outer, inner) + halved[-1], F32)]
-    for lead in ((outer, inner), (outer,), (outer + 1,), ()):
-        scratch += [pltpu.VMEM(lead + shape, dtype) for shape, dtype in zip(halved, dtypes)]
-    one = dma((kinds,))
-    scratch += [one, one, one, one, one, dma((2, outer, kinds)), dma((outer + 1, kinds)), one, one, one, one,
-                dma((2, 3)), dma((2, 3)), dma((2,)), dma((1,))]
-    rows = jax.ShapeDtypeStruct((4, SLOTS, BLK, D), BF16)
-    outs = pl.pallas_call(
-        partial(back_kernel, outer, inner, early),
-        out_shape=tuple(jax.ShapeDtypeStruct(shape, F32) for shape in shapes) + (rows, rows),
-        grid=(1,),
-        in_specs=[SMEM] + [VMEM] * 9 + [pl.BlockSpec((D, 3 * D), lambda step: (0, 0))] + [ANY] * early + [VMEM],
-        out_specs=(VMEM,) * kinds + (ANY, ANY),
-        scratch_shapes=scratch,
-        compiler_params=pltpu.CompilerParams(
-            collective_id=2, has_side_effects=True, vmem_limit_bytes=VMEM_LIMIT
-        ),
-        name="attend_back_and_reduce",
-    )(table, x, gh, ga, att, lse, n, qkv, gain, gc, w, *grads, y.reshape(SLOTS, BLK, D))
-    return outs[:kinds], outs[kinds], outs[kinds + 1]
 
 
 TABLE_ROWS = 56
@@ -1805,6 +1710,246 @@
     )(lens, rows, cots, *weights, wd, wc)
 
 
+def rear_kernel(outer, inner, *refs):
+    (tab_ref, x_ref, att_ref, lse_ref, gc_ref), refs = refs[:5], refs[5:]
+    (cot_any, n_any, qkv_any, wqkv_any, wf_any, wd_any), refs = refs[:6], refs[6:]
+    kinds = 8
+    totals, (ry_ref, rg_ref), refs = refs[:kinds], refs[kinds : kinds + 2], refs[kinds + 2 :]
+    (y_ref, gh_ref, fa_ref, dk_ref, b0_ref, b1_ref, b2_ref, n_ref, ntt_ref, gres_ref, ga_ref), refs = refs[:11], refs[11:]
+    (wf_ref, wd_ref, dg_ref, du_ref, db_ref, do_ref, dc_ref, mine_ref), refs = refs[:8], refs[8:]
+    (gate_recv, up_recv, down_recv, out_recv, gain_recv), refs = refs[:5], refs[5:]
+    narrow = D // 2
+    crecv = (gate_recv, up_recv, down_recv, out_recv, gate_recv.at[:, :, :, :narrow],
+             gate_recv.at[:, :, :, narrow : 2 * narrow], up_recv.at[:, :, :, :narrow], gain_recv)
+    yrecv, zrecv, xrecv, stages = (refs[kinds * i : kinds * (i + 1)] for i in range(4))
+    sems = dict(zip(SEM_NAMES, refs[4 * kinds :]))
+    load_sem, free_sem = refs[4 * kinds + len(SEM_NAMES) :]
+    links = Links(outer, inner)
+    rank = links.rank
+    hidden = wd_ref.shape[0]
+    part = wf_ref.shape[2]
+    group = 4 * part
+
+    def fetch(number, src, dst):
+        copy = pltpu.make_async_copy(src, dst, load_sem.at[number])
+        copy.start()
+        return copy
+
+    load_cot = fetch(0, cot_any, ga_ref)
+    load_out = fetch(1, wf_any.at[:, :, :, :D], wf_ref.at[:, :, :, :D])
+    load_in = fetch(2, wf_any.at[:, :, :, D:], wf_ref.at[:, :, :, D:])
+    load_down = fetch(3, wd_any, wd_ref)
+    links.greet()
+
+    def weight(start, size):
+        return wf_ref[:, :, :, pl.ds(start, size)].reshape(D, size)
+
+    grads = [dg_ref, du_ref, db_ref, do_ref] + [wf_ref.at[:, :, :, i * D : (i + 1) * D] for i in range(3)] + [dc_ref]
+    tasks = [
+        Reduction(links, grads[i], totals[i], mine_ref if i == kinds - 1 else None,
+                  crecv[i], yrecv[i], zrecv[i], xrecv[i], stages[i], sems, i)
+        for i in range(kinds)
+    ]
+    rows_y, rows_g = Return(links, y_ref, ry_ref, sems, 0), Return(links, gres_ref, rg_ref, sems, 1)
+
+    gains = gains_of(gc_ref)
+    gain = gains[2:3]
+    valid = valid_column(tab_ref, rank)
+    h1_ref = fa_ref
+    load_cot.wait()
+    load_out.wait()
+    for tile in range(TILES):
+        rows = pl.ds(tile * QT, QT)
+        value = x_ref[rows, :].astype(F32) + mm(att_ref[rows, :], weight(0, D))
+        h1_ref[rows, :] = value
+        normed = (value * lax.rsqrt(mean_square(value) + EPSILON) * gain).astype(BF16)
+        n_ref[rows, :] = normed
+        ntt_ref[:, tile * QT : (tile + 1) * QT] = jnp.transpose(normed)
+        gres_ref[rows, :] = (ga_ref[rows, :].astype(F32) * valid[tile * QT : (tile + 1) * QT]).astype(BF16)
+    load_in.wait()
+    load_down.wait()
+
+    def inward(tile, carry):
+        at = pl.multiple_of(tile * FF_TILE, FF_TILE)
+        cols = pl.ds(at, FF_TILE)
+        normed = n_ref[:ROWS, :]
+        gate = mm(normed, weight(D + at, FF_TILE))
+        up = mm(normed, weight(D + hidden + at, FF_TILE))
+        back = mm_cols(gres_ref[...], wd_ref[cols, :])
+        square = gate * gate
+        bend = jnp.tanh(GELU_C * (gate * (1.0 + GELU_A * square)))
+        half = 0.5 * (1.0 + bend)
+        act = gate * half
+        slope = half + (0.5 * GELU_C) * gate * (1.0 - bend * bend) * (1.0 + (3.0 * GELU_A) * square)
+        b0_ref[:ROWS, cols] = (act * up).astype(BF16)
+        b1_ref[:ROWS, cols] = (back * up * slope).astype(BF16)
+        b2_ref[:ROWS, cols] = (back * act).astype(BF16)
+        return carry
+
+    lax.fori_loop(0, hidden // FF_TILE, inward, 0)
+
+    def outer_products(ref, right_ref):
+        def step(tile, carry):
+            cols = pl.ds(pl.multiple_of(tile * FF_TILE, FF_TILE), FF_TILE)
+            value = mm(ntt_ref[...], right_ref[:ROWS, cols]).astype(BF16)
+            ref[:, :, :, cols] = value.reshape(outer, inner, part, FF_TILE)
+            return carry
+
+        lax.fori_loop(0, hidden // FF_TILE, step, 0)
+
+    outer_products(dg_ref, b1_ref)
+    tasks[0].begin()
+    outer_products(du_ref, b2_ref)
+    tasks[0].pair()
+    tasks[1].begin()
+
+    def down_products(tile, carry):
+        cols = pl.ds(pl.multiple_of(tile * FF_TILE, FF_TILE), FF_TILE)
+        db_ref[tile // inner, tile % inner] = mm_rows(b0_ref[:ROWS, cols], gres_ref[...]).astype(BF16)
+        return carry
+
+    lax.fori_loop(0, hidden // FF_TILE, down_products, 0)
+    tasks[1].pair()
+    pl.semaphore_signal(free_sem, inc=1, device_id={"rep": links.mate}, device_id_type=MESH)
+    tasks[2].begin()
+
+    def outward(tile, carry):
+        cols = pl.ds(pl.multiple_of(tile * group, 128), group)
+        value = h1_ref[:ROWS, cols] + mm(b0_ref[:ROWS, :hidden], wd_ref[:, cols])
+        y_ref[:, cols] = (value * valid).astype(BF16)
+        shards = pl.ds(tile * (4 // inner), 4 // inner)
+        gh_ref[:, cols] = mm_cols(
+            b1_ref[:ROWS, :hidden], wf_ref[shards, :, :, D : D + hidden].reshape(group, hidden)
+        ) + mm_cols(b2_ref[:ROWS, :hidden], wf_ref[shards, :, :, D + hidden :].reshape(group, hidden))
+        return carry
+
+    lax.fori_loop(0, D // group, outward, 0)
+    tasks[2].pair()
+    rows_y.begin()
+    load_qkv = fetch(4, qkv_any, b1_ref)
+    load_wqkv = fetch(5, wqkv_any, b2_ref)
+
+    gain_grad = jnp.zeros((1, D), F32)
+    for tile in range(TILES):
+        rows = pl.ds(tile * QT, QT)
+        value, grad = h1_ref[rows, :], gh_ref[rows, :]
+        root = lax.rsqrt(mean_square(value) + EPSILON)
+        unit = value * root
+        gain_grad = gain_grad + jnp.sum(grad * unit, axis=0, keepdims=True)
+        grad = grad * gain
+        grad = gres_ref[rows, :].astype(F32) + root * (
+            grad - unit * jnp.mean(grad * unit, axis=-1, keepdims=True)
+        )
+        gh_ref[rows, :] = grad
+        low = grad.astype(BF16)
+        n_ref[rows, :] = low
+        ga_ref[rows, :] = mm_cols(low, weight(0, D)).astype(BF16)
+
+    def out_products(tile, carry):
+        cols = pl.ds(pl.multiple_of(tile * QUAD, QUAD), QUAD)
+        value = mm_rows(att_ref[...], n_ref[:ROWS, cols]).astype(BF16)
+        do_ref[:, :, :, cols] = value.reshape(outer, inner, part, QUAD)
+        return carry
+
+    lax.fori_loop(0, D // QUAD, out_products, 0)
+    tasks[3].begin()
+    load_n = fetch(6, n_any, n_ref)
+    dv_ref = fa_ref
+    backward_attention_start(dk_ref, dv_ref)
+    load_qkv.wait()
+    tasks[3].pair()
+
+    def attention(begin, end):
+        backward_attention_tiles(tab_ref, rank, b1_ref, att_ref, ga_ref, lse_ref, b0_ref, dk_ref, dv_ref, begin, end)
+
+    def round_of(number):
+        if number < kinds:
+            tasks[number].column()
+        for turn in range(1, outer):
+            if 0 <= number - turn < kinds:
+                tasks[number - turn].hop(turn)
+        if 0 <= number - outer + 1 < kinds:
+            tasks[number - outer + 1].cross()
+        if 0 <= number - outer < kinds:
+            tasks[number - outer].finish()
+
+    attention(0, 3)
+    round_of(0)
+    attention(3, TILES)
+    backward_attention_end(b0_ref, dk_ref, dv_ref)
+    load_n.wait()
+    load_wqkv.wait()
+
+    def project_products(tile, carry):
+        cols = pl.ds(pl.multiple_of(tile * QUAD, QUAD), QUAD)
+        value = mm_rows(n_ref[...], b0_ref[:, cols]).astype(BF16)
+        wf_ref[:, :, :, cols] = value.reshape(outer, inner, part, QUAD)
+        return carry
+
+    lax.fori_loop(0, 3 * D // QUAD, project_products, 0)
+    pl.semaphore_wait(free_sem, 1)
+    for task in tasks[4:7]:
+        task.begin()
+    round_of(1)
+    rows_y.relay()
+    one, side = backward_project(tab_ref, rank, x_ref, gh_ref, gains, n_ref, b0_ref, b2_ref, dk_ref, gres_ref)
+    rows_g.begin()
+    for task in tasks[4:7]:
+        task.pair()
+    spread_gain_grads(jnp.concatenate([one, side, gain_grad, jnp.zeros((5, D), F32)], axis=0), dc_ref)
+    tasks[7].begin()
+    tasks[7].pair()
+    for number in range(2, kinds + outer):
+        round_of(number)
+        if number == 3:
+            rows_g.relay()
+    rows_y.settle()
+    rows_g.settle()
+    for task in tasks:
+        task.settle()
+    links.drain()
+
+
+def feed_and_reduce(count, table, x, att, lse, gc, cot, n, qkv, wqkv, wf, wd):
+    outer, inner = grid_of(count)
+    part, tall = D // count, wd.shape[1]
+    hidden = count * tall
+    wf = wf.reshape((outer, inner) + wf.shape[1:])
+    shapes = [(part, hidden), (part, hidden), (tall, D)] + [(part, D)] * 4 + [(8, 128)]
+    kinds = len(shapes)
+    dtypes = [BF16] * (kinds - 1) + [F32]
+    halved = [(a, b // 2 if b % 256 == 0 else b) for a, b in shapes]
+    dma, vmem = pltpu.SemaphoreType.DMA, pltpu.VMEM
+    scratch = [
+        vmem((ROWS, D), BF16), vmem((ROWS, D), F32), vmem((ALL_ROWS, D), F32), vmem((ALL_ROWS, D), F32),
+        vmem((ALL_ROWS, 3 * D), BF16), vmem((ALL_ROWS, 3 * D), BF16), vmem((D, 3 * D), BF16),
+        vmem((ALL_ROWS, D), BF16), vmem((D, ROWS), BF16), vmem((ROWS, D), BF16), vmem((ROWS, D), BF16),
+        vmem(wf.shape, BF16), vmem((hidden, D), BF16),
+    ]
+    scratch += [vmem((outer, inner) + shape, BF16) for shape in shapes[:4]]
+    scratch += [vmem((outer, inner) + shapes[-1], F32)] * 2
+    scratch += [vmem((outer, inner) + halved[i], dtypes[i]) for i in (0, 1, 2, 3, 7)]
+    for lead in ((outer,), (outer + 1,), ()):
+        scratch += [vmem(lead + shape, dtype) for shape, dtype in zip(halved, dtypes)]
+    scratch += [vmem(shape, F32) for shape in halved]
+    one = dma((kinds,))
+    scratch += [one, one, one, one, one, dma((2, outer, kinds)), dma((outer + 1, kinds)), one, one, one, one,
+                dma((2, 3)), dma((2, 3)), dma((2,)), dma((1,)), dma((7,)), pltpu.SemaphoreType.REGULAR]
+    rows = jax.ShapeDtypeStruct((4, ROWS, D), BF16)
+    outs = pl.pallas_call(
+        partial(rear_kernel, outer, inner),
+        out_shape=tuple(jax.ShapeDtypeStruct(shape, F32) for shape in shapes) + (rows, rows),
+        in_specs=[SMEM] + [VMEM] * 4 + [ANY] * 6,
+        out_specs=(ANY,) * (kinds + 2),
+        scratch_shapes=scratch,
+        compiler_params=pltpu.CompilerParams(
+            collective_id=2, has_side_effects=True, vmem_limit_bytes=67043328
+        ),
+        name="feed_and_reduce",
+    )(table, x, att, lse, gc, cot, n, qkv, wqkv, wf, wd.reshape(hidden, D))
+    return outs[:kinds], outs[kinds], outs[kinds + 1]
+
+
 def per_device(count, layer_input, cotangent, lengths, attn_gain, global_gain, query_weight, key_weight,
                value_weight, out_weight, ffn_gain, gate_weight, up_weight, down_weight):
     micro, span, width = layer_input.shape
@@ -1822,10 +1967,8 @@
         table, x, cot, n, qkv, att, lse, wqkv, gc, ga, gb = gather_and_attend(
             count, lens, rows_in, cots_in, weights, down_weight, wc
         )
-        y, gh, gatt, dg, du, db, do, gain = feed(
-            table, x, cot, att, gc, ga.reshape(width, -1), gb.reshape(-1, width)
-        )
-        totals, ry, rg = attend_back(count, table, x, gh, gatt, att, lse, n, qkv, gain, gc, wqkv, (dg, du, db, do), y)
+        totals, ry, rg = feed_and_reduce(count, table, x, att, lse, gc, cot, n, qkv, wqkv, ga, gb)
+        ry, rg = (rows.reshape(4, SLOTS, BLK, width) for rows in (ry, rg))
         og, ou, ob, oo, oq, ok, ov, oc = totals
     else:
         table = deal_table(lengths)

time: 262 us -> 232 us (0.89)
  Pallas kernels: 251 us -> 222 us
    pallas_call x2 -> x1, Pallas kernels: 149 us -> 120 us  [feed_and_reduce(): pl.pallas_call(partial(rear_kernel, outer, inner), out_shape=tuple((jax.S...]
where the time goes in v6:
time: 232 us
  Pallas kernels  222 us (96%)
  local copies, waits for them, and re-layouts  8.29 us (4%)
    pallas_call x1, Pallas kernels, feed_and_reduce(): pl.pallas_call(partial(rear_kernel, outer, inner), out_shape=tuple((jax.S...  120 us
    pallas_call x1, Pallas kernels, gather_and_attend(): pl.pallas_call(partial(front_kernel, outer, inner), out_shape=(shape((TAB...  95.1 us
    pallas_call x1, Pallas kernels, bring_home(): pl.pallas_call(home_kernel, out_shape=(shape, shape), in_specs=[SMEM, VME...  6.72 us
    unnamed x23, local copies, waits for them, and re-layouts  6.11 us

profile of v6, /device:TPU:0, one launch (start us, length us, event | category | flops | bytes accessed | tf_op | source)
XLA Modules:
  0.0 232.1 jit_solution(9708046692768955982)
XLA Ops:
  0.6 0.8 reshape.51
  1.4 1.3 fusion.8.refs_10_
  2.7 0.1 dynamic_update_slice.3.refs_0_
  2.8 0.0 copy-start.7
  2.8 0.6 copy-done.7
  3.4 95.1 %gather_and_attend.1 = (s32[56,128]{1,0:T(8,128)}, bf16[640,768]{1,0:T(8,128)(2,1)}, bf16[640,768]{1,0:T(8,128)(2,1)}, bf16[688,768]{1,0:T(8,128)(2,1)}, bf16[68...) custom-call(s32[8,128]{1,0:T(8,128)} %copy-done.7, ...), custom_call_target="tpu_custom_call" | custom-call | tf_op jit(solution)/shard_map/gather_and_attend/pallas_call | solution.py:1687
  98.5 120.0 %feed_and_reduce.1 = (f32[96,2048]{1,0:T(8,128)}, f32[96,2048]{1,0:T(8,128)}, f32[256,768]{1,0:T(8,128)}, f32[96,768]{1,0:T(8,128)}, f32[96,768]{1,0:T(8,128)}, ...) custom-call(s32[56,128]{1,0:T(8,128)} %get-tuple-element.35.refs_0_., ...), custom_call_target="tpu_custom_call" | custom-call | tf_op jit(solution)/shard_map/feed_and_reduce/pallas_call | solution.py:1939
  218.5 0.0 copy-start.6
  218.5 0.0 copy-start.5
  218.5 0.0 copy-start.4
  218.5 0.0 copy-start.3
  218.5 0.0 copy-start.2
  218.5 6.7 %place_rows.1 = (bf16[24,64,768]{2,1,0:T(8,128)(2,1)}, bf16[24,64,768]{2,1,0:T(8,128)(2,1)}) custom-call(s32[56,128]{1,0:T(8,128)} %get-tuple-element.35.refs_0_.tab_ref, bf16[4,10,64,768]{3,2,1,0:T(8,128)(2,1)} %bitcast.18, bf16[4,10,64,768]{3,2,1,0:T(8,128)(2,1)} %bitcast.19), custom_call_target="tpu_custom_call" | custom-call | tf_op jit(solution)/shard_map/place_rows/pallas_call | solution.py:669
  225.2 0.0 copy-start.1
  225.2 0.0 copy-start
  225.2 1.3 slice_bitcast_fusion
  226.6 0.0 copy-done.6
  226.6 0.7 copy.33
  227.3 0.0 copy-done.5
  227.3 0.7 copy.34
  228.0 0.0 copy-done.4
  228.0 0.7 copy.35
  228.7 0.0 copy-done.3
  228.7 0.7 copy.36
  229.4 0.0 copy-done.2
  229.5 0.9 copy.37
  230.3 0.0 copy-done.1
  230.3 0.9 copy.38
  231.2 0.0 copy-done
  231.2 0.9 copy.39
  (1 shorter events, 0.0 us)
Async XLA Ops:
  2.8 0.6 copy-start.7
  218.5 8.1 %copy-start.6 = (f32[96,768]{1,0:T(8,128)S(1)}, f32[96,768]{1,0:T(8,128)}, u32[]{:S(2)}) copy-start(f32[96,768]{1,0:T(8,128)} %get-tuple-element.77) | copy-start | bytes 884740
  218.5 8.8 %copy-start.5 = (f32[96,768]{1,0:T(8,128)S(1)}, f32[96,768]{1,0:T(8,128)}, u32[]{:S(2)}) copy-start(f32[96,768]{1,0:T(8,128)} %get-tuple-element.78) | copy-start | bytes 884740
  218.5 9.5 %copy-start.4 = (f32[96,768]{1,0:T(8,128)S(1)}, f32[96,768]{1,0:T(8,128)}, u32[]{:S(2)}) copy-start(f32[96,768]{1,0:T(8,128)} %get-tuple-element.79) | copy-start | bytes 884740
  218.5 10.2 %copy-start.3 = (f32[96,768]{1,0:T(8,128)S(1)}, f32[96,768]{1,0:T(8,128)}, u32[]{:S(2)}) copy-start(f32[96,768]{1,0:T(8,128)} %get-tuple-element.80) | copy-start | bytes 884740
  218.5 10.9 %copy-start.2 = (f32[96,2048]{1,0:T(8,128)S(1)}, f32[96,2048]{1,0:T(8,128)}, u32[]{:S(2)}) copy-start(f32[96,2048]{1,0:T(8,128)} %get-tuple-element.82) | copy-start | bytes 2359300
  225.2 5.1 %copy-start.1 = (f32[96,2048]{1,0:T(8,128)S(1)}, f32[96,2048]{1,0:T(8,128)}, u32[]{:S(2)}) copy-start(f32[96,2048]{1,0:T(8,128)} %get-tuple-element.83) | copy-start | bytes 2359300
  225.2 6.0 %copy-start = (f32[256,768]{1,0:T(8,128)S(1)}, f32[256,768]{1,0:T(8,128)}, u32[]{:S(2)}) copy-start(f32[256,768]{1,0:T(8,128)} %get-tuple-element.84) | copy-start | bytes 2359300
